TPU v7x, 256 devices: a whole 4x4x8 slice. The times are simulated.
256 devices in a mesh: tm: 8 (over z), par: 32 (over x, y, core).
Axes of the slice: x: 4, y: 4, z: 8, core: 2. Of those that a mesh axis runs over, the one named last changes fastest.
Arguments:
- kernel: bfloat16 [128, 256, 4096], P('tm', None, 'par'), may hold values from -0.015625 to 0.015625
- history: bfloat16 [128, 4096, 128], P('tm', 'par'), may hold values from -6 to 6
- arrivals: bfloat16 [2, 16, 4096, 128], P(None, 'tm', 'par'), may hold values from -6 to 6
Outputs:
- observations: bfloat16 [2, 16, 256, 128], P(None, None, ('tm', 'par'))
All inputs are finite; a program needn't handle non-finite values.
Results may differ from a plain program's by a relative error of at most 0.014.
Values may be sent and summed in bfloat16 or wider, within the bound.
No kernel may reach another device: no remote copies, remote signals or barrier semaphores. Data moves between devices by JAX's collectives and lax.ppermute only.
A program may use at most 64 MiB of HBM per device.

v0:
```python
import math

import jax
import jax.numpy as jnp
from jax import lax
from jax.sharding import Mesh
from jax.sharding import PartitionSpec as P

TM_PAR = ("tm", "par_0", "par_1", "par_2")
PAR = ("par_0", "par_1", "par_2")


def from_everyone(array, axis):
    copies = jnp.broadcast_to(array, (lax.axis_size(axis), *array.shape))
    return lax.all_to_all(copies, axis, split_axis=0, concat_axis=0, tiled=True)


def laid_out(parts, dim):
    lengths = list(parts.shape[1:])
    lengths[dim] *= parts.shape[0]
    return jnp.moveaxis(parts, 0, dim).reshape(lengths)


def gathered_copies(array, axis, dim):
    parts = from_everyone(array, axis)
    return laid_out(parts, dim)


def from_behind(array, axis, by):
    size = lax.axis_size(axis)
    pairs = [(i, i + by) for i in range(size) if 0 <= i + by < size]
    return lax.ppermute(array, axis, pairs)


def split_up(array, dim, size):
    lengths = array.shape
    parts = array.reshape(*lengths[:dim], size, lengths[dim] // size, *lengths[dim + 1 :])
    return jnp.moveaxis(parts, dim, 0)


def sent_and_summed(array, axis, dim):
    parts = split_up(array, dim, lax.axis_size(axis))
    arrived = lax.all_to_all(parts, axis, split_axis=0, concat_axis=0, tiled=True)
    return arrived.astype(jnp.float32).sum(axis=0)


def sum_by_axis(array, axes, dim):
    far, near = axes
    parts = split_up(array, dim, lax.axis_size(far))
    nearer = sent_and_summed(parts, near, dim + 1)
    arrived = lax.all_to_all(
        nearer.astype(jnp.bfloat16), far, split_axis=0, concat_axis=0, tiled=True
    )
    return arrived.astype(jnp.float32).sum(axis=0)


def tables(block_len):
    length = 2 * block_len
    freq_count = block_len + 1
    freq_index = lax.broadcasted_iota(jnp.int32, (freq_count, length), 0)
    time_index = lax.broadcasted_iota(jnp.int32, (freq_count, length), 1)
    angles = (freq_index * time_index % length).astype(jnp.float32) * (2.0 * math.pi / length)
    forward = jnp.concatenate([jnp.cos(angles), -jnp.sin(angles)], 0)
    forward_high = forward.astype(jnp.bfloat16)
    forward_low = (forward - forward_high.astype(jnp.float32)).astype(jnp.bfloat16)
    out_index = lax.broadcasted_iota(jnp.int32, (block_len, freq_count), 0) + block_len
    spec_index = lax.broadcasted_iota(jnp.int32, (block_len, freq_count), 1)
    out_angles = (out_index * spec_index % length).astype(jnp.float32) * (2.0 * math.pi / length)
    edge_freq = (spec_index == 0) | (spec_index == block_len)
    cos_weight = jnp.where(edge_freq, 1.0, 2.0) / length
    sin_weight = jnp.where(edge_freq, 0.0, 2.0) / length
    inverse = jnp.concatenate(
        [cos_weight * jnp.cos(out_angles), -sin_weight * jnp.sin(out_angles)], 1
    )
    return ((forward_high, forward_low), inverse)


def transform(table_pair, data):
    high_part = jnp.dot(table_pair[0], data, preferred_element_type=jnp.float32)
    return high_part + jnp.dot(table_pair[1], data, preferred_element_type=jnp.float32)


def product(left_operand, right_operand):
    return jnp.einsum(
        "njy,nyv->njv", left_operand, right_operand, preferred_element_type=jnp.float32
    )


def observe(older_block, newer_block, spectrum, forward, inverse):
    block_len, params, fields = older_block.shape
    freq_count = block_len + 1
    sensors = spectrum.shape[2]
    window = jnp.concatenate([older_block, newer_block], 0)
    window = window.reshape(2 * block_len, params * fields)
    window_spec = transform(forward, window)
    window_spec = window_spec.astype(jnp.bfloat16).reshape(2, freq_count, params, fields)
    real_component = product(spectrum[0], window_spec[0]) - product(spectrum[1], window_spec[1])
    imaginary_component = product(spectrum[0], window_spec[1]) + product(
        spectrum[1], window_spec[0]
    )
    stacked = jnp.concatenate([real_component, imaginary_component], 0).reshape(
        2 * freq_count, sensors * fields
    )
    signal = jnp.dot(inverse, stacked, preferred_element_type=jnp.float32)
    return signal.reshape(block_len, sensors, fields)


def per_device(kernel, history, arrivals):
    block_len, sensors, params = kernel.shape
    step_count = arrivals.shape[0]
    freq_count = block_len + 1
    forward, inverse = tables(block_len)
    kernel_flat = kernel.reshape(block_len, sensors * params)
    lag_tables = (forward[0][:, :block_len], forward[1][:, :block_len])
    spectrum = transform(lag_tables, kernel_flat)
    spectrum = spectrum.astype(jnp.bfloat16).reshape(2, freq_count, sensors, params)
    incoming = gathered_copies(arrivals, "tm", 1)
    position = lax.axis_index("tm")
    partials = []
    older_block = history
    for step_index in range(step_count):
        shifted = from_behind(older_block, "tm", 1)
        newer_block = jnp.where(position == 0, incoming[step_index], shifted)
        partials.append(observe(older_block, newer_block, spectrum, forward, inverse))
        older_block = newer_block
    result = sum_by_axis(
        jnp.stack(partials, 0).astype(jnp.bfloat16), (("tm", "par_0"), ("par_1", "par_2")), 2
    ).astype(jnp.bfloat16)
    return result


def solution(mesh):
    split = Mesh(mesh.devices.reshape(mesh.shape["tm"], 4, 4, 2), ("tm", "par_0", "par_1", "par_2"))
    placed = (P("tm", None, PAR), P("tm", PAR, None), P(None, "tm", PAR, None))
    return jax.shard_map(
        per_device,
        mesh=split,
        in_specs=placed,
        out_specs=P(None, None, TM_PAR, None),
        check_vma=False,
    )
```

profile of v0, /device:TPU:32, one launch (start us, length us, event | category | flops | bytes accessed | tf_op | source)
XLA Modules:
  0.0 129.5 jit_solution(15863421673612094853)
XLA Ops:
  0.0 0.0 copy-start.2
  0.0 0.0 copy-start
  0.0 2.3 %broadcast_in_dim.18 = bf16[8,2,2,128,128]{4,3,2,1,0:T(8,128)(2,1)} broadcast(bf16[2,2,128,128]{3,2,1,0:T(8,128)(2,1)} %param.5), dimensions={1,2,3,4} | broadcast | bytes 1179648 | tf_op jit(solution)/shard_map/broadcast_in_dim | solution.py:14
  2.3 8.6 %all-to-all-start = ((bf16[8,2,2,128,128]{4,3,2,1,0:T(8,128)(2,1)}), bf16[8,2,2,128,128]{4,3,2,1,0:T(8,128)(2,1)}, u32[]{:S(2)}, u32[]{:S(2)}) async-start(bf16[8,2,2,128,128]{4,3,2,1,0:T(8,128)(2,1)} %broadcast_in_dim.18), calls=%async_computation | async-start | bytes 2097152 | tf_op jit(solution)/shard_map/all_to_all | solution.py:15
  10.9 0.0 copy-done.2
  10.9 3.4 %collective-permute-start = (bf16[16,128,128]{2,1,0:T(8,128)(2,1)S(1)}, bf16[16,128,128]{2,1,0:T(8,128)(2,1)}, u32[]{:S(2)}, u32[]{:S(2)}) collective-permute-start(bf16[16,128,128]{2,1,0:T(8,128)(2,1)S(1)} %copy-done.2), channel_id=1, source_target_pairs={{0,32},{32,64},{64,96},{96,128},{128,160},{160,192},{192,224},{1,3... | collective-permute-start | bytes 1572872 | tf_op jit(solution)/shard_map/ppermute | solution.py:32
  14.2 0.1 sine_negate_fusion
  14.3 0.0 copy-done
  14.3 0.0 copy-start.1
  14.4 0.9 fusion.26
  15.2 0.3 copy-done.1
  15.6 0.9 fusion
  16.5 21.7 %all-to-all-done = bf16[8,2,2,128,128]{4,3,2,1,0:T(8,128)(2,1)} async-done(((bf16[8,2,2,128,128]{4,3,2,1,0:T(8,128)(2,1)}), bf16[8,2,2,128,128]{4,3,2,1,0:T(8,128)(2,1)}, u32[]{:S(2)}, u32[]{:S(2)}) %all-to-all-start) | async-done | bytes 1048608 | tf_op jit(solution)/shard_map/all_to_all | solution.py:15
  38.2 1.3 fusion.76
  39.5 5.8 %collective-permute-done = bf16[16,128,128]{2,1,0:T(8,128)(2,1)} collective-permute-done((bf16[16,128,128]{2,1,0:T(8,128)(2,1)S(1)}, bf16[16,128,128]{2,1,0:T(8,128)(2,1)}, u32[]{:S(2)}, u32[]{:S(2)}) %collective-permute-start) | collective-permute-done | bytes 524320 | tf_op jit(solution)/shard_map/ppermute | solution.py:32
  45.3 1.1 bitcast_select_fusion.1
  46.4 3.5 %collective-permute-start.1 = (bf16[16,128,128]{2,1,0:T(8,128)(2,1)S(1)}, bf16[16,128,128]{2,1,0:T(8,128)(2,1)S(1)}, u32[]{:S(2)}, u32[]{:S(2)}) collective-permute-start(bf16[16,128,128]{2,1,0:T(8,128)(2,1)S(1)} %bitcast_select_fusion.1), channel_id=1, source_target_pairs={{0,32},{32,64},{64,96},{96,128},{128,160},{160,192},{192,224},{1,3... | collective-permute-start | bytes 1572872 | tf_op jit(solution)/shard_map/ppermute | solution.py:32
  50.0 0.4 fusion.73
  50.3 0.3 copy.14
  50.7 0.3 copy.17
  51.1 0.1 cosine_multiply_fusion
  51.2 9.9 %collective-permute-done.1 = bf16[16,128,128]{2,1,0:T(8,128)(2,1)S(1)} collective-permute-done((bf16[16,128,128]{2,1,0:T(8,128)(2,1)S(1)}, bf16[16,128,128]{2,1,0:T(8,128)(2,1)S(1)}, u32[]{:S(2)}, u32[]{:S(2)}) %collective-permute-start.1) | collective-permute-done | bytes 524320 | tf_op jit(solution)/shard_map/ppermute | solution.py:32
  61.1 0.1 bitcast_select_fusion
  61.3 0.2 pad_maximum_fusion.2
  61.5 0.8 fusion.20
  62.2 0.8 fusion.2
  63.1 0.2 fusion.75
  63.3 0.2 copy.23
  63.4 0.2 copy.22
  63.6 0.5 fusion.38
  64.1 0.4 fusion.40
  64.5 0.5 convolution_add_fusion.3
  65.0 0.5 convolution_subtract_fusion
  65.5 0.2 pad_maximum_fusion.1
  65.7 0.2 slice_bitcast_fusion
  65.9 0.8 fusion.23
  66.7 0.8 fusion.1
  67.5 0.2 fusion.74
  67.7 0.2 copy.18
  67.9 0.4 fusion.42
  68.3 0.2 copy.16
  68.5 0.4 fusion.44
  68.9 0.5 convolution_add_fusion.4
  69.4 0.5 convolution_subtract_fusion.1
  69.9 0.2 pad_maximum_fusion
  70.1 0.2 slice_bitcast_fusion.1
  70.3 1.6 %fusion.13 = bf16[1,16,32,8,128]{4,1,3,2,0:T(8,128)(2,1)S(1)} fusion(bf16[32,8,128,34]{2,1,0,3:T(8,128)(2,1)S(1)} %slice_bitcast_fusion, bf16[16,17]{1,0:T(8,128)(2,1)S(1)} %get-tuple-element.18, bf16[16,17]{1,0:T(8,128)(2,1)S(1)} %get-tuple-element.17), kind=kOutput, calls=%fused_computation.21 | convolution fusion | flops 35653760 | bytes 3277888 | tf_op jit(solution)/shard_map/dot_general | solution.py:104
  71.9 1.6 %fusion.16 = bf16[1,16,32,8,128]{4,1,3,2,0:T(8,128)(2,1)S(1)} fusion(bf16[32,8,128,34]{2,1,0,3:T(8,128)(2,1)S(1)} %slice_bitcast_fusion.1, bf16[16,17]{1,0:T(8,128)(2,1)S(1)} %get-tuple-element.18, bf16[16,17]{1,0:T(8,128)(2,1)S(1)} %get-tuple-element.17), kind=kOutput, calls=%fused_computation.22 | convolution fusion | flops 35653760 | bytes 3277888 | tf_op jit(solution)/shard_map/dot_general | solution.py:104
  73.5 0.2 maximum_bitcast_fusion
  73.7 0.5 copy.8
  74.3 31.5 %all_to_all.15 = bf16[8,32,2,16,1,128]{5,3,1,2,4,0:T(8,128)(2,1)S(1)} all-to-all(bf16[8,32,2,16,1,128]{5,3,1,2,4,0:T(8,128)(2,1)S(1)} %copy.8), channel_id=1, replica_groups=mesh['tm'=8,'par_0'=4,'par_1'=4,'par_2'=2] {'par_1','par_2'}, dimensions={0} | all-to-all | bytes 4194304 | tf_op jit(solution)/shard_map/all_to_all | solution.py:43
  105.8 0.4 reduce_sum.28
  106.2 22.7 %all_to_all.16 = bf16[32,2,16,1,128]{4,2,1,3,0:T(8,128)(2,1)S(1)} all-to-all(bf16[32,2,16,1,128]{4,2,1,3,0:T(8,128)(2,1)S(1)} %copy.10), channel_id=1, replica_groups=mesh['tm'=8,'par_0'=4,'par_1'=4,'par_2'=2] {'tm','par_0'}, dimensions={0} | all-to-all | bytes 524288 | tf_op jit(solution)/shard_map/all_to_all | solution.py:51
  128.9 0.6 reduce_sum.30
  (4 shorter events, 0.0 us)
Async XLA Ops:
  0.0 10.9 %copy-start.2 = (bf16[16,128,128]{2,1,0:T(8,128)(2,1)S(1)}, bf16[16,128,128]{2,1,0:T(8,128)(2,1)}, u32[]{:S(2)}) copy-start(bf16[16,128,128]{2,1,0:T(8,128)(2,1)} %param.4) | copy-start | bytes 1572868
  0.0 14.3 %copy-start = (bf16[16,256,128]{2,1,0:T(8,128)(2,1)S(1)}, bf16[16,256,128]{2,1,0:T(8,128)(2,1)}, u32[]{:S(2)}) copy-start(bf16[16,256,128]{2,1,0:T(8,128)(2,1)} %param.3) | copy-start | bytes 3145732
  2.3 35.9 %all-to-all-start = ((bf16[8,2,2,128,128]{4,3,2,1,0:T(8,128)(2,1)}), bf16[8,2,2,128,128]{4,3,2,1,0:T(8,128)(2,1)}, u32[]{:S(2)}, u32[]{:S(2)}) async-start(bf16[8,2,2,128,128]{4,3,2,1,0:T(8,128)(2,1)} %broadcast_in_dim.18), calls=%async_computation | async-start | bytes 2097152 | tf_op jit(solution)/shard_map/all_to_all | solution.py:15
  10.9 34.5 %collective-permute-start = (bf16[16,128,128]{2,1,0:T(8,128)(2,1)S(1)}, bf16[16,128,128]{2,1,0:T(8,128)(2,1)}, u32[]{:S(2)}, u32[]{:S(2)}) collective-permute-start(bf16[16,128,128]{2,1,0:T(8,128)(2,1)S(1)} %copy-done.2), channel_id=1, source_target_pairs={{0,32},{32,64},{64,96},{96,128},{128,160},{160,192},{192,224},{1,3... | collective-permute-start | bytes 1572872 | tf_op jit(solution)/shard_map/ppermute | solution.py:32
  14.3 1.2 copy-start.1
  46.4 14.7 %collective-permute-start.1 = (bf16[16,128,128]{2,1,0:T(8,128)(2,1)S(1)}, bf16[16,128,128]{2,1,0:T(8,128)(2,1)S(1)}, u32[]{:S(2)}, u32[]{:S(2)}) collective-permute-start(bf16[16,128,128]{2,1,0:T(8,128)(2,1)S(1)} %bitcast_select_fusion.1), channel_id=1, source_target_pairs={{0,32},{32,64},{64,96},{96,128},{128,160},{160,192},{192,224},{1,3... | collective-permute-start | bytes 1572872 | tf_op jit(solution)/shard_map/ppermute | solution.py:32
where the time goes:
time: 130 us
  blocking collectives  54.2 us (42%)
  waiting for transfers between devices  37.5 us (29%)
  starting transfers between devices  15.5 us (12%)
  matrix products  11.8 us (9%)
  local copies, waits for them, and re-layouts  7.03 us (5%)
  other arithmetic  3.27 us (3%)
    all_to_all x1, blocking collectives, sent_and_summed(): lax.all_to_all(parts, axis, split_axis=0, concat_axis=0, tiled=True)  31.5 us
    all_to_all x1, blocking collectives, sum_by_axis(): lax.all_to_all(nearer.astype(jnp.bfloat16), far, split_axis=0, concat_axi...  22.7 us
    all_to_all x1, waiting for transfers between devices, from_everyone(): return lax.all_to_all(copies, axis, split_axis=0, concat_axis=0, tiled=True)  21.7 us
    ppermute x2, waiting for transfers between devices, from_behind(): return lax.ppermute(array, axis, pairs)  15.7 us
    all_to_all x1, starting transfers between devices, from_everyone(): return lax.all_to_all(copies, axis, split_axis=0, concat_axis=0, tiled=True)  8.57 us
    ppermute x2, starting transfers between devices, from_behind(): return lax.ppermute(array, axis, pairs)  6.9 us
    dot_general x8, matrix products, product(): jnp.einsum('njy,nyv->njv', left_operand, right_operand, preferred_element...  3.61 us
    dot_general x2, matrix products, observe(): signal = jnp.dot(inverse, stacked, preferred_element_type=jnp.float32)  3.2 us
  transfers between devices with their start and end apart: 3, of which 3 were waited for; matrix products, arithmetic and copies ran while one was open for 3% of the time, Pallas kernels for 0%

commit v1 on v0

v1 whole, which is shorter than its diff:
```python
import jax
import jax.numpy as jnp
from jax import lax
from jax.experimental import pallas as pl
from jax.experimental.pallas import tpu as pltpu
from jax.sharding import Mesh
from jax.sharding import PartitionSpec as P

PAR = ("x", "y", "c")
EVERY = ("z", "x", "y", "c")


def ordered_kernel(position, kernel, ordered):
    lags, sensors, params = kernel.shape
    planes = position[1]
    half = sensors // 2
    row = lax.broadcasted_iota(jnp.int32, (sensors, sensors), 0)
    col = lax.broadcasted_iota(jnp.int32, (sensors, sensors), 1)
    other = (row >= half).astype(jnp.int32)
    place = row - half * other
    core = position[0] + other - 2 * position[0] * other
    planes = 8
    sensor = (place % planes) * (sensors // planes) + (place // planes) * 2 + core
    select = (col == sensor).astype(jnp.bfloat16)
    for lag in range(lags):
        rows = jnp.dot(select, kernel[lag], preferred_element_type=jnp.float32)
        ordered[:, lag * params : (lag + 1) * params] = rows.astype(jnp.bfloat16)


def convolve(position, ordered, older, shifted, shifted_twice, arrived, mine, theirs, times):
    block, params, fields = older.shape
    steps = arrived.shape[1]
    rows_each = arrived.shape[2]
    sensors = ordered.shape[0]
    total = (steps + 1) * block
    plane = position[0]

    def put(time, value):
        times[(total - 1 - time) * params : (total - time) * params, :fields] = value
        if time:
            times[(total - time) * params : (total - time + 1) * params, fields:] = value

    for time in range(total):
        which, at = divmod(time, block)
        if which == 0:
            put(time, older[at])
            continue
        near = arrived[at // rows_each, which - 1, at % rows_each]
        if which == 1:
            put(time, jnp.where(plane == 0, near, shifted[at]))
        else:
            near_one = arrived[at // rows_each, 0, at % rows_each]
            late = jnp.where(plane == 1, near_one, shifted_twice[at])
            put(time, jnp.where(plane == 0, near, late))

    half = sensors // 2

    def pair(index, carry):
        first = index * 2
        start = pl.multiple_of((total - 1 - block - first) * params, params)
        window = times[pl.ds(start, block * params), :]
        sums = jnp.dot(ordered[...], window, preferred_element_type=jnp.float32)
        sums = sums.astype(jnp.bfloat16)
        for odd in range(2):
            part = sums[:, odd * fields : (odd + 1) * fields]
            mine[:, first + odd] = part[:half].reshape(mine.shape[0], mine.shape[2], fields)
            theirs[:, first + odd] = part[half:].reshape(mine.shape[0], mine.shape[2], fields)
        return carry

    lax.fori_loop(0, steps * block // 2, pair, 0)


def shift(array, axis, by):
    size = lax.axis_size(axis)
    return lax.ppermute(array, axis, [(i, (i + by) % size) for i in range(size)])


def exchange(parts, axis):
    return lax.all_to_all(parts, axis, split_axis=0, concat_axis=0, tiled=True)


def per_device(kernel, history, arrivals):
    block, sensors, params = kernel.shape
    steps, rows_each, _, fields = arrivals.shape
    planes = lax.axis_size("z")
    chips = lax.axis_size("x") * lax.axis_size("y")
    plane = lax.axis_index("z")
    core = lax.axis_index("c")
    vmem = pl.BlockSpec(memory_space=pltpu.VMEM)
    smem = pl.BlockSpec(memory_space=pltpu.SMEM)

    arrived = exchange(jnp.broadcast_to(arrivals, (planes, *arrivals.shape)), "z")
    shifted = shift(history, "z", 1)
    shifted_twice = shift(shifted, "z", 1)
    ordered = pl.pallas_call(
        ordered_kernel,
        out_shape=jax.ShapeDtypeStruct((sensors, block * params), jnp.bfloat16),
        in_specs=[smem, vmem],
        out_specs=vmem,
        name="ordered_kernel",
    )(jnp.stack([core, plane]).astype(jnp.int32), kernel)
    part = jax.ShapeDtypeStruct((chips, steps * block, planes, fields), jnp.bfloat16)
    mine, theirs = pl.pallas_call(
        convolve,
        out_shape=(part, part),
        in_specs=[smem] + [vmem] * 5,
        out_specs=(vmem, vmem),
        scratch_shapes=[pltpu.VMEM(((steps + 1) * block * params, 2 * fields), jnp.bfloat16)],
        compiler_params=pltpu.CompilerParams(vmem_limit_bytes=24 * 1024 * 1024),
        name="convolve",
    )(plane.astype(jnp.int32).reshape(1), ordered, history, shifted, shifted_twice, arrived)
    paired = mine.astype(jnp.float32) + shift(theirs, "c", 1).astype(jnp.float32)
    in_plane = exchange(paired.astype(jnp.bfloat16), ("x", "y"))
    in_plane = in_plane.astype(jnp.float32).sum(axis=0)
    across = exchange(jnp.moveaxis(in_plane, 1, 0).astype(jnp.bfloat16), "z")
    across = across.astype(jnp.float32).sum(axis=0).astype(jnp.bfloat16)
    return across.reshape(steps, block, 1, fields)


def solution(mesh):
    split = Mesh(mesh.devices.reshape(mesh.shape["tm"], 4, 4, 2), EVERY)
    placed = (P("z", None, PAR), P("z", PAR, None), P(None, "z", PAR, None))
    return jax.shard_map(
        per_device,
        mesh=split,
        in_specs=placed,
        out_specs=P(None, None, EVERY, None),
        check_vma=False,
    )
```

time: 130 us -> 111 us (0.85)
  blocking collectives: 54.2 us -> 38.3 us
  matrix products: 11.8 us -> 0 us
  Pallas kernels: 0 us -> 10.6 us
  waiting for transfers between devices: 37.5 us -> 44.7 us
  starting transfers between devices: 15.5 us -> 11.7 us
  local copies, waits for them, and re-layouts: 7.03 us -> 3.36 us
  other arithmetic: 3.27 us -> 1.59 us
    ppermute x2 -> x3, waiting for transfers between devices: 15.7 us -> 44.7 us  [shift(): lax.ppermute(array, axis, [(i, (i + by) % size) for i in range(size)])]
    all_to_all x1, waiting for transfers between devices: 21.7 us -> 0.01 us  [exchange(): return lax.all_to_all(parts, axis, split_axis=0, concat_axis=0, tiled=True)]
    all_to_all x2, blocking collectives: 54.2 us -> 38.3 us  [exchange(): return lax.all_to_all(parts, axis, split_axis=0, concat_axis=0, tiled=True)]
    dot_general x16 -> x0, matrix products: 11.8 us -> none  [the longest x8 3.61 us: product(): jnp.einsum('njy,nyv->njv', left_operand, right_operand, preferred_element...]
    pallas_call x0 -> x2, Pallas kernels: none -> 10.6 us  [the longest x1 7.64 us: per_device(): pl.pallas_call(convolve, out_shape=(part, part), in_specs=[smem] + [vmem]...]
    ppermute x2 -> x3, starting transfers between devices: 6.9 us -> 3.01 us  [shift(): lax.ppermute(array, axis, [(i, (i + by) % size) for i in range(size)])]
    slice x4 -> x0, local copies, waits for them, and re-layouts: 2.01 us -> none  [the longest x1 1.28 us: per_device(): newer_block = jnp.where(position == 0, incoming[step_index], shifted)]
  transfers between devices with their start and end apart: 3 -> 4, of which waited for: 3 -> 3; matrix products, arithmetic and copies ran while one was open for 3% -> 1% of each run, Pallas kernels for 0% -> 3%
where the time goes in v1:
time: 111 us; the launch traced here: 110 us
  waiting for transfers between devices  44.7 us (40%)
  blocking collectives  38.3 us (35%)
  starting transfers between devices  11.7 us (11%)
  Pallas kernels  10.6 us (10%)
  local copies, waits for them, and re-layouts  3.36 us (3%)
  other arithmetic  1.59 us (1%)
    ppermute x3, waiting for transfers between devices, shift(): lax.ppermute(array, axis, [(i, (i + by) % size) for i in range(size)])  44.7 us
    all_to_all x2, blocking collectives, exchange(): return lax.all_to_all(parts, axis, split_axis=0, concat_axis=0, tiled=True)  38.3 us
    all_to_all x1, starting transfers between devices, exchange(): return lax.all_to_all(parts, axis, split_axis=0, concat_axis=0, tiled=True)  8.7 us
    pallas_call x1, Pallas kernels, per_device(): pl.pallas_call(convolve, out_shape=(part, part), in_specs=[smem] + [vmem]...  7.64 us
    ppermute x3, starting transfers between devices, shift(): lax.ppermute(array, axis, [(i, (i + by) % size) for i in range(size)])  3.01 us
    pallas_call x1, Pallas kernels, per_device(): pl.pallas_call(ordered_kernel, out_shape=jax.ShapeDtypeStruct((sensors, b...  2.95 us
  transfers between devices with their start and end apart: 4, of which 3 were waited for; matrix products, arithmetic and copies ran while one was open for 1% of the time, Pallas kernels for 3%

profile of v1, /device:TPU:32, one launch (start us, length us, event | category | flops | bytes accessed | tf_op | source)
XLA Modules:
  0.0 110.3 jit_solution(3444176818085151288)
XLA Ops:
  0.0 2.1 %broadcast_in_dim.3 = bf16[8,2,2,128,128]{4,3,2,1,0:T(8,128)(2,1)} broadcast(bf16[2,2,128,128]{3,2,1,0:T(8,128)(2,1)} %param.5), dimensions={1,2,3,4} | broadcast | bytes 1179648 | tf_op jit(solution)/shard_map/broadcast_in_dim | solution.py:92
  2.1 0.0 copy-start.1
  2.1 8.7 %all-to-all-start = ((bf16[8,2,2,128,128]{4,3,2,1,0:T(8,128)(2,1)}), bf16[8,2,2,128,128]{4,3,2,1,0:T(8,128)(2,1)S(1)}, u32[]{:S(2)}, u32[]{:S(2)}) async-start(bf16[8,2,2,128,128]{4,3,2,1,0:T(8,128)(2,1)} %broadcast_in_dim.3), calls=%async_computation | async-start | bytes 2097152 | tf_op jit(solution)/shard_map/all_to_all | solution.py:79
  10.8 0.0 copy-done.1
  10.8 1.5 %collective-permute-start = (bf16[16,128,128]{2,1,0:T(8,128)(2,1)S(1)}, bf16[16,128,128]{2,1,0:T(8,128)(2,1)S(1)}, u32[]{:S(2)}, u32[]{:S(2)}) collective-permute-start(bf16[16,128,128]{2,1,0:T(8,128)(2,1)S(1)} %copy-done.1), channel_id=1, source_target_pairs={{0,32},{32,64},{64,96},{96,128},{128,160},{160,192},{192,224},{224... | collective-permute-start | bytes 1572872 | tf_op jit(solution)/shard_map/ppermute | solution.py:75
  12.3 32.9 %collective-permute-done.shifted = bf16[16,128,128]{2,1,0:T(8,128)(2,1)S(1)} collective-permute-done((bf16[16,128,128]{2,1,0:T(8,128)(2,1)S(1)}, bf16[16,128,128]{2,1,0:T(8,128)(2,1)S(1)}, u32[]{:S(2)}, u32[]{:S(2)}) %collective-permute-start) | collective-permute-done | bytes 524320 | tf_op jit(solution)/shard_map/ppermute | solution.py:75
  45.2 1.5 %collective-permute-start.1 = (bf16[16,128,128]{2,1,0:T(8,128)(2,1)S(1)}, bf16[16,128,128]{2,1,0:T(8,128)(2,1)S(1)}, u32[]{:S(2)}, u32[]{:S(2)}) collective-permute-start(bf16[16,128,128]{2,1,0:T(8,128)(2,1)S(1)} %collective-permute-done.shifted), channel_id=1, source_target_pairs={{0,32},{32,64},{64,96},{96,128},{128,160},{160,192},{192,224},{224... | collective-permute-start | bytes 1572872 | tf_op jit(solution)/shard_map/ppermute | solution.py:75
  46.6 0.6 pad_add_fusion.position
  47.2 3.0 %ordered_kernel.1.ordered = bf16[256,2048]{1,0:T(8,128)(2,1)} custom-call(s32[2]{0:T(128)} %pad_add_fusion.position, bf16[16,256,128]{2,1,0:T(8,128)(2,1)} %kernel.1), custom_call_target="tpu_custom_call" | custom-call | tf_op jit(solution)/shard_map/ordered_kernel/pallas_call | solution.py:95
  50.1 9.2 %collective-permute-done.1.shifted_twice = bf16[16,128,128]{2,1,0:T(8,128)(2,1)S(1)} collective-permute-done((bf16[16,128,128]{2,1,0:T(8,128)(2,1)S(1)}, bf16[16,128,128]{2,1,0:T(8,128)(2,1)S(1)}, u32[]{:S(2)}, u32[]{:S(2)}) %collective-permute-start.1) | collective-permute-done | bytes 524320 | tf_op jit(solution)/shard_map/ppermute | solution.py:75
  59.3 0.0 all-to-all-done.arrived
  59.3 0.0 copy-start
  59.3 1.2 %copy-done = bf16[256,2048]{1,0:T(8,128)(2,1)S(1)} copy-done((bf16[256,2048]{1,0:T(8,128)(2,1)S(1)}, bf16[256,2048]{1,0:T(8,128)(2,1)}, u32[]{:S(2)}) %copy-start) | copy-done | bytes 1048600
  60.5 7.6 %convolve.1 = (bf16[16,32,8,128]{3,2,1,0:T(8,128)(2,1)S(1)}, bf16[16,32,8,128]{3,2,1,0:T(8,128)(2,1)S(1)}) custom-call(s32[1]{0:T(128)} %bitcast.position, bf16[256,2048]{1,0:T(8,128)(2,1)S(1)} %copy-done, bf16[16,128,128]{2,1,0:T(8,128)(2,1)S(1)} %copy-done.1, bf16[16,128,128]{2,1,0:T(8,128)(2,1)S(1)} %collective-permute-done.shifted, ...), custom_call_target="tpu_custom_call" | custom-call | tf_op jit(solution)/shard_map/convolve/pallas_call | solution.py:103
  68.2 0.1 collective-permute-start.2
  68.3 2.6 %collective-permute-done.2 = bf16[16,32,8,128]{3,2,1,0:T(8,128)(2,1)S(1)} collective-permute-done((bf16[16,32,8,128]{3,2,1,0:T(8,128)(2,1)S(1)}, bf16[16,32,8,128]{3,2,1,0:T(8,128)(2,1)S(1)}, u32[]{:S(2)}, u32[]{:S(2)}) %collective-permute-start.2) | collective-permute-done | bytes 1048608 | tf_op jit(solution)/shard_map/ppermute | solution.py:75
  70.9 0.3 add_convert_fusion
  71.2 24.2 %all_to_all.15 = bf16[16,32,8,128]{3,2,1,0:T(8,128)(2,1)S(1)} all-to-all(bf16[16,32,8,128]{3,2,1,0:T(8,128)(2,1)S(1)} %add_convert_fusion), channel_id=1, replica_groups=mesh['z'=8,'x'=4,'y'=4,'c'=2] {'x','y'}, dimensions={0} | all-to-all | bytes 2097152 | tf_op jit(solution)/shard_map/all_to_all | solution.py:79
  95.5 0.1 reduce_sum.24
  95.6 14.1 %all_to_all.16 = bf16[8,32,128]{2,1,0:T(8,128)(2,1)S(1)} all-to-all(bf16[8,32,128]{2,1,0:T(8,128)(2,1)S(1)} %copy.4), channel_id=1, replica_groups=mesh['z'=8,'x'=4,'y'=4,'c'=2] {'z'}, dimensions={0} | all-to-all | bytes 131072 | tf_op jit(solution)/shard_map/all_to_all | solution.py:79
  109.7 0.6 reduce_sum.25
  (1 shorter events, 0.0 us)
Async XLA Ops:
  2.1 8.7 %copy-start.1 = (bf16[16,128,128]{2,1,0:T(8,128)(2,1)S(1)}, bf16[16,128,128]{2,1,0:T(8,128)(2,1)}, u32[]{:S(2)}) copy-start(bf16[16,128,128]{2,1,0:T(8,128)(2,1)} %older.1) | copy-start | bytes 1572868
  2.1 57.2 %all-to-all-start = ((bf16[8,2,2,128,128]{4,3,2,1,0:T(8,128)(2,1)}), bf16[8,2,2,128,128]{4,3,2,1,0:T(8,128)(2,1)S(1)}, u32[]{:S(2)}, u32[]{:S(2)}) async-start(bf16[8,2,2,128,128]{4,3,2,1,0:T(8,128)(2,1)} %broadcast_in_dim.3), calls=%async_computation | async-start | bytes 2097152 | tf_op jit(solution)/shard_map/all_to_all | solution.py:79
  10.8 34.4 %collective-permute-start = (bf16[16,128,128]{2,1,0:T(8,128)(2,1)S(1)}, bf16[16,128,128]{2,1,0:T(8,128)(2,1)S(1)}, u32[]{:S(2)}, u32[]{:S(2)}) collective-permute-start(bf16[16,128,128]{2,1,0:T(8,128)(2,1)S(1)} %copy-done.1), channel_id=1, source_target_pairs={{0,32},{32,64},{64,96},{96,128},{128,160},{160,192},{192,224},{224... | collective-permute-start | bytes 1572872 | tf_op jit(solution)/shard_map/ppermute | solution.py:75
  45.2 14.1 %collective-permute-start.1 = (bf16[16,128,128]{2,1,0:T(8,128)(2,1)S(1)}, bf16[16,128,128]{2,1,0:T(8,128)(2,1)S(1)}, u32[]{:S(2)}, u32[]{:S(2)}) collective-permute-start(bf16[16,128,128]{2,1,0:T(8,128)(2,1)S(1)} %collective-permute-done.shifted), channel_id=1, source_target_pairs={{0,32},{32,64},{64,96},{96,128},{128,160},{160,192},{192,224},{224... | collective-permute-start | bytes 1572872 | tf_op jit(solution)/shard_map/ppermute | solution.py:75
  59.3 1.2 %copy-start = (bf16[256,2048]{1,0:T(8,128)(2,1)S(1)}, bf16[256,2048]{1,0:T(8,128)(2,1)}, u32[]{:S(2)}) copy-start(bf16[256,2048]{1,0:T(8,128)(2,1)} %ordered_kernel.1.ordered) | copy-start | bytes 3145732
  68.2 2.7 %collective-permute-start.2 = (bf16[16,32,8,128]{3,2,1,0:T(8,128)(2,1)S(1)}, bf16[16,32,8,128]{3,2,1,0:T(8,128)(2,1)S(1)}, u32[]{:S(2)}, u32[]{:S(2)}) collective-permute-start(bf16[16,32,8,128]{3,2,1,0:T(8,128)(2,1)S(1)} %get-tuple-element.8), channel_id=1, source_target_pairs={{0,1},{1,0},{2,3},{3,2},{4,5},{5,4},{6,7},{7,6},{8,9},{9,8},{10,11... | collective-permute-start | bytes 3145736 | tf_op jit(solution)/shard_map/ppermute | solution.py:75

commit v2 on v1

v2 whole, which is shorter than its diff:
```python
import jax
import jax.numpy as jnp
from jax import lax
from jax.experimental import pallas as pl
from jax.experimental.pallas import tpu as pltpu
from jax.sharding import Mesh
from jax.sharding import PartitionSpec as P

PAR = ("x", "y", "c")
EVERY = ("z", "x", "y", "c")
VMEM = pl.BlockSpec(memory_space=pltpu.VMEM)
SMEM = pl.BlockSpec(memory_space=pltpu.SMEM)
LIMIT = pltpu.CompilerParams(vmem_limit_bytes=24 * 1024 * 1024)


def work(flops, nbytes):
    return pl.CostEstimate(flops=flops, bytes_accessed=nbytes, transcendentals=0)


def upper_part(ordered, older, upper, times):
    block, params, fields = older.shape
    last = block - 2
    for time in range(1, block):
        if time <= last:
            times[(last - time) * params : (last - time + 1) * params, :fields] = older[time]
        if time >= 2:
            at = last + 1 - time
            times[at * params : (at + 1) * params, fields:] = older[time]
    for pair in range(block // 2 - 1):
        lag = (2 * pair + 2) * params
        upper[pair] = jnp.dot(
            ordered[:, lag:], times[: block * params - lag], preferred_element_type=jnp.float32
        )


def first_part(core, kernel, older, ordered, upper, times):
    lags, sensors, params = kernel.shape
    planes = 8
    half = sensors // 2
    row = lax.broadcasted_iota(jnp.int32, (sensors, sensors), 0)
    col = lax.broadcasted_iota(jnp.int32, (sensors, sensors), 1)
    other = (row >= half).astype(jnp.int32)
    place = row - half * other
    parity = core[0] + other - 2 * core[0] * other
    sensor = (place % planes) * (sensors // planes) + (place // planes) * 2 + parity
    select = (col == sensor).astype(jnp.bfloat16)
    for lag in range(lags):
        rows = jnp.dot(select, kernel[lag], preferred_element_type=jnp.float32)
        ordered[:, lag * params : (lag + 1) * params] = rows.astype(jnp.bfloat16)
    upper_part(ordered, older, upper, times)


def lower_part(ordered, older, newer, upper, mine, theirs, times):
    block, params, fields = newer.shape
    half = ordered.shape[0] // 2
    for time in range(-1, block):
        value = newer[time] if time >= 0 else older[block - 1]
        at = block - 2 - time
        if time <= block - 2:
            times[at * params : (at + 1) * params, :fields] = value
        if time >= 0:
            times[(at + 1) * params : (at + 2) * params, fields:] = value
    for pair in range(block // 2):
        lag = (2 * pair + 2) * params
        sums = jnp.dot(
            ordered[:, :lag], times[block * params - lag :], preferred_element_type=jnp.float32
        )
        if pair < block // 2 - 1:
            sums = sums + upper[pair]
        sums = sums.astype(jnp.bfloat16)
        for odd in range(2):
            part = sums[:, odd * fields : (odd + 1) * fields]
            mine[:, 2 * pair + odd] = part[:half].reshape(mine.shape[0], mine.shape[2], fields)
            theirs[:, 2 * pair + odd] = part[half:].reshape(mine.shape[0], mine.shape[2], fields)


def ring(array, axis, by):
    size = lax.axis_size(axis)
    return lax.ppermute(array, axis, [(i, (i + by) % size) for i in range(size)])


def onward(array, axis):
    return lax.ppermute(array, axis, [(i, i + 1) for i in range(lax.axis_size(axis) - 1)])


def exchange(parts, axis):
    return lax.all_to_all(parts, axis, split_axis=0, concat_axis=0, tiled=True)


def observed(kernel, history, arrivals):
    block, sensors, params = kernel.shape
    steps, _, _, fields = arrivals.shape
    planes = lax.axis_size("z")
    chips = lax.axis_size("x") * lax.axis_size("y")
    plane = lax.axis_index("z")
    core = lax.axis_index("c").astype(jnp.int32).reshape(1)
    pairs = (block // 2 - 1, sensors, 2 * fields)
    scratch = [pltpu.VMEM((block * params, 2 * fields), jnp.bfloat16)]
    part = jax.ShapeDtypeStruct((chips, block, planes, fields), jnp.bfloat16)

    shifted = onward(history, "z")
    sources = [4, 3, 5, 2, 6, 1, 7]
    pieces = {0: arrivals}
    for source in sources:
        pieces[source] = lax.ppermute(arrivals, "z", [(source, 0)])

    def newer_of(step, received):
        newest = jnp.concatenate([pieces[i][step] for i in range(planes)], 0)
        return jnp.where(plane == 0, newest, received)

    ordered, upper = pl.pallas_call(
        first_part,
        out_shape=(
            jax.ShapeDtypeStruct((sensors, block * params), jnp.bfloat16),
            jax.ShapeDtypeStruct(pairs, jnp.float32),
        ),
        in_specs=[SMEM, VMEM, VMEM],
        out_specs=(VMEM, VMEM),
        scratch_shapes=scratch,
        compiler_params=LIMIT,
        cost_estimate=work(2 * 10**9, 4 * 10**6),
        name="first_part",
    )(core, kernel, history)

    def lower(older, newer, upper):
        return pl.pallas_call(
            lower_part,
            out_shape=(part, part),
            in_specs=[VMEM] * 4,
            out_specs=(VMEM, VMEM),
            scratch_shapes=scratch,
            compiler_params=LIMIT,
            cost_estimate=work(2 * 10**9, 6 * 10**6),
            name="lower_part",
        )(ordered, older, newer, upper)

    def in_plane(mine, theirs):
        received = ring(theirs, "c", 1)
        paired = (mine.astype(jnp.float32) + received.astype(jnp.float32)).astype(jnp.bfloat16)
        return exchange(paired, ("x", "y"))

    newer = newer_of(0, shifted)
    shifted_twice = onward(newer, "z")
    mine, theirs = lower(history, newer, upper)
    arrived_first = in_plane(mine, theirs)
    upper = pl.pallas_call(
        upper_part,
        out_shape=jax.ShapeDtypeStruct(pairs, jnp.float32),
        in_specs=[VMEM] * 2,
        out_specs=VMEM,
        scratch_shapes=scratch,
        compiler_params=LIMIT,
        cost_estimate=work(10**9, 4 * 10**6),
        name="upper_part",
    )(ordered, newer)
    newest = newer_of(1, shifted_twice)
    mine, theirs = lower(newer, newest, upper)
    arrived_second = in_plane(mine, theirs)
    summed = jnp.concatenate(
        [part.astype(jnp.float32).sum(axis=0) for part in (arrived_first, arrived_second)], 0
    )
    across = exchange(jnp.moveaxis(summed, 1, 0).astype(jnp.bfloat16), "z")
    across = across.astype(jnp.float32).sum(axis=0).astype(jnp.bfloat16)
    return across.reshape(steps, block, 1, fields)


def solution(mesh):
    split = Mesh(mesh.devices.reshape(mesh.shape["tm"], 4, 4, 2), EVERY)
    placed = (P("z", None, PAR), P("z", PAR, None), P(None, "z", PAR, None))
    return jax.shard_map(
        observed,
        mesh=split,
        in_specs=placed,
        out_specs=P(None, None, EVERY, None),
        check_vma=False,
    )
```

time: 111 us -> 100 us (0.901)
  blocking collectives: 38.3 us -> 13.6 us
  starting transfers between devices: 11.7 us -> 27.3 us
  Pallas kernels: 10.6 us -> 5.65 us
  waiting for transfers between devices: 44.7 us -> 48.7 us
  local copies, waits for them, and re-layouts: 3.36 us -> 1.16 us
  other arithmetic: 1.59 us -> 2.77 us
    all_to_all x2 -> x1, blocking collectives: 38.3 us -> 13.6 us  [exchange(): return lax.all_to_all(parts, axis, split_axis=0, concat_axis=0, tiled=True)]
    all_to_all x1 -> x2, waiting for transfers between devices: 0.01 us -> 22 us  [exchange(): return lax.all_to_all(parts, axis, split_axis=0, concat_axis=0, tiled=True)]
    ppermute x3 -> x11, waiting for transfers between devices: 44.7 us -> 26.7 us  [the longest x2 22.3 us: onward(): lax.ppermute(array, axis, [(i, i + 1) for i in range(lax.axis_size(axis)...]
    ppermute x3 -> x11, starting transfers between devices: 3.01 us -> 14.2 us  [the longest x7 10.2 us: observed(): pieces[source] = lax.ppermute(arrivals, 'z', [(source, 0)])]
    pallas_call x2 -> x4, Pallas kernels: 10.6 us -> 5.65 us  [the longest x2 2.88 us: lower(): pl.pallas_call(lower_part, out_shape=(part, part), in_specs=[VMEM] * 4, o...]
    all_to_all x1 -> x2, starting transfers between devices: 8.7 us -> 13 us  [exchange(): return lax.all_to_all(parts, axis, split_axis=0, concat_axis=0, tiled=True)]
    broadcast_in_dim x1 -> x0, local copies, waits for them, and re-layouts: 2.12 us -> none  [per_device(): jnp.broadcast_to(arrivals, (planes, *arrivals.shape))]
    convert_element_type x1 -> x3, other arithmetic: 0.28 us -> 1.89 us  [the longest x2 1.88 us: in_plane(): (mine.astype(jnp.float32) + received.astype(jnp.float32)).astype(jnp.bflo...]
  transfers between devices with their start and end apart: 4 -> 13, of which waited for: 3 -> 5; matrix products, arithmetic and copies ran while one was open for 1% -> 3% of each run, Pallas kernels for 3% -> 6%
where the time goes in v2:
time: 100 us; the launch traced here: 99.5 us
  waiting for transfers between devices  48.7 us (49%)
  starting transfers between devices  27.3 us (27%)
  blocking collectives  13.6 us (14%)
  Pallas kernels  5.65 us (6%)
  other arithmetic  2.77 us (3%)
  local copies, waits for them, and re-layouts  1.16 us (1%)
    ppermute x2, waiting for transfers between devices, onward(): lax.ppermute(array, axis, [(i, i + 1) for i in range(lax.axis_size(axis)...  22.3 us
    all_to_all x2, waiting for transfers between devices, exchange(): return lax.all_to_all(parts, axis, split_axis=0, concat_axis=0, tiled=True)  22 us
    all_to_all x1, blocking collectives, exchange(): return lax.all_to_all(parts, axis, split_axis=0, concat_axis=0, tiled=True)  13.6 us
    all_to_all x2, starting transfers between devices, exchange(): return lax.all_to_all(parts, axis, split_axis=0, concat_axis=0, tiled=True)  13 us
    ppermute x7, starting transfers between devices, observed(): pieces[source] = lax.ppermute(arrivals, 'z', [(source, 0)])  10.2 us
    ppermute x7, waiting for transfers between devices, observed(): pieces[source] = lax.ppermute(arrivals, 'z', [(source, 0)])  4.36 us
    ppermute x2, starting transfers between devices, onward(): lax.ppermute(array, axis, [(i, i + 1) for i in range(lax.axis_size(axis)...  3.84 us
    pallas_call x2, Pallas kernels, lower(): pl.pallas_call(lower_part, out_shape=(part, part), in_specs=[VMEM] * 4, o...  2.88 us
  transfers between devices with their start and end apart: 13, of which 5 were waited for; matrix products, arithmetic and copies ran while one was open for 3% of the time, Pallas kernels for 6%

profile of v2, /device:TPU:32, one launch (start us, length us, event | category | flops | bytes accessed | tf_op | source)
XLA Modules:
  0.0 99.5 jit_solution(4676114242192779942)
XLA Ops:
  0.0 0.7 collective-permute-start.4
  0.7 0.7 collective-permute-start.3
  1.3 0.7 collective-permute-start.2
  2.0 0.7 collective-permute-start.1
  2.7 6.2 %collective-permute-start = (bf16[2,2,128,128]{3,2,1,0:T(8,128)(2,1)}, bf16[2,2,128,128]{3,2,1,0:T(8,128)(2,1)S(1)}, u32[]{:S(2)}, u32[]{:S(2)}) collective-permute-start(bf16[2,2,128,128]{3,2,1,0:T(8,128)(2,1)} %param.5), channel_id=1, source_target_pairs={{32,0},{33,1},{34,2},{35,3},{36,4},{37,5},{38,6},{39,7},{40,8},{41... | collective-permute-start | bytes 393224 | tf_op jit(solution)/shard_map/ppermute | solution.py:105
  8.9 0.0 copy-start
  8.9 0.0 copy-start.1
  9.0 1.0 %bitcast_dynamic-update-slice_fusion = (bf16[16,128,128]{2,1,0:T(8,128)(2,1)S(1)}, bf16[16,128,128]{2,1,0:T(8,128)(2,1)S(1)}) fusion(bf16[2,2,128,128]{3,2,1,0:T(8,128)(2,1)} %param.5), kind=kLoop, calls=%fused_computation.33 | loop fusion | bytes 262144
  10.0 4.3 %collective-permute-done = bf16[2,2,128,128]{3,2,1,0:T(8,128)(2,1)S(1)} collective-permute-done((bf16[2,2,128,128]{3,2,1,0:T(8,128)(2,1)}, bf16[2,2,128,128]{3,2,1,0:T(8,128)(2,1)S(1)}, u32[]{:S(2)}, u32[]{:S(2)}) %collective-permute-start) | collective-permute-done | bytes 131104 | tf_op jit(solution)/shard_map/ppermute | solution.py:105
  14.3 0.7 collective-permute-start.5
  15.0 0.0 collective-permute-done.1
  15.0 0.7 collective-permute-start.6
  15.7 0.0 collective-permute-done.2
  15.7 1.9 %collective-permute-start.7 = (bf16[16,128,128]{2,1,0:T(8,128)(2,1)}, bf16[16,128,128]{2,1,0:T(8,128)(2,1)S(1)}, u32[]{:S(2)}, u32[]{:S(2)}) collective-permute-start(bf16[16,128,128]{2,1,0:T(8,128)(2,1)} %older.3), channel_id=1, source_target_pairs={{0,32},{32,64},{64,96},{96,128},{128,160},{160,192},{192,224},{1,3... | collective-permute-start | bytes 1572872 | tf_op jit(solution)/shard_map/ppermute | solution.py:83
  17.7 0.0 collective-permute-done.3
  17.7 0.0 collective-permute-done.4
  17.8 0.0 collective-permute-done.5
  17.8 0.0 collective-permute-done.6
  17.8 14.3 %collective-permute-done.7 = bf16[16,128,128]{2,1,0:T(8,128)(2,1)S(1)} collective-permute-done((bf16[16,128,128]{2,1,0:T(8,128)(2,1)}, bf16[16,128,128]{2,1,0:T(8,128)(2,1)S(1)}, u32[]{:S(2)}, u32[]{:S(2)}) %collective-permute-start.7) | collective-permute-done | bytes 524320 | tf_op jit(solution)/shard_map/ppermute | solution.py:83
  32.1 0.1 broadcast_select_fusion.1.newer.older
  32.2 1.9 %collective-permute-start.9 = (bf16[16,128,128]{2,1,0:T(8,128)(2,1)S(1)}, bf16[16,128,128]{2,1,0:T(8,128)(2,1)S(1)}, u32[]{:S(2)}, u32[]{:S(2)}) collective-permute-start(bf16[16,128,128]{2,1,0:T(8,128)(2,1)S(1)} %broadcast_select_fusion.1.newer.older), channel_id=1, source_target_pairs={{0,32},{32,64},{64,96},{96,128},{128,160},{160,192},{192,224},{1,3... | collective-permute-start | bytes 1572872 | tf_op jit(solution)/shard_map/ppermute | solution.py:83
  34.1 0.0 copy-done
  34.1 0.0 copy-done.1
  34.1 1.6 %first_part.1 = (bf16[256,2048]{1,0:T(8,128)(2,1)S(1)}, f32[7,256,256]{2,1,0:T(8,128)S(1)}) custom-call(s32[1]{0:T(128)} %bitcast.core, bf16[16,256,128]{2,1,0:T(8,128)(2,1)S(1)} %copy-done, bf16[16,128,128]{2,1,0:T(8,128)(2,1)S(1)} %copy-done.1), custom_call_target="tpu_custom_call" | custom-call | flops 2000000000 | bytes 4000000 | tf_op jit(solution)/shard_map/first_part/pallas_call | solution.py:111
  35.8 1.5 %lower_part.2 = (bf16[16,16,8,128]{3,2,1,0:T(8,128)(2,1)S(1)}, bf16[16,16,8,128]{3,2,1,0:T(8,128)(2,1)S(1)}) custom-call(bf16[256,2048]{1,0:T(8,128)(2,1)S(1)} %get-tuple-element.11.ordered, bf16[16,128,128]{2,1,0:T(8,128)(2,1)S(1)} %copy-done.1, bf16[16,128,128]{2,1,0:T(8,128)(2,1)S(1)} %broadcast_select_fusion.1.newer.older, ...), custom_call_target="tpu_custom_call" | custom-call | flops 2000000000 | bytes 6000000 | tf_op jit(solution)/shard_map/lower_part/pallas_call | solution.py:126
  37.2 0.1 collective-permute-start.8
  37.3 1.1 %upper_part.1.upper = f32[7,256,256]{2,1,0:T(8,128)S(1)} custom-call(bf16[256,2048]{1,0:T(8,128)(2,1)S(1)} %get-tuple-element.11.ordered, bf16[16,128,128]{2,1,0:T(8,128)(2,1)S(1)} %broadcast_select_fusion.1.newer.older), custom_call_target="tpu_custom_call" | custom-call | flops 1000000000 | bytes 4000000 | tf_op jit(solution)/shard_map/upper_part/pallas_call | solution.py:146
  38.5 8.0 %collective-permute-done.9 = bf16[16,128,128]{2,1,0:T(8,128)(2,1)S(1)} collective-permute-done((bf16[16,128,128]{2,1,0:T(8,128)(2,1)S(1)}, bf16[16,128,128]{2,1,0:T(8,128)(2,1)S(1)}, u32[]{:S(2)}, u32[]{:S(2)}) %collective-permute-start.9) | collective-permute-done | bytes 524320 | tf_op jit(solution)/shard_map/ppermute | solution.py:83
  46.5 0.1 broadcast_select_fusion.newer
  46.6 1.4 %lower_part.3 = (bf16[16,16,8,128]{3,2,1,0:T(8,128)(2,1)S(1)}, bf16[16,16,8,128]{3,2,1,0:T(8,128)(2,1)S(1)}) custom-call(bf16[256,2048]{1,0:T(8,128)(2,1)S(1)} %get-tuple-element.11.ordered, bf16[16,128,128]{2,1,0:T(8,128)(2,1)S(1)} %broadcast_select_fusion.1.newer.older, bf16[16,128,128]{2,1,0:T(8,128)(2,1)S(1)} %broadcast_select_fusion.newer, ...), custom_call_target="tpu_custom_call" | custom-call | flops 2000000000 | bytes 6000000 | tf_op jit(solution)/shard_map/lower_part/pallas_call | solution.py:126
  48.0 0.1 collective-permute-start.10
  48.1 0.0 collective-permute-done.8
  48.1 0.9 add_convert_fusion.1
  49.1 9.4 %all-to-all-start = ((bf16[16,16,8,128]{3,2,1,0:T(8,128)(2,1)}), bf16[16,16,8,128]{3,2,1,0:T(8,128)(2,1)S(1)}, u32[]{:S(2)}, u32[]{:S(2)}) async-start(bf16[16,16,8,128]{3,2,1,0:T(8,128)(2,1)} %add_convert_fusion.1), calls=%async_computation | async-start | bytes 1048576 | tf_op jit(solution)/shard_map/all_to_all | solution.py:87
  58.5 0.0 collective-permute-done.10
  58.5 0.9 add_convert_fusion
  59.5 11.2 %all-to-all-done = bf16[16,16,8,128]{3,2,1,0:T(8,128)(2,1)S(1)} async-done(((bf16[16,16,8,128]{3,2,1,0:T(8,128)(2,1)}), bf16[16,16,8,128]{3,2,1,0:T(8,128)(2,1)S(1)}, u32[]{:S(2)}, u32[]{:S(2)}) %all-to-all-start) | async-done | bytes 524320 | tf_op jit(solution)/shard_map/all_to_all | solution.py:87
  70.7 3.6 %all-to-all-start.1 = ((bf16[16,16,8,128]{3,2,1,0:T(8,128)(2,1)}), bf16[16,16,8,128]{3,2,1,0:T(8,128)(2,1)S(1)}, u32[]{:S(2)}, u32[]{:S(2)}) async-start(bf16[16,16,8,128]{3,2,1,0:T(8,128)(2,1)} %add_convert_fusion), calls=%async_computation.1 | async-start | bytes 1048576 | tf_op jit(solution)/shard_map/all_to_all | solution.py:87
  74.2 0.1 reduce.1
  74.3 10.8 %all-to-all-done.1 = bf16[16,16,8,128]{3,2,1,0:T(8,128)(2,1)S(1)} async-done(((bf16[16,16,8,128]{3,2,1,0:T(8,128)(2,1)}), bf16[16,16,8,128]{3,2,1,0:T(8,128)(2,1)S(1)}, u32[]{:S(2)}, u32[]{:S(2)}) %all-to-all-start.1) | async-done | bytes 524320 | tf_op jit(solution)/shard_map/all_to_all | solution.py:87
  85.1 0.1 reduce.2
  85.2 13.6 %all_to_all.15 = bf16[8,32,128]{2,1,0:T(8,128)(2,1)S(1)} all-to-all(bf16[8,32,128]{2,1,0:T(8,128)(2,1)S(1)} %copy.4), channel_id=1, replica_groups=mesh['z'=8,'x'=4,'y'=4,'c'=2] {'z'}, dimensions={0} | all-to-all | bytes 131072 | tf_op jit(solution)/shard_map/all_to_all | solution.py:87
  98.9 0.6 reduce_sum.32
  (9 shorter events, 0.2 us)
Async XLA Ops:
  0.0 17.7 %collective-permute-start.4 = (bf16[2,2,128,128]{3,2,1,0:T(8,128)(2,1)}, bf16[2,2,128,128]{3,2,1,0:T(8,128)(2,1)S(1)}, u32[]{:S(2)}, u32[]{:S(2)}) collective-permute-start(bf16[2,2,128,128]{3,2,1,0:T(8,128)(2,1)} %param.5), channel_id=1, source_target_pairs={{160,0},{161,1},{162,2},{163,3},{164,4},{165,5},{166,6},{167,7},{1... | collective-permute-start | bytes 393224 | tf_op jit(solution)/shard_map/ppermute | solution.py:105
  0.7 17.0 %collective-permute-start.3 = (bf16[2,2,128,128]{3,2,1,0:T(8,128)(2,1)}, bf16[2,2,128,128]{3,2,1,0:T(8,128)(2,1)S(1)}, u32[]{:S(2)}, u32[]{:S(2)}) collective-permute-start(bf16[2,2,128,128]{3,2,1,0:T(8,128)(2,1)} %param.5), channel_id=1, source_target_pairs={{128,0},{129,1},{130,2},{131,3},{132,4},{133,5},{134,6},{135,7},{1... | collective-permute-start | bytes 393224 | tf_op jit(solution)/shard_map/ppermute | solution.py:105
  1.3 14.4 %collective-permute-start.2 = (bf16[2,2,128,128]{3,2,1,0:T(8,128)(2,1)}, bf16[2,2,128,128]{3,2,1,0:T(8,128)(2,1)S(1)}, u32[]{:S(2)}, u32[]{:S(2)}) collective-permute-start(bf16[2,2,128,128]{3,2,1,0:T(8,128)(2,1)} %param.5), channel_id=1, source_target_pairs={{96,0},{97,1},{98,2},{99,3},{100,4},{101,5},{102,6},{103,7},{104,8... | collective-permute-start | bytes 393224 | tf_op jit(solution)/shard_map/ppermute | solution.py:105
  2.0 13.0 %collective-permute-start.1 = (bf16[2,2,128,128]{3,2,1,0:T(8,128)(2,1)}, bf16[2,2,128,128]{3,2,1,0:T(8,128)(2,1)S(1)}, u32[]{:S(2)}, u32[]{:S(2)}) collective-permute-start(bf16[2,2,128,128]{3,2,1,0:T(8,128)(2,1)} %param.5), channel_id=1, source_target_pairs={{64,0},{65,1},{66,2},{67,3},{68,4},{69,5},{70,6},{71,7},{72,8},{73... | collective-permute-start | bytes 393224 | tf_op jit(solution)/shard_map/ppermute | solution.py:105
  2.7 11.6 %collective-permute-start = (bf16[2,2,128,128]{3,2,1,0:T(8,128)(2,1)}, bf16[2,2,128,128]{3,2,1,0:T(8,128)(2,1)S(1)}, u32[]{:S(2)}, u32[]{:S(2)}) collective-permute-start(bf16[2,2,128,128]{3,2,1,0:T(8,128)(2,1)} %param.5), channel_id=1, source_target_pairs={{32,0},{33,1},{34,2},{35,3},{36,4},{37,5},{38,6},{39,7},{40,8},{41... | collective-permute-start | bytes 393224 | tf_op jit(solution)/shard_map/ppermute | solution.py:105
  8.9 25.2 %copy-start = (bf16[16,256,128]{2,1,0:T(8,128)(2,1)S(1)}, bf16[16,256,128]{2,1,0:T(8,128)(2,1)}, u32[]{:S(2)}) copy-start(bf16[16,256,128]{2,1,0:T(8,128)(2,1)} %kernel.1) | copy-start | bytes 3145732
  8.9 25.2 %copy-start.1 = (bf16[16,128,128]{2,1,0:T(8,128)(2,1)S(1)}, bf16[16,128,128]{2,1,0:T(8,128)(2,1)}, u32[]{:S(2)}) copy-start(bf16[16,128,128]{2,1,0:T(8,128)(2,1)} %older.3) | copy-start | bytes 1572868
  14.3 3.5 %collective-permute-start.5 = (bf16[2,2,128,128]{3,2,1,0:T(8,128)(2,1)}, bf16[2,2,128,128]{3,2,1,0:T(8,128)(2,1)S(1)}, u32[]{:S(2)}, u32[]{:S(2)}) collective-permute-start(bf16[2,2,128,128]{3,2,1,0:T(8,128)(2,1)} %param.5), channel_id=1, source_target_pairs={{192,0},{193,1},{194,2},{195,3},{196,4},{197,5},{198,6},{199,7},{2... | collective-permute-start | bytes 393224 | tf_op jit(solution)/shard_map/ppermute | solution.py:105
  15.0 2.8 %collective-permute-start.6 = (bf16[2,2,128,128]{3,2,1,0:T(8,128)(2,1)}, bf16[2,2,128,128]{3,2,1,0:T(8,128)(2,1)S(1)}, u32[]{:S(2)}, u32[]{:S(2)}) collective-permute-start(bf16[2,2,128,128]{3,2,1,0:T(8,128)(2,1)} %param.5), channel_id=1, source_target_pairs={{224,0},{225,1},{226,2},{227,3},{228,4},{229,5},{230,6},{231,7},{2... | collective-permute-start | bytes 393224 | tf_op jit(solution)/shard_map/ppermute | solution.py:105
  15.7 16.4 %collective-permute-start.7 = (bf16[16,128,128]{2,1,0:T(8,128)(2,1)}, bf16[16,128,128]{2,1,0:T(8,128)(2,1)S(1)}, u32[]{:S(2)}, u32[]{:S(2)}) collective-permute-start(bf16[16,128,128]{2,1,0:T(8,128)(2,1)} %older.3), channel_id=1, source_target_pairs={{0,32},{32,64},{64,96},{96,128},{128,160},{160,192},{192,224},{1,3... | collective-permute-start | bytes 1572872 | tf_op jit(solution)/shard_map/ppermute | solution.py:83
  32.2 14.3 %collective-permute-start.9 = (bf16[16,128,128]{2,1,0:T(8,128)(2,1)S(1)}, bf16[16,128,128]{2,1,0:T(8,128)(2,1)S(1)}, u32[]{:S(2)}, u32[]{:S(2)}) collective-permute-start(bf16[16,128,128]{2,1,0:T(8,128)(2,1)S(1)} %broadcast_select_fusion.1.newer.older), channel_id=1, source_target_pairs={{0,32},{32,64},{64,96},{96,128},{128,160},{160,192},{192,224},{1,3... | collective-permute-start | bytes 1572872 | tf_op jit(solution)/shard_map/ppermute | solution.py:83
  37.2 10.9 %collective-permute-start.8 = (bf16[16,16,8,128]{3,2,1,0:T(8,128)(2,1)S(1)}, bf16[16,16,8,128]{3,2,1,0:T(8,128)(2,1)S(1)}, u32[]{:S(2)}, u32[]{:S(2)}) collective-permute-start(bf16[16,16,8,128]{3,2,1,0:T(8,128)(2,1)S(1)} %get-tuple-element.14), channel_id=1, source_target_pairs={{0,1},{1,0},{2,3},{3,2},{4,5},{5,4},{6,7},{7,6},{8,9},{9,8},{10,11... | collective-permute-start | bytes 1572872 | tf_op jit(solution)/shard_map/ppermute | solution.py:79
  48.0 10.5 %collective-permute-start.10 = (bf16[16,16,8,128]{3,2,1,0:T(8,128)(2,1)S(1)}, bf16[16,16,8,128]{3,2,1,0:T(8,128)(2,1)S(1)}, u32[]{:S(2)}, u32[]{:S(2)}) collective-permute-start(bf16[16,16,8,128]{3,2,1,0:T(8,128)(2,1)S(1)} %get-tuple-element.16), channel_id=1, source_target_pairs={{0,1},{1,0},{2,3},{3,2},{4,5},{5,4},{6,7},{7,6},{8,9},{9,8},{10,11... | collective-permute-start | bytes 1572872 | tf_op jit(solution)/shard_map/ppermute | solution.py:79
  49.1 21.6 %all-to-all-start = ((bf16[16,16,8,128]{3,2,1,0:T(8,128)(2,1)}), bf16[16,16,8,128]{3,2,1,0:T(8,128)(2,1)S(1)}, u32[]{:S(2)}, u32[]{:S(2)}) async-start(bf16[16,16,8,128]{3,2,1,0:T(8,128)(2,1)} %add_convert_fusion.1), calls=%async_computation | async-start | bytes 1048576 | tf_op jit(solution)/shard_map/all_to_all | solution.py:87
  70.7 14.5 %all-to-all-start.1 = ((bf16[16,16,8,128]{3,2,1,0:T(8,128)(2,1)}), bf16[16,16,8,128]{3,2,1,0:T(8,128)(2,1)S(1)}, u32[]{:S(2)}, u32[]{:S(2)}) async-start(bf16[16,16,8,128]{3,2,1,0:T(8,128)(2,1)} %add_convert_fusion), calls=%async_computation.1 | async-start | bytes 1048576 | tf_op jit(solution)/shard_map/all_to_all | solution.py:87

commit v3 on v2

--- a/solution.py
+++ b/solution.py
@@ -9,8 +9,8 @@
 PAR = ("x", "y", "c")
 EVERY = ("z", "x", "y", "c")
 VMEM = pl.BlockSpec(memory_space=pltpu.VMEM)
-SMEM = pl.BlockSpec(memory_space=pltpu.SMEM)
-LIMIT = pltpu.CompilerParams(vmem_limit_bytes=24 * 1024 * 1024)
+HBM = pl.BlockSpec(memory_space=pltpu.HBM)
+LIMIT = pltpu.CompilerParams(vmem_limit_bytes=8 * 1024 * 1024)
 
 
 def work(flops, nbytes):
@@ -33,7 +33,14 @@
         )
 
 
-def first_part(core, kernel, older, ordered, upper, times):
+def first_part(kernel_hbm, older_hbm, ordered, upper, times, kernel, older, arrived):
+    copies = [
+        pltpu.make_async_copy(kernel_hbm.at[lag], kernel.at[lag], arrived.at[lag])
+        for lag in range(kernel.shape[0])
+    ]
+    copies.append(pltpu.make_async_copy(older_hbm, older, arrived.at[kernel.shape[0]]))
+    for copy in copies:
+        copy.start()
     lags, sensors, params = kernel.shape
     planes = 8
     half = sensors // 2
@@ -41,20 +48,27 @@
     col = lax.broadcasted_iota(jnp.int32, (sensors, sensors), 1)
     other = (row >= half).astype(jnp.int32)
     place = row - half * other
-    parity = core[0] + other - 2 * core[0] * other
+    core = lax.axis_index("c")
+    parity = core + other - 2 * core * other
     sensor = (place % planes) * (sensors // planes) + (place // planes) * 2 + parity
     select = (col == sensor).astype(jnp.bfloat16)
     for lag in range(lags):
+        copies[lag].wait()
         rows = jnp.dot(select, kernel[lag], preferred_element_type=jnp.float32)
         ordered[:, lag * params : (lag + 1) * params] = rows.astype(jnp.bfloat16)
+    copies[lags].wait()
     upper_part(ordered, older, upper, times)
 
 
-def lower_part(ordered, older, newer, upper, mine, theirs, times):
-    block, params, fields = newer.shape
+def lower_part(ordered, older, received, upper, *refs):
+    *late, mine, theirs, times = refs
+    block, params, fields = received.shape
+    here = lax.axis_index("z") == 0
     half = ordered.shape[0] // 2
     for time in range(-1, block):
-        value = newer[time] if time >= 0 else older[block - 1]
+        value = received[time] if time >= 0 else older[block - 1]
+        if late and time >= 0:
+            value = jnp.where(here, late[0][time], value)
         at = block - 2 - time
         if time <= block - 2:
             times[at * params : (at + 1) * params, :fields] = value
@@ -74,6 +88,30 @@
             theirs[:, 2 * pair + odd] = part[half:].reshape(mine.shape[0], mine.shape[2], fields)
 
 
+def newer_part(*refs):
+    *pieces, received, newer, late = refs
+    here = lax.axis_index("z") == 0
+    each = pieces[0].shape[1]
+    for time in range(newer.shape[0]):
+        piece = pieces[time // each]
+        newer[time] = jnp.where(here, piece[0, time % each], received[time])
+        late[time] = piece[1, time % each]
+
+
+def pair_part(mine, received, paired):
+    for chip in range(mine.shape[0]):
+        both = mine[chip].astype(jnp.float32) + received[chip].astype(jnp.float32)
+        paired[chip] = both.astype(jnp.bfloat16)
+
+
+def plane_part(arrived, summed):
+    for time in range(arrived.shape[1]):
+        total = arrived[0, time].astype(jnp.float32)
+        for chip in range(1, arrived.shape[0]):
+            total = total + arrived[chip, time].astype(jnp.float32)
+        summed[time] = total.astype(jnp.bfloat16)
+
+
 def ring(array, axis, by):
     size = lax.axis_size(axis)
     return lax.ppermute(array, axis, [(i, (i + by) % size) for i in range(size)])
@@ -92,8 +130,6 @@
     steps, _, _, fields = arrivals.shape
     planes = lax.axis_size("z")
     chips = lax.axis_size("x") * lax.axis_size("y")
-    plane = lax.axis_index("z")
-    core = lax.axis_index("c").astype(jnp.int32).reshape(1)
     pairs = (block // 2 - 1, sensors, 2 * fields)
     scratch = [pltpu.VMEM((block * params, 2 * fields), jnp.bfloat16)]
     part = jax.ShapeDtypeStruct((chips, block, planes, fields), jnp.bfloat16)
@@ -103,10 +139,6 @@
     pieces = {0: arrivals}
     for source in sources:
         pieces[source] = lax.ppermute(arrivals, "z", [(source, 0)])
-
-    def newer_of(step, received):
-        newest = jnp.concatenate([pieces[i][step] for i in range(planes)], 0)
-        return jnp.where(plane == 0, newest, received)
 
     ordered, upper = pl.pallas_call(
         first_part,
@@ -114,32 +146,58 @@
             jax.ShapeDtypeStruct((sensors, block * params), jnp.bfloat16),
             jax.ShapeDtypeStruct(pairs, jnp.float32),
         ),
-        in_specs=[SMEM, VMEM, VMEM],
+        in_specs=[HBM, HBM],
         out_specs=(VMEM, VMEM),
-        scratch_shapes=scratch,
+        scratch_shapes=scratch
+        + [
+            pltpu.VMEM(kernel.shape, jnp.bfloat16),
+            pltpu.VMEM(history.shape, jnp.bfloat16),
+            pltpu.SemaphoreType.DMA((block + 1,)),
+        ],
         compiler_params=LIMIT,
         cost_estimate=work(2 * 10**9, 4 * 10**6),
         name="first_part",
-    )(core, kernel, history)
-
-    def lower(older, newer, upper):
+    )(kernel, history)
+
+    def lower(older, received, upper, *late):
         return pl.pallas_call(
             lower_part,
             out_shape=(part, part),
-            in_specs=[VMEM] * 4,
+            in_specs=[VMEM] * (4 + len(late)),
             out_specs=(VMEM, VMEM),
             scratch_shapes=scratch,
             compiler_params=LIMIT,
             cost_estimate=work(2 * 10**9, 6 * 10**6),
-            name="lower_part",
-        )(ordered, older, newer, upper)
+        )(ordered, older, received, upper, *late)
 
     def in_plane(mine, theirs):
         received = ring(theirs, "c", 1)
-        paired = (mine.astype(jnp.float32) + received.astype(jnp.float32)).astype(jnp.bfloat16)
-        return exchange(paired, ("x", "y"))
-
-    newer = newer_of(0, shifted)
+        paired = pl.pallas_call(
+            pair_part,
+            out_shape=part,
+            in_specs=[VMEM] * 2,
+            out_specs=VMEM,
+            compiler_params=LIMIT,
+            name="pair_part",
+        )(mine, received)
+        arrived = exchange(paired, ("x", "y"))
+        return pl.pallas_call(
+            plane_part,
+            out_shape=jax.ShapeDtypeStruct((block, planes, fields), jnp.bfloat16),
+            in_specs=[VMEM],
+            out_specs=VMEM,
+            compiler_params=LIMIT,
+            name="plane_part",
+        )(arrived)
+
+    newer, late = pl.pallas_call(
+        newer_part,
+        out_shape=(jax.ShapeDtypeStruct(shifted.shape, jnp.bfloat16),) * 2,
+        in_specs=[VMEM] * (planes + 1),
+        out_specs=(VMEM, VMEM),
+        compiler_params=LIMIT,
+        name="newer_part",
+    )(*[pieces[i] for i in range(planes)], shifted)
     shifted_twice = onward(newer, "z")
     mine, theirs = lower(history, newer, upper)
     arrived_first = in_plane(mine, theirs)
@@ -153,13 +211,10 @@
         cost_estimate=work(10**9, 4 * 10**6),
         name="upper_part",
     )(ordered, newer)
-    newest = newer_of(1, shifted_twice)
-    mine, theirs = lower(newer, newest, upper)
+    mine, theirs = lower(newer, shifted_twice, upper, late)
     arrived_second = in_plane(mine, theirs)
-    summed = jnp.concatenate(
-        [part.astype(jnp.float32).sum(axis=0) for part in (arrived_first, arrived_second)], 0
-    )
-    across = exchange(jnp.moveaxis(summed, 1, 0).astype(jnp.bfloat16), "z")
+    summed = jnp.concatenate([arrived_first, arrived_second], 0)
+    across = exchange(jnp.moveaxis(summed, 1, 0), "z")
     across = across.astype(jnp.float32).sum(axis=0).astype(jnp.bfloat16)
     return across.reshape(steps, block, 1, fields)
 

time: 100 us -> 101 us (1.010)
  waiting for transfers between devices: 48.7 us -> 28.3 us
  starting transfers between devices: 27.3 us -> 46.1 us
  Pallas kernels: 5.65 us -> 12.1 us
  blocking collectives: 13.6 us -> 10 us
  other arithmetic: 2.77 us -> 0.62 us
  local copies, waits for them, and re-layouts: 1.16 us -> 3.18 us
    ppermute x2, waiting for transfers between devices: 22.3 us -> 2.36 us  [onward(): lax.ppermute(array, axis, [(i, i + 1) for i in range(lax.axis_size(axis)...]
    ppermute x7, starting transfers between devices: 10.2 us -> 29.6 us  [observed(): pieces[source] = lax.ppermute(arrivals, 'z', [(source, 0)])]
    pallas_call x1, Pallas kernels: 1.64 us -> 5.92 us  [observed(): pl.pallas_call(first_part, out_shape=(jax.ShapeDtypeStruct((sensors, bloc...]
    all_to_all x1, blocking collectives: 13.6 us -> 10 us  [exchange(): return lax.all_to_all(parts, axis, split_axis=0, concat_axis=0, tiled=True)]
    all_to_all x2, starting transfers between devices: 13 us -> 10.6 us  [exchange(): return lax.all_to_all(parts, axis, split_axis=0, concat_axis=0, tiled=True)]
    pallas_call x2 -> x7, Pallas kernels: 2.88 us -> 5.03 us  [the longest x2 2.88 us: lower(): pl.pallas_call(lower_part, out_shape=(part, part), in_specs=[VMEM] * (4 +...]
    unnamed x11 -> x8, local copies, waits for them, and re-layouts: 1.13 us -> 3.17 us
    ppermute x2, starting transfers between devices: 3.84 us -> 5.74 us  [onward(): lax.ppermute(array, axis, [(i, i + 1) for i in range(lax.axis_size(axis)...]
  transfers between devices with their start and end apart: 13 -> 13, of which waited for: 5 -> 4; matrix products, arithmetic and copies ran while one was open for 3% -> 0% of each run, Pallas kernels for 6% -> 12%
where the time goes in v3:
time: 101 us
  starting transfers between devices  46.1 us (46%)
  waiting for transfers between devices  28.3 us (28%)
  Pallas kernels  12.1 us (12%)
  blocking collectives  10 us (10%)
  local copies, waits for them, and re-layouts  3.18 us (3%)
    ppermute x7, starting transfers between devices, observed(): pieces[source] = lax.ppermute(arrivals, 'z', [(source, 0)])  29.6 us
    all_to_all x2, waiting for transfers between devices, exchange(): return lax.all_to_all(parts, axis, split_axis=0, concat_axis=0, tiled=True)  22 us
    all_to_all x2, starting transfers between devices, exchange(): return lax.all_to_all(parts, axis, split_axis=0, concat_axis=0, tiled=True)  10.6 us
    all_to_all x1, blocking collectives, exchange(): return lax.all_to_all(parts, axis, split_axis=0, concat_axis=0, tiled=True)  10 us
    pallas_call x1, Pallas kernels, observed(): pl.pallas_call(first_part, out_shape=(jax.ShapeDtypeStruct((sensors, bloc...  5.92 us
    ppermute x2, starting transfers between devices, onward(): lax.ppermute(array, axis, [(i, i + 1) for i in range(lax.axis_size(axis)...  5.74 us
    ppermute x7, waiting for transfers between devices, observed(): pieces[source] = lax.ppermute(arrivals, 'z', [(source, 0)])  3.9 us
    unnamed x8, local copies, waits for them, and re-layouts  3.17 us
  transfers between devices with their start and end apart: 13, of which 4 were waited for; matrix products, arithmetic and copies ran while one was open for 0% of the time, Pallas kernels for 12%

profile of v3, /device:TPU:32, one launch (start us, length us, event | category | flops | bytes accessed | tf_op | source)
XLA Modules:
  0.0 100.5 jit_solution(4250314174707385159)
XLA Ops:
  0.0 3.8 %collective-permute-start.7 = (bf16[16,128,128]{2,1,0:T(8,128)(2,1)}, bf16[16,128,128]{2,1,0:T(8,128)(2,1)S(1)}, u32[]{:S(2)}, u32[]{:S(2)}) collective-permute-start(bf16[16,128,128]{2,1,0:T(8,128)(2,1)} %older.1), channel_id=1, source_target_pairs={{0,32},{32,64},{64,96},{96,128},{128,160},{160,192},{192,224},{1,3... | collective-permute-start | bytes 1572872 | tf_op jit(solution)/shard_map/ppermute | solution.py:121
  3.8 0.7 collective-permute-start.5
  4.5 0.7 collective-permute-start.4
  5.2 0.7 collective-permute-start.3
  5.9 0.7 collective-permute-start.2
  6.5 0.0 collective-permute-done.5.refs_6_
  6.5 0.7 collective-permute-start.1
  7.2 0.0 collective-permute-done.4.refs_5_
  7.2 25.6 %collective-permute-start = (bf16[2,2,128,128]{3,2,1,0:T(8,128)(2,1)}, bf16[2,2,128,128]{3,2,1,0:T(8,128)(2,1)S(1)}, u32[]{:S(2)}, u32[]{:S(2)}) collective-permute-start(bf16[2,2,128,128]{3,2,1,0:T(8,128)(2,1)} %refs_0_.1), channel_id=1, source_target_pairs={{32,0},{33,1},{34,2},{35,3},{36,4},{37,5},{38,6},{39,7},{40,8},{41... | collective-permute-start | bytes 393224 | tf_op jit(solution)/shard_map/ppermute | solution.py:141
  32.8 0.0 collective-permute-done.3.refs_4_
  32.8 0.7 collective-permute-start.6
  33.5 0.0 collective-permute-done.2.refs_3_
  33.5 0.0 collective-permute-done.1.refs_2_
  33.5 3.9 %collective-permute-done.refs_1_ = bf16[2,2,128,128]{3,2,1,0:T(8,128)(2,1)S(1)} collective-permute-done((bf16[2,2,128,128]{3,2,1,0:T(8,128)(2,1)}, bf16[2,2,128,128]{3,2,1,0:T(8,128)(2,1)S(1)}, u32[]{:S(2)}, u32[]{:S(2)}) %collective-permute-start) | collective-permute-done | bytes 131104 | tf_op jit(solution)/shard_map/ppermute | solution.py:141
  37.4 0.0 collective-permute-done.6.refs_7_
  37.4 0.0 collective-permute-done.7.refs_8_
  37.4 0.0 copy-start
  37.4 0.9 copy-done
  38.3 0.2 newer_part.1
  38.5 1.9 %collective-permute-start.9 = (bf16[16,128,128]{2,1,0:T(8,128)(2,1)S(1)}, bf16[16,128,128]{2,1,0:T(8,128)(2,1)S(1)}, u32[]{:S(2)}, u32[]{:S(2)}) collective-permute-start(bf16[16,128,128]{2,1,0:T(8,128)(2,1)S(1)} %get-tuple-element.14.received.older), channel_id=1, source_target_pairs={{0,32},{32,64},{64,96},{96,128},{128,160},{160,192},{192,224},{1,3... | collective-permute-start | bytes 1572872 | tf_op jit(solution)/shard_map/ppermute | solution.py:121
  40.4 0.0 copy-start.1
  40.4 1.2 %copy-done.1 = bf16[16,256,128]{2,1,0:T(8,128)(2,1)S(1)} copy-done((bf16[16,256,128]{2,1,0:T(8,128)(2,1)S(1)}, bf16[16,256,128]{2,1,0:T(8,128)(2,1)}, u32[]{:S(2)}) %copy-start.1) | copy-done | bytes 1048600
  41.6 0.0 copy-start.2
  41.6 1.0 %copy-done.2 = bf16[16,128,128]{2,1,0:T(8,128)(2,1)S(1)} copy-done((bf16[16,128,128]{2,1,0:T(8,128)(2,1)S(1)}, bf16[16,128,128]{2,1,0:T(8,128)(2,1)}, u32[]{:S(2)}) %copy-start.2) | copy-done | bytes 524312
  42.7 0.0 copy-start.3
  42.7 5.9 %first_part.1 = (bf16[256,2048]{1,0:T(8,128)(2,1)S(1)}, f32[7,256,256]{2,1,0:T(8,128)S(1)}) custom-call(bf16[16,256,128]{2,1,0:T(8,128)(2,1)S(1)} %copy-done.1, bf16[16,128,128]{2,1,0:T(8,128)(2,1)S(1)} %copy-done.2), custom_call_target="tpu_custom_call" | custom-call | flops 2000000000 | bytes 4000000 | tf_op jit(solution)/shard_map/first_part/pallas_call | solution.py:143
  48.6 0.0 copy-done.3
  48.6 1.4 %shard_map.37 = (bf16[16,16,8,128]{3,2,1,0:T(8,128)(2,1)S(1)}, bf16[16,16,8,128]{3,2,1,0:T(8,128)(2,1)S(1)}) custom-call(bf16[256,2048]{1,0:T(8,128)(2,1)S(1)} %get-tuple-element.13.ordered, bf16[16,128,128]{2,1,0:T(8,128)(2,1)S(1)} %copy-done.3, bf16[16,128,128]{2,1,0:T(8,128)(2,1)S(1)} %get-tuple-element.14.received.older, ...), custom_call_target="tpu_custom_call" | custom-call | flops 2000000000 | bytes 6000000 | tf_op jit(solution)/shard_map/pallas_call | solution.py:163
  50.0 0.1 collective-permute-start.8
  50.1 1.1 %upper_part.1.upper = f32[7,256,256]{2,1,0:T(8,128)S(1)} custom-call(bf16[256,2048]{1,0:T(8,128)(2,1)S(1)} %get-tuple-element.13.ordered, bf16[16,128,128]{2,1,0:T(8,128)(2,1)S(1)} %get-tuple-element.14.received.older), custom_call_target="tpu_custom_call" | custom-call | flops 1000000000 | bytes 4000000 | tf_op jit(solution)/shard_map/upper_part/pallas_call | solution.py:204
  51.3 2.4 %collective-permute-done.9.received = bf16[16,128,128]{2,1,0:T(8,128)(2,1)S(1)} collective-permute-done((bf16[16,128,128]{2,1,0:T(8,128)(2,1)S(1)}, bf16[16,128,128]{2,1,0:T(8,128)(2,1)S(1)}, u32[]{:S(2)}, u32[]{:S(2)}) %collective-permute-start.9) | collective-permute-done | bytes 524320 | tf_op jit(solution)/shard_map/ppermute | solution.py:121
  53.6 1.5 %shard_map.38 = (bf16[16,16,8,128]{3,2,1,0:T(8,128)(2,1)S(1)}, bf16[16,16,8,128]{3,2,1,0:T(8,128)(2,1)S(1)}) custom-call(bf16[256,2048]{1,0:T(8,128)(2,1)S(1)} %get-tuple-element.13.ordered, bf16[16,128,128]{2,1,0:T(8,128)(2,1)S(1)} %get-tuple-element.14.received.older, bf16[16,128,128]{2,1,0:T(8,128)(2,1)S(1)} %collective-permute-done.9.received, ...), custom_call_target="tpu_custom_call" | custom-call | flops 2000000000 | bytes 6000000 | tf_op jit(solution)/shard_map/pallas_call | solution.py:163
  55.1 0.1 collective-permute-start.10
  55.2 0.0 collective-permute-done.8.received
  55.2 0.9 pair_part.2
  56.1 7.0 %all-to-all-start = ((bf16[16,16,8,128]{3,2,1,0:T(8,128)(2,1)}), bf16[16,16,8,128]{3,2,1,0:T(8,128)(2,1)S(1)}, u32[]{:S(2)}, u32[]{:S(2)}) async-start(bf16[16,16,8,128]{3,2,1,0:T(8,128)(2,1)} %pair_part.2), calls=%async_computation | async-start | bytes 1048576 | tf_op jit(solution)/shard_map/all_to_all | solution.py:125
  63.2 0.0 collective-permute-done.10.received
  63.2 0.9 pair_part.3
  64.1 11.2 %all-to-all-done.arrived = bf16[16,16,8,128]{3,2,1,0:T(8,128)(2,1)S(1)} async-done(((bf16[16,16,8,128]{3,2,1,0:T(8,128)(2,1)}), bf16[16,16,8,128]{3,2,1,0:T(8,128)(2,1)S(1)}, u32[]{:S(2)}, u32[]{:S(2)}) %all-to-all-start) | async-done | bytes 524320 | tf_op jit(solution)/shard_map/all_to_all | solution.py:125
  75.3 3.6 %all-to-all-start.1 = ((bf16[16,16,8,128]{3,2,1,0:T(8,128)(2,1)}), bf16[16,16,8,128]{3,2,1,0:T(8,128)(2,1)S(1)}, u32[]{:S(2)}, u32[]{:S(2)}) async-start(bf16[16,16,8,128]{3,2,1,0:T(8,128)(2,1)} %pair_part.3), calls=%async_computation.1 | async-start | bytes 1048576 | tf_op jit(solution)/shard_map/all_to_all | solution.py:125
  78.9 0.1 plane_part.2
  79.0 10.8 %all-to-all-done.1.arrived = bf16[16,16,8,128]{3,2,1,0:T(8,128)(2,1)S(1)} async-done(((bf16[16,16,8,128]{3,2,1,0:T(8,128)(2,1)}), bf16[16,16,8,128]{3,2,1,0:T(8,128)(2,1)S(1)}, u32[]{:S(2)}, u32[]{:S(2)}) %all-to-all-start.1) | async-done | bytes 524320 | tf_op jit(solution)/shard_map/all_to_all | solution.py:125
  89.8 0.1 plane_part.3
  89.9 10.0 %all_to_all.15 = bf16[8,32,128]{2,1,0:T(8,128)(2,1)S(1)} all-to-all(bf16[8,32,128]{2,1,0:T(8,128)(2,1)S(1)} %copy.4), channel_id=1, replica_groups=mesh['z'=8,'x'=4,'y'=4,'c'=2] {'z'}, dimensions={0} | all-to-all | bytes 131072 | tf_op jit(solution)/shard_map/all_to_all | solution.py:125
  99.9 0.6 reduce_sum.12
  (2 shorter events, 0.0 us)
Async XLA Ops:
  0.0 37.4 %collective-permute-start.7 = (bf16[16,128,128]{2,1,0:T(8,128)(2,1)}, bf16[16,128,128]{2,1,0:T(8,128)(2,1)S(1)}, u32[]{:S(2)}, u32[]{:S(2)}) collective-permute-start(bf16[16,128,128]{2,1,0:T(8,128)(2,1)} %older.1), channel_id=1, source_target_pairs={{0,32},{32,64},{64,96},{96,128},{128,160},{160,192},{192,224},{1,3... | collective-permute-start | bytes 1572872 | tf_op jit(solution)/shard_map/ppermute | solution.py:121
  3.8 2.7 %collective-permute-start.5 = (bf16[2,2,128,128]{3,2,1,0:T(8,128)(2,1)}, bf16[2,2,128,128]{3,2,1,0:T(8,128)(2,1)S(1)}, u32[]{:S(2)}, u32[]{:S(2)}) collective-permute-start(bf16[2,2,128,128]{3,2,1,0:T(8,128)(2,1)} %refs_0_.1), channel_id=1, source_target_pairs={{192,0},{193,1},{194,2},{195,3},{196,4},{197,5},{198,6},{199,7},{2... | collective-permute-start | bytes 393224 | tf_op jit(solution)/shard_map/ppermute | solution.py:141
  4.5 2.7 %collective-permute-start.4 = (bf16[2,2,128,128]{3,2,1,0:T(8,128)(2,1)}, bf16[2,2,128,128]{3,2,1,0:T(8,128)(2,1)S(1)}, u32[]{:S(2)}, u32[]{:S(2)}) collective-permute-start(bf16[2,2,128,128]{3,2,1,0:T(8,128)(2,1)} %refs_0_.1), channel_id=1, source_target_pairs={{160,0},{161,1},{162,2},{163,3},{164,4},{165,5},{166,6},{167,7},{1... | collective-permute-start | bytes 393224 | tf_op jit(solution)/shard_map/ppermute | solution.py:141
  5.2 27.6 %collective-permute-start.3 = (bf16[2,2,128,128]{3,2,1,0:T(8,128)(2,1)}, bf16[2,2,128,128]{3,2,1,0:T(8,128)(2,1)S(1)}, u32[]{:S(2)}, u32[]{:S(2)}) collective-permute-start(bf16[2,2,128,128]{3,2,1,0:T(8,128)(2,1)} %refs_0_.1), channel_id=1, source_target_pairs={{128,0},{129,1},{130,2},{131,3},{132,4},{133,5},{134,6},{135,7},{1... | collective-permute-start | bytes 393224 | tf_op jit(solution)/shard_map/ppermute | solution.py:141
  5.9 27.6 %collective-permute-start.2 = (bf16[2,2,128,128]{3,2,1,0:T(8,128)(2,1)}, bf16[2,2,128,128]{3,2,1,0:T(8,128)(2,1)S(1)}, u32[]{:S(2)}, u32[]{:S(2)}) collective-permute-start(bf16[2,2,128,128]{3,2,1,0:T(8,128)(2,1)} %refs_0_.1), channel_id=1, source_target_pairs={{96,0},{97,1},{98,2},{99,3},{100,4},{101,5},{102,6},{103,7},{104,8... | collective-permute-start | bytes 393224 | tf_op jit(solution)/shard_map/ppermute | solution.py:141
  6.5 27.0 %collective-permute-start.1 = (bf16[2,2,128,128]{3,2,1,0:T(8,128)(2,1)}, bf16[2,2,128,128]{3,2,1,0:T(8,128)(2,1)S(1)}, u32[]{:S(2)}, u32[]{:S(2)}) collective-permute-start(bf16[2,2,128,128]{3,2,1,0:T(8,128)(2,1)} %refs_0_.1), channel_id=1, source_target_pairs={{64,0},{65,1},{66,2},{67,3},{68,4},{69,5},{70,6},{71,7},{72,8},{73... | collective-permute-start | bytes 393224 | tf_op jit(solution)/shard_map/ppermute | solution.py:141
  7.2 30.2 %collective-permute-start = (bf16[2,2,128,128]{3,2,1,0:T(8,128)(2,1)}, bf16[2,2,128,128]{3,2,1,0:T(8,128)(2,1)S(1)}, u32[]{:S(2)}, u32[]{:S(2)}) collective-permute-start(bf16[2,2,128,128]{3,2,1,0:T(8,128)(2,1)} %refs_0_.1), channel_id=1, source_target_pairs={{32,0},{33,1},{34,2},{35,3},{36,4},{37,5},{38,6},{39,7},{40,8},{41... | collective-permute-start | bytes 393224 | tf_op jit(solution)/shard_map/ppermute | solution.py:141
  32.8 4.6 %collective-permute-start.6 = (bf16[2,2,128,128]{3,2,1,0:T(8,128)(2,1)}, bf16[2,2,128,128]{3,2,1,0:T(8,128)(2,1)S(1)}, u32[]{:S(2)}, u32[]{:S(2)}) collective-permute-start(bf16[2,2,128,128]{3,2,1,0:T(8,128)(2,1)} %refs_0_.1), channel_id=1, source_target_pairs={{224,0},{225,1},{226,2},{227,3},{228,4},{229,5},{230,6},{231,7},{2... | collective-permute-start | bytes 393224 | tf_op jit(solution)/shard_map/ppermute | solution.py:141
  37.4 0.9 copy-start
  38.5 15.2 %collective-permute-start.9 = (bf16[16,128,128]{2,1,0:T(8,128)(2,1)S(1)}, bf16[16,128,128]{2,1,0:T(8,128)(2,1)S(1)}, u32[]{:S(2)}, u32[]{:S(2)}) collective-permute-start(bf16[16,128,128]{2,1,0:T(8,128)(2,1)S(1)} %get-tuple-element.14.received.older), channel_id=1, source_target_pairs={{0,32},{32,64},{64,96},{96,128},{128,160},{160,192},{192,224},{1,3... | collective-permute-start | bytes 1572872 | tf_op jit(solution)/shard_map/ppermute | solution.py:121
  40.4 1.2 %copy-start.1 = (bf16[16,256,128]{2,1,0:T(8,128)(2,1)S(1)}, bf16[16,256,128]{2,1,0:T(8,128)(2,1)}, u32[]{:S(2)}) copy-start(bf16[16,256,128]{2,1,0:T(8,128)(2,1)} %kernel_hbm.1) | copy-start | bytes 3145732
  41.6 1.0 %copy-start.2 = (bf16[16,128,128]{2,1,0:T(8,128)(2,1)S(1)}, bf16[16,128,128]{2,1,0:T(8,128)(2,1)}, u32[]{:S(2)}) copy-start(bf16[16,128,128]{2,1,0:T(8,128)(2,1)} %older.1) | copy-start | bytes 1572868
  42.7 5.9 %copy-start.3 = (bf16[16,128,128]{2,1,0:T(8,128)(2,1)S(1)}, bf16[16,128,128]{2,1,0:T(8,128)(2,1)}, u32[]{:S(2)}) copy-start(bf16[16,128,128]{2,1,0:T(8,128)(2,1)} %older.1) | copy-start | bytes 1572868
  50.0 5.2 %collective-permute-start.8 = (bf16[16,16,8,128]{3,2,1,0:T(8,128)(2,1)S(1)}, bf16[16,16,8,128]{3,2,1,0:T(8,128)(2,1)S(1)}, u32[]{:S(2)}, u32[]{:S(2)}) collective-permute-start(bf16[16,16,8,128]{3,2,1,0:T(8,128)(2,1)S(1)} %get-tuple-element.17), channel_id=1, source_target_pairs={{0,1},{1,0},{2,3},{3,2},{4,5},{5,4},{6,7},{7,6},{8,9},{9,8},{10,11... | collective-permute-start | bytes 1572872 | tf_op jit(solution)/shard_map/ppermute | solution.py:117
  55.1 8.1 %collective-permute-start.10 = (bf16[16,16,8,128]{3,2,1,0:T(8,128)(2,1)S(1)}, bf16[16,16,8,128]{3,2,1,0:T(8,128)(2,1)S(1)}, u32[]{:S(2)}, u32[]{:S(2)}) collective-permute-start(bf16[16,16,8,128]{3,2,1,0:T(8,128)(2,1)S(1)} %get-tuple-element.20), channel_id=1, source_target_pairs={{0,1},{1,0},{2,3},{3,2},{4,5},{5,4},{6,7},{7,6},{8,9},{9,8},{10,11... | collective-permute-start | bytes 1572872 | tf_op jit(solution)/shard_map/ppermute | solution.py:117
  56.1 19.2 %all-to-all-start = ((bf16[16,16,8,128]{3,2,1,0:T(8,128)(2,1)}), bf16[16,16,8,128]{3,2,1,0:T(8,128)(2,1)S(1)}, u32[]{:S(2)}, u32[]{:S(2)}) async-start(bf16[16,16,8,128]{3,2,1,0:T(8,128)(2,1)} %pair_part.2), calls=%async_computation | async-start | bytes 1048576 | tf_op jit(solution)/shard_map/all_to_all | solution.py:125
  75.3 14.5 %all-to-all-start.1 = ((bf16[16,16,8,128]{3,2,1,0:T(8,128)(2,1)}), bf16[16,16,8,128]{3,2,1,0:T(8,128)(2,1)S(1)}, u32[]{:S(2)}, u32[]{:S(2)}) async-start(bf16[16,16,8,128]{3,2,1,0:T(8,128)(2,1)} %pair_part.3), calls=%async_computation.1 | async-start | bytes 1048576 | tf_op jit(solution)/shard_map/all_to_all | solution.py:125

commit v4 on v2

v4 whole, which is shorter than its diff:
```python
import functools

import jax
import jax.numpy as jnp
from jax import lax
from jax.experimental import pallas as pl
from jax.experimental.pallas import tpu as pltpu
from jax.sharding import Mesh
from jax.sharding import PartitionSpec as P

ORDER = (5, 6, 7, 4, 3, 2, 1)
PAR = ("x", "y", "c")
EVERY = ("z", "x", "y", "c")
VMEM = pl.BlockSpec(memory_space=pltpu.VMEM)
LIMIT = pltpu.CompilerParams(vmem_limit_bytes=8 * 1024 * 1024)


def work(flops, nbytes):
    return pl.CostEstimate(flops=flops, bytes_accessed=nbytes, transcendentals=0)


def upper_part(ordered, older, upper, times):
    block, params, fields = older.shape
    last = block - 2
    for time in range(1, block):
        if time <= last:
            times[(last - time) * params : (last - time + 1) * params, :fields] = older[time]
        if time >= 2:
            at = last + 1 - time
            times[at * params : (at + 1) * params, fields:] = older[time]
    for pair in range(block // 2 - 1):
        lag = (2 * pair + 2) * params
        upper[pair] = jnp.dot(
            ordered[:, lag:], times[: block * params - lag], preferred_element_type=jnp.float32
        )


def order_rows(kernel, ordered):
    lags, sensors, params = kernel.shape
    planes = 8
    half = sensors // 2
    row = lax.broadcasted_iota(jnp.int32, (sensors, sensors), 0)
    col = lax.broadcasted_iota(jnp.int32, (sensors, sensors), 1)
    other = (row >= half).astype(jnp.int32)
    place = row - half * other
    core = lax.axis_index("c")
    parity = core + other - 2 * core * other
    sensor = (place % planes) * (sensors // planes) + (place // planes) * 2 + parity
    select = (col == sensor).astype(jnp.bfloat16)
    for lag in range(lags):
        rows = jnp.dot(select, kernel[lag], preferred_element_type=jnp.float32)
        ordered[:, lag * params : (lag + 1) * params] = rows.astype(jnp.bfloat16)


def first_part(kernel, older, ordered, leading, upper, times):
    order_rows(kernel, ordered)
    leading[...] = ordered[:, : leading.shape[1]]
    upper_part(ordered, older, upper, times)


def windows(value, low, high, params, fields, times):
    for time in range(low, high + 2):
        if time <= high:
            times[(high - time) * params : (high - time + 1) * params, :fields] = value(time)
        if time > low:
            at = high + 1 - time
            times[at * params : (at + 1) * params, fields:] = value(time)


def put(sums, pair, mine, theirs):
    half = sums.shape[0] // 2
    fields = sums.shape[1] // 2
    sums = sums.astype(jnp.bfloat16)
    for odd in range(2):
        part = sums[:, odd * fields : (odd + 1) * fields]
        mine[:, 2 * pair + odd] = part[:half].reshape(mine.shape[0], mine.shape[2], fields)
        theirs[:, 2 * pair + odd] = part[half:].reshape(mine.shape[0], mine.shape[2], fields)


def second_part(
    ordered, following, older, newer, head, last, mine, theirs, ahead, behind, arrivals
):
    block, params, fields = older.shape
    lags = following.shape[1] // params
    plane = lax.axis_index("z")

    def after(first, then):
        return lambda time: first[time] if time < block else then[time - block]

    windows(after(older, newer), lags + 1, 2 * block - 2, params, fields, ahead)

    def conv(left, right, pair):
        start = (block - 2 - 2 * pair) * params
        return jnp.dot(
            left, right[start : start + left.shape[1]], preferred_element_type=jnp.float32
        )

    @pl.when(plane != 0)
    def _():
        windows(after(newer, head), 1, 2 * block - 2 - lags, params, fields, behind)
        for pair in range(block // 2):
            sums = conv(following[...], ahead, pair)
            sums = sums + conv(ordered[:, lags * params :], behind, pair)
            put(sums, pair, mine, theirs)

    @pl.when(plane == 0)
    def _():
        windows(after(newer, last), 1, 2 * block - 2, params, fields, arrivals)
        for pair in range(block // 2):
            sums = conv(following[...], ahead, pair) + conv(ordered[...], arrivals, pair)
            put(sums, pair, mine, theirs)


def lower_part(ordered, older, newer, upper, mine, theirs, times):
    block, params, fields = newer.shape
    for time in range(-1, block):
        value = newer[time] if time >= 0 else older[block - 1]
        at = block - 2 - time
        if time <= block - 2:
            times[at * params : (at + 1) * params, :fields] = value
        if time >= 0:
            times[(at + 1) * params : (at + 2) * params, fields:] = value
    for pair in range(block // 2):
        lag = (2 * pair + 2) * params
        sums = jnp.dot(
            ordered[:, :lag], times[block * params - lag :], preferred_element_type=jnp.float32
        )
        if pair < block // 2 - 1:
            sums = sums + upper[pair]
        put(sums, pair, mine, theirs)


def head_part(*refs):
    *pieces, received, head = refs
    here = lax.axis_index("z") == 0
    each = pieces[0].shape[1]
    for time in range(head.shape[0]):
        piece = pieces[time // each]
        head[time] = jnp.where(here, piece[0, time % each], received[time])


def newer_part(*refs):
    *pieces, received, newer, last = refs
    here = lax.axis_index("z") == 0
    each = pieces[0].shape[1]
    for time in range(newer.shape[0]):
        piece = pieces[time // each]
        newer[time] = jnp.where(here, piece[0, time % each], received[time])
        last[time] = piece[1, time % each]


def pair_part(step, mine, received, *refs):
    paired = refs[-1]
    block = mine.shape[1]
    for chip in range(mine.shape[0]):
        both = mine[chip].astype(jnp.float32) + received[chip].astype(jnp.float32)
        paired[chip, step * block : (step + 1) * block] = both.astype(jnp.bfloat16)


def plane_part(arrived, summed):
    for time in range(arrived.shape[1]):
        total = arrived[0, time].astype(jnp.float32)
        for chip in range(1, arrived.shape[0]):
            total = total + arrived[chip, time].astype(jnp.float32)
        summed[time] = total.astype(jnp.bfloat16)


def ring(array, axis, by):
    size = lax.axis_size(axis)
    return lax.ppermute(array, axis, [(i, (i + by) % size) for i in range(size)])


def onward(array, axis, by):
    size = lax.axis_size(axis)
    return lax.ppermute(array, axis, [(i, i + by) for i in range(size) if 0 <= i + by < size])


def exchange(parts, axis):
    return lax.all_to_all(parts, axis, split_axis=0, concat_axis=0, tiled=True)


def observed(kernel, history, arrivals):
    block, sensors, params = kernel.shape
    steps, _, _, fields = arrivals.shape
    planes = lax.axis_size("z")
    chips = lax.axis_size("x") * lax.axis_size("y")
    pairs = (block // 2 - 1, sensors, 2 * fields)
    scratch = [pltpu.VMEM((block * params, 2 * fields), jnp.bfloat16)]
    part = jax.ShapeDtypeStruct((chips, block, planes, fields), jnp.bfloat16)

    shifted = onward(history, "z", 1)
    pieces = [arrivals] + [None] * (planes - 1)
    for source in ORDER:
        pieces[source] = lax.ppermute(arrivals, "z", [(source, 0)])

    ordered, leading, upper = pl.pallas_call(
        first_part,
        out_shape=(
            jax.ShapeDtypeStruct((sensors, block * params), jnp.bfloat16),
            jax.ShapeDtypeStruct((sensors, block // 2 * params), jnp.bfloat16),
            jax.ShapeDtypeStruct(pairs, jnp.float32),
        ),
        in_specs=[VMEM, VMEM],
        out_specs=(VMEM, VMEM, VMEM),
        scratch_shapes=scratch,
        compiler_params=LIMIT,
        cost_estimate=work(2 * 10**9, 4 * 10**6),
        name="first_part",
    )(kernel, history)

    following = onward(leading, "z", -1)

    def pair(step, mine, theirs, *paired):
        received = ring(theirs, "c", 1)
        return pl.pallas_call(
            functools.partial(pair_part, step),
            out_shape=jax.ShapeDtypeStruct((chips, steps * block, planes, fields), jnp.bfloat16),
            in_specs=[VMEM] * (2 + len(paired)),
            out_specs=VMEM,
            input_output_aliases={2: 0} if paired else {},
            compiler_params=LIMIT,
            name="pair_part",
        )(mine, received, *paired)

    near = planes // 2
    head = pl.pallas_call(
        head_part,
        out_shape=jax.ShapeDtypeStruct((block // 2, params, fields), jnp.bfloat16),
        in_specs=[VMEM] * (near + 1),
        out_specs=VMEM,
        compiler_params=LIMIT,
        name="head_part",
    )(*pieces[:near], shifted)
    head_twice = onward(head, "z", 1)
    newer, last = pl.pallas_call(
        newer_part,
        out_shape=(jax.ShapeDtypeStruct(shifted.shape, jnp.bfloat16),) * 2,
        in_specs=[VMEM] * (planes + 1),
        out_specs=(VMEM, VMEM),
        compiler_params=LIMIT,
        name="newer_part",
    )(*pieces, shifted)
    mine, theirs = pl.pallas_call(
        lower_part,
        out_shape=(part, part),
        in_specs=[VMEM] * 4,
        out_specs=(VMEM, VMEM),
        scratch_shapes=scratch,
        compiler_params=LIMIT,
        cost_estimate=work(2 * 10**9, 6 * 10**6),
        name="lower_part",
    )(ordered, history, newer, upper)
    paired = pair(0, mine, theirs)
    width = 2 * fields
    mine, theirs = pl.pallas_call(
        second_part,
        out_shape=(part, part),
        in_specs=[VMEM] * 6,
        out_specs=(VMEM, VMEM),
        scratch_shapes=[
            pltpu.VMEM(((3 * block // 2 - 2) * params, width), jnp.bfloat16),
            pltpu.VMEM(((3 * block // 2 - 2) * params, width), jnp.bfloat16),
            pltpu.VMEM(((2 * block - 2) * params, width), jnp.bfloat16),
        ],
        compiler_params=pltpu.CompilerParams(vmem_limit_bytes=12 * 1024 * 1024),
        cost_estimate=work(4 * 10**9, 8 * 10**6),
        name="second_part",
    )(ordered, following, history, newer, head_twice, last)
    paired = pair(1, mine, theirs, paired)
    arrived = exchange(paired, ("x", "y"))
    summed = pl.pallas_call(
        plane_part,
        out_shape=jax.ShapeDtypeStruct((steps * block, planes, fields), jnp.bfloat16),
        in_specs=[VMEM],
        out_specs=VMEM,
        compiler_params=LIMIT,
        name="plane_part",
    )(arrived)
    across = exchange(jnp.moveaxis(summed, 1, 0), "z")
    across = across.astype(jnp.float32).sum(axis=0).astype(jnp.bfloat16)
    return across.reshape(steps, block, 1, fields)


def solution(mesh):
    split = Mesh(mesh.devices.reshape(mesh.shape["tm"], 4, 4, 2), EVERY)
    placed = (P("z", None, PAR), P("z", PAR, None), P(None, "z", PAR, None))
    return jax.shard_map(
        observed,
        mesh=split,
        in_specs=placed,
        out_specs=P(None, None, EVERY, None),
        check_vma=False,
    )
```

time: 100 us -> 89.9 us (0.90)
  blocking collectives: 13.6 us -> 42.1 us
  waiting for transfers between devices: 48.7 us -> 22.7 us
  starting transfers between devices: 27.3 us -> 14.8 us
  other arithmetic: 2.77 us -> 0.61 us
  local copies, waits for them, and re-layouts: 1.16 us -> 2.28 us
    all_to_all x1 -> x2, blocking collectives: 13.6 us -> 42.1 us  [exchange(): return lax.all_to_all(parts, axis, split_axis=0, concat_axis=0, tiled=True)]
    all_to_all x2 -> x0, waiting for transfers between devices: 22 us -> none  [exchange(): return lax.all_to_all(parts, axis, split_axis=0, concat_axis=0, tiled=True)]
    ppermute x2 -> x3, waiting for transfers between devices: 22.3 us -> 7.46 us  [onward(): lax.ppermute(array, axis, [(i, i + by) for i in range(size) if 0 <= i + b...]
    all_to_all x2 -> x0, starting transfers between devices: 13 us -> none  [exchange(): return lax.all_to_all(parts, axis, split_axis=0, concat_axis=0, tiled=True)]
    ppermute x7, waiting for transfers between devices: 4.36 us -> 13.5 us  [observed(): pieces[source] = lax.ppermute(arrivals, 'z', [(source, 0)])]
    ppermute x2 -> x3, starting transfers between devices: 3.84 us -> 8.67 us  [onward(): lax.ppermute(array, axis, [(i, i + by) for i in range(size) if 0 <= i + b...]
    ppermute x7, starting transfers between devices: 10.2 us -> 5.92 us  [observed(): pieces[source] = lax.ppermute(arrivals, 'z', [(source, 0)])]
    convert_element_type x3 -> x0, other arithmetic: 1.89 us -> none  [the longest x2 1.88 us: in_plane(): (mine.astype(jnp.float32) + received.astype(jnp.float32)).astype(jnp.bflo...]
  transfers between devices with their start and end apart: 13 -> 12, of which waited for: 5 -> 3; matrix products, arithmetic and copies ran while one was open for 3% -> 0% of each run, Pallas kernels for 6% -> 7%
where the time goes in v4:
time: 89.9 us; the launch traced here: 89.1 us
  blocking collectives  42.1 us (47%)
  waiting for transfers between devices  22.7 us (25%)
  starting transfers between devices  14.8 us (16%)
  Pallas kernels  6.38 us (7%)
  local copies, waits for them, and re-layouts  2.28 us (3%)
    all_to_all x2, blocking collectives, exchange(): return lax.all_to_all(parts, axis, split_axis=0, concat_axis=0, tiled=True)  42.1 us
    ppermute x7, waiting for transfers between devices, observed(): pieces[source] = lax.ppermute(arrivals, 'z', [(source, 0)])  13.5 us
    ppermute x3, starting transfers between devices, onward(): lax.ppermute(array, axis, [(i, i + by) for i in range(size) if 0 <= i + b...  8.67 us
    ppermute x3, waiting for transfers between devices, onward(): lax.ppermute(array, axis, [(i, i + by) for i in range(size) if 0 <= i + b...  7.46 us
    ppermute x7, starting transfers between devices, observed(): pieces[source] = lax.ppermute(arrivals, 'z', [(source, 0)])  5.92 us
    pallas_call x1, Pallas kernels, observed(): pl.pallas_call(second_part, out_shape=(part, part), in_specs=[VMEM] * 6,...  2.55 us
    unnamed x8, local copies, waits for them, and re-layouts  2.27 us
  transfers between devices with their start and end apart: 12, of which 3 were waited for; matrix products, arithmetic and copies ran while one was open for 0% of the time, Pallas kernels for 7%

profile of v4, /device:TPU:32, one launch (start us, length us, event | category | flops | bytes accessed | tf_op | source)
XLA Modules:
  0.0 89.1 jit_solution(18299389526029192137)
XLA Ops:
  0.0 0.0 copy-start
  0.0 3.9 %collective-permute-start.8 = (bf16[16,128,128]{2,1,0:T(8,128)(2,1)}, bf16[16,128,128]{2,1,0:T(8,128)(2,1)S(1)}, u32[]{:S(2)}, u32[]{:S(2)}) collective-permute-start(bf16[16,128,128]{2,1,0:T(8,128)(2,1)} %older.5), channel_id=1, source_target_pairs={{0,32},{32,64},{64,96},{96,128},{128,160},{160,192},{192,224},{1,3... | collective-permute-start | bytes 1572872 | tf_op jit(solution)/shard_map/ppermute | solution.py:175
  4.0 0.7 collective-permute-start.3
  4.6 0.0 copy-start.1
  4.6 1.2 %copy-done.1 = bf16[16,256,128]{2,1,0:T(8,128)(2,1)S(1)} copy-done((bf16[16,256,128]{2,1,0:T(8,128)(2,1)S(1)}, bf16[16,256,128]{2,1,0:T(8,128)(2,1)}, u32[]{:S(2)}) %copy-start.1) | copy-done | bytes 1048600
  5.9 0.0 copy-start.2
  5.9 1.0 %copy-done.2 = bf16[16,128,128]{2,1,0:T(8,128)(2,1)S(1)} copy-done((bf16[16,128,128]{2,1,0:T(8,128)(2,1)S(1)}, bf16[16,128,128]{2,1,0:T(8,128)(2,1)}, u32[]{:S(2)}) %copy-start.2) | copy-done | bytes 524312
  6.9 1.8 %first_part.1 = (bf16[256,2048]{1,0:T(8,128)(2,1)S(1)}, bf16[256,1024]{1,0:T(8,128)(2,1)S(1)}, f32[7,256,256]{2,1,0:T(8,128)S(1)}) custom-call(bf16[16,256,128]{2,1,0:T(8,128)(2,1)S(1)} %copy-done.1, bf16[16,128,128]{2,1,0:T(8,128)(2,1)S(1)} %copy-done.2), custom_call_target="tpu_custom_call" | custom-call | flops 2000000000 | bytes 4000000 | tf_op jit(solution)/shard_map/first_part/pallas_call | solution.py:196
  8.7 0.0 copy-start.3
  8.7 2.8 %collective-permute-start = (bf16[256,1024]{1,0:T(8,128)(2,1)S(1)}, bf16[256,1024]{1,0:T(8,128)(2,1)S(1)}, u32[]{:S(2)}, u32[]{:S(2)}) collective-permute-start(bf16[256,1024]{1,0:T(8,128)(2,1)S(1)} %get-tuple-element.15), channel_id=1, source_target_pairs={{32,0},{64,32},{96,64},{128,96},{160,128},{192,160},{224,192},{33,... | collective-permute-start | bytes 1572872 | tf_op jit(solution)/shard_map/ppermute | solution.py:175
  11.5 0.0 copy-done
  11.5 0.7 collective-permute-start.2
  12.2 1.9 %collective-permute-start.1 = (bf16[2,2,128,128]{3,2,1,0:T(8,128)(2,1)S(1)}, bf16[2,2,128,128]{3,2,1,0:T(8,128)(2,1)S(1)}, u32[]{:S(2)}, u32[]{:S(2)}) collective-permute-start(bf16[2,2,128,128]{3,2,1,0:T(8,128)(2,1)S(1)} %copy-done), channel_id=1, source_target_pairs={{32,0},{33,1},{34,2},{35,3},{36,4},{37,5},{38,6},{39,7},{40,8},{41... | collective-permute-start | bytes 393224 | tf_op jit(solution)/shard_map/ppermute | solution.py:194
  14.1 0.0 collective-permute-done.3.refs_3_
  14.1 0.7 collective-permute-start.7
  14.8 0.0 collective-permute-done.2.refs_2_
  14.8 0.7 collective-permute-start.6
  15.5 13.5 %collective-permute-done.1.refs_1_ = bf16[2,2,128,128]{3,2,1,0:T(8,128)(2,1)S(1)} collective-permute-done((bf16[2,2,128,128]{3,2,1,0:T(8,128)(2,1)S(1)}, bf16[2,2,128,128]{3,2,1,0:T(8,128)(2,1)S(1)}, u32[]{:S(2)}, u32[]{:S(2)}) %collective-permute-start.1) | collective-permute-done | bytes 131104 | tf_op jit(solution)/shard_map/ppermute | solution.py:194
  29.0 0.7 collective-permute-start.5
  29.6 0.0 collective-permute-done.8.refs_8_.refs_4_
  29.6 0.7 collective-permute-start.4
  30.3 0.1 head_part.1
  30.4 0.0 collective-permute-done.7.refs_7_
  30.4 1.9 %collective-permute-start.9 = (bf16[8,128,128]{2,1,0:T(8,128)(2,1)S(1)}, bf16[8,128,128]{2,1,0:T(8,128)(2,1)S(1)}, u32[]{:S(2)}, u32[]{:S(2)}) collective-permute-start(bf16[8,128,128]{2,1,0:T(8,128)(2,1)S(1)} %head_part.1), channel_id=1, source_target_pairs={{0,32},{32,64},{64,96},{96,128},{128,160},{160,192},{192,224},{1,3... | collective-permute-start | bytes 786440 | tf_op jit(solution)/shard_map/ppermute | solution.py:175
  32.3 0.0 collective-permute-done.6.refs_6_
  32.4 0.0 collective-permute-done.5.refs_5_
  32.4 0.0 collective-permute-done.4.refs_4_
  32.4 0.2 newer_part.1
  32.6 0.0 copy-done.3
  32.6 1.4 %lower_part.1 = (bf16[16,16,8,128]{3,2,1,0:T(8,128)(2,1)S(1)}, bf16[16,16,8,128]{3,2,1,0:T(8,128)(2,1)S(1)}) custom-call(bf16[256,2048]{1,0:T(8,128)(2,1)S(1)} %get-tuple-element.14.ordered, bf16[16,128,128]{2,1,0:T(8,128)(2,1)S(1)} %copy-done.3, bf16[16,128,128]{2,1,0:T(8,128)(2,1)S(1)} %get-tuple-element.16.newer, f32[7,256,256]{2,1,0:T(8,128)S(1)} %get-tuple-element.20.upper), custom_call_target="tpu_custom_call" | custom-call | flops 2000000000 | bytes 6000000 | tf_op jit(solution)/shard_map/lower_part/pallas_call | solution.py:243
  34.0 0.1 collective-permute-start.11
  34.1 0.0 collective-permute-done.following
  34.1 7.5 %collective-permute-done.9.head = bf16[8,128,128]{2,1,0:T(8,128)(2,1)S(1)} collective-permute-done((bf16[8,128,128]{2,1,0:T(8,128)(2,1)S(1)}, bf16[8,128,128]{2,1,0:T(8,128)(2,1)S(1)}, u32[]{:S(2)}, u32[]{:S(2)}) %collective-permute-start.9) | collective-permute-done | bytes 262176 | tf_op jit(solution)/shard_map/ppermute | solution.py:175
  41.6 2.6 %second_part.1 = (bf16[16,16,8,128]{3,2,1,0:T(8,128)(2,1)S(1)}, bf16[16,16,8,128]{3,2,1,0:T(8,128)(2,1)S(1)}) custom-call(bf16[256,2048]{1,0:T(8,128)(2,1)S(1)} %get-tuple-element.14.ordered, bf16[256,1024]{1,0:T(8,128)(2,1)S(1)} %collective-permute-done.following, bf16[16,128,128]{2,1,0:T(8,128)(2,1)S(1)} %copy-done.3, ...), custom_call_target="tpu_custom_call" | custom-call | flops 4000000000 | bytes 8000000 | tf_op jit(solution)/shard_map/second_part/pallas_call | solution.py:255
  44.1 0.1 collective-permute-start.10
  44.2 0.0 collective-permute-done.11.received
  44.2 0.1 pair_part.2.refs_0_
  44.4 1.8 %collective-permute-done.10.received = bf16[16,16,8,128]{3,2,1,0:T(8,128)(2,1)S(1)} collective-permute-done((bf16[16,16,8,128]{3,2,1,0:T(8,128)(2,1)S(1)}, bf16[16,16,8,128]{3,2,1,0:T(8,128)(2,1)S(1)}, u32[]{:S(2)}, u32[]{:S(2)}) %collective-permute-start.10) | collective-permute-done | bytes 524320 | tf_op jit(solution)/shard_map/ppermute | solution.py:170
  46.1 0.1 pair_part.3
  46.2 24.3 %all_to_all.10.arrived = bf16[16,32,8,128]{3,2,1,0:T(8,128)(2,1)S(1)} all-to-all(bf16[16,32,8,128]{3,2,1,0:T(8,128)(2,1)S(1)} %pair_part.3), channel_id=1, replica_groups=mesh['z'=8,'x'=4,'y'=4,'c'=2] {'x','y'}, dimensions={0} | all-to-all | bytes 2097152 | tf_op jit(solution)/shard_map/all_to_all | solution.py:179
  70.5 0.1 plane_part.1
  70.7 17.8 %all_to_all.11 = bf16[8,32,128]{2,1,0:T(8,128)(2,1)S(1)} all-to-all(bf16[8,32,128]{2,1,0:T(8,128)(2,1)S(1)} %copy.5), channel_id=1, replica_groups=mesh['z'=8,'x'=4,'y'=4,'c'=2] {'z'}, dimensions={0} | all-to-all | bytes 131072 | tf_op jit(solution)/shard_map/all_to_all | solution.py:179
  88.5 0.6 reduce_sum.12
  (1 shorter events, 0.0 us)
Async XLA Ops:
  0.0 11.5 %copy-start = (bf16[2,2,128,128]{3,2,1,0:T(8,128)(2,1)S(1)}, bf16[2,2,128,128]{3,2,1,0:T(8,128)(2,1)}, u32[]{:S(2)}) copy-start(bf16[2,2,128,128]{3,2,1,0:T(8,128)(2,1)} %refs_0_.3) | copy-start | bytes 393220
  0.0 29.6 %collective-permute-start.8 = (bf16[16,128,128]{2,1,0:T(8,128)(2,1)}, bf16[16,128,128]{2,1,0:T(8,128)(2,1)S(1)}, u32[]{:S(2)}, u32[]{:S(2)}) collective-permute-start(bf16[16,128,128]{2,1,0:T(8,128)(2,1)} %older.5), channel_id=1, source_target_pairs={{0,32},{32,64},{64,96},{96,128},{128,160},{160,192},{192,224},{1,3... | collective-permute-start | bytes 1572872 | tf_op jit(solution)/shard_map/ppermute | solution.py:175
  4.0 10.2 %collective-permute-start.3 = (bf16[2,2,128,128]{3,2,1,0:T(8,128)(2,1)}, bf16[2,2,128,128]{3,2,1,0:T(8,128)(2,1)S(1)}, u32[]{:S(2)}, u32[]{:S(2)}) collective-permute-start(bf16[2,2,128,128]{3,2,1,0:T(8,128)(2,1)} %refs_0_.3), channel_id=1, source_target_pairs={{96,0},{97,1},{98,2},{99,3},{100,4},{101,5},{102,6},{103,7},{104,8... | collective-permute-start | bytes 393224 | tf_op jit(solution)/shard_map/ppermute | solution.py:194
  4.6 1.2 %copy-start.1 = (bf16[16,256,128]{2,1,0:T(8,128)(2,1)S(1)}, bf16[16,256,128]{2,1,0:T(8,128)(2,1)}, u32[]{:S(2)}) copy-start(bf16[16,256,128]{2,1,0:T(8,128)(2,1)} %kernel.1) | copy-start | bytes 3145732
  5.9 1.0 %copy-start.2 = (bf16[16,128,128]{2,1,0:T(8,128)(2,1)S(1)}, bf16[16,128,128]{2,1,0:T(8,128)(2,1)}, u32[]{:S(2)}) copy-start(bf16[16,128,128]{2,1,0:T(8,128)(2,1)} %older.5) | copy-start | bytes 1572868
  8.7 23.9 %copy-start.3 = (bf16[16,128,128]{2,1,0:T(8,128)(2,1)S(1)}, bf16[16,128,128]{2,1,0:T(8,128)(2,1)}, u32[]{:S(2)}) copy-start(bf16[16,128,128]{2,1,0:T(8,128)(2,1)} %older.5) | copy-start | bytes 1572868
  8.7 25.4 %collective-permute-start = (bf16[256,1024]{1,0:T(8,128)(2,1)S(1)}, bf16[256,1024]{1,0:T(8,128)(2,1)S(1)}, u32[]{:S(2)}, u32[]{:S(2)}) collective-permute-start(bf16[256,1024]{1,0:T(8,128)(2,1)S(1)} %get-tuple-element.15), channel_id=1, source_target_pairs={{32,0},{64,32},{96,64},{128,96},{160,128},{192,160},{224,192},{33,... | collective-permute-start | bytes 1572872 | tf_op jit(solution)/shard_map/ppermute | solution.py:175
  11.5 3.3 %collective-permute-start.2 = (bf16[2,2,128,128]{3,2,1,0:T(8,128)(2,1)S(1)}, bf16[2,2,128,128]{3,2,1,0:T(8,128)(2,1)S(1)}, u32[]{:S(2)}, u32[]{:S(2)}) collective-permute-start(bf16[2,2,128,128]{3,2,1,0:T(8,128)(2,1)S(1)} %copy-done), channel_id=1, source_target_pairs={{64,0},{65,1},{66,2},{67,3},{68,4},{69,5},{70,6},{71,7},{72,8},{73... | collective-permute-start | bytes 393224 | tf_op jit(solution)/shard_map/ppermute | solution.py:194
  12.2 16.8 %collective-permute-start.1 = (bf16[2,2,128,128]{3,2,1,0:T(8,128)(2,1)S(1)}, bf16[2,2,128,128]{3,2,1,0:T(8,128)(2,1)S(1)}, u32[]{:S(2)}, u32[]{:S(2)}) collective-permute-start(bf16[2,2,128,128]{3,2,1,0:T(8,128)(2,1)S(1)} %copy-done), channel_id=1, source_target_pairs={{32,0},{33,1},{34,2},{35,3},{36,4},{37,5},{38,6},{39,7},{40,8},{41... | collective-permute-start | bytes 393224 | tf_op jit(solution)/shard_map/ppermute | solution.py:194
  14.1 16.3 %collective-permute-start.7 = (bf16[2,2,128,128]{3,2,1,0:T(8,128)(2,1)S(1)}, bf16[2,2,128,128]{3,2,1,0:T(8,128)(2,1)S(1)}, u32[]{:S(2)}, u32[]{:S(2)}) collective-permute-start(bf16[2,2,128,128]{3,2,1,0:T(8,128)(2,1)S(1)} %copy-done), channel_id=1, source_target_pairs={{224,0},{225,1},{226,2},{227,3},{228,4},{229,5},{230,6},{231,7},{2... | collective-permute-start | bytes 393224 | tf_op jit(solution)/shard_map/ppermute | solution.py:194
  14.8 17.5 %collective-permute-start.6 = (bf16[2,2,128,128]{3,2,1,0:T(8,128)(2,1)S(1)}, bf16[2,2,128,128]{3,2,1,0:T(8,128)(2,1)S(1)}, u32[]{:S(2)}, u32[]{:S(2)}) collective-permute-start(bf16[2,2,128,128]{3,2,1,0:T(8,128)(2,1)S(1)} %copy-done), channel_id=1, source_target_pairs={{192,0},{193,1},{194,2},{195,3},{196,4},{197,5},{198,6},{199,7},{2... | collective-permute-start | bytes 393224 | tf_op jit(solution)/shard_map/ppermute | solution.py:194
  29.0 3.4 %collective-permute-start.5 = (bf16[2,2,128,128]{3,2,1,0:T(8,128)(2,1)S(1)}, bf16[2,2,128,128]{3,2,1,0:T(8,128)(2,1)S(1)}, u32[]{:S(2)}, u32[]{:S(2)}) collective-permute-start(bf16[2,2,128,128]{3,2,1,0:T(8,128)(2,1)S(1)} %copy-done), channel_id=1, source_target_pairs={{160,0},{161,1},{162,2},{163,3},{164,4},{165,5},{166,6},{167,7},{1... | collective-permute-start | bytes 393224 | tf_op jit(solution)/shard_map/ppermute | solution.py:194
  29.6 2.7 %collective-permute-start.4 = (bf16[2,2,128,128]{3,2,1,0:T(8,128)(2,1)S(1)}, bf16[2,2,128,128]{3,2,1,0:T(8,128)(2,1)S(1)}, u32[]{:S(2)}, u32[]{:S(2)}) collective-permute-start(bf16[2,2,128,128]{3,2,1,0:T(8,128)(2,1)S(1)} %copy-done), channel_id=1, source_target_pairs={{128,0},{129,1},{130,2},{131,3},{132,4},{133,5},{134,6},{135,7},{1... | collective-permute-start | bytes 393224 | tf_op jit(solution)/shard_map/ppermute | solution.py:194
  30.4 11.1 %collective-permute-start.9 = (bf16[8,128,128]{2,1,0:T(8,128)(2,1)S(1)}, bf16[8,128,128]{2,1,0:T(8,128)(2,1)S(1)}, u32[]{:S(2)}, u32[]{:S(2)}) collective-permute-start(bf16[8,128,128]{2,1,0:T(8,128)(2,1)S(1)} %head_part.1), channel_id=1, source_target_pairs={{0,32},{32,64},{64,96},{96,128},{128,160},{160,192},{192,224},{1,3... | collective-permute-start | bytes 786440 | tf_op jit(solution)/shard_map/ppermute | solution.py:175
  34.0 10.2 %collective-permute-start.11 = (bf16[16,16,8,128]{3,2,1,0:T(8,128)(2,1)S(1)}, bf16[16,16,8,128]{3,2,1,0:T(8,128)(2,1)S(1)}, u32[]{:S(2)}, u32[]{:S(2)}) collective-permute-start(bf16[16,16,8,128]{3,2,1,0:T(8,128)(2,1)S(1)} %get-tuple-element.22), channel_id=1, source_target_pairs={{0,1},{1,0},{2,3},{3,2},{4,5},{5,4},{6,7},{7,6},{8,9},{9,8},{10,11... | collective-permute-start | bytes 1572872 | tf_op jit(solution)/shard_map/ppermute | solution.py:170
  44.1 2.0 %collective-permute-start.10 = (bf16[16,16,8,128]{3,2,1,0:T(8,128)(2,1)S(1)}, bf16[16,16,8,128]{3,2,1,0:T(8,128)(2,1)S(1)}, u32[]{:S(2)}, u32[]{:S(2)}) collective-permute-start(bf16[16,16,8,128]{3,2,1,0:T(8,128)(2,1)S(1)} %get-tuple-element.19), channel_id=1, source_target_pairs={{0,1},{1,0},{2,3},{3,2},{4,5},{5,4},{6,7},{7,6},{8,9},{9,8},{10,11... | collective-permute-start | bytes 1572872 | tf_op jit(solution)/shard_map/ppermute | solution.py:170

commit v5 on v4

v5 whole, which is shorter than its diff:
```python
import functools

import jax
import jax.numpy as jnp
from jax import lax
from jax.experimental import pallas as pl
from jax.experimental.pallas import tpu as pltpu
from jax.sharding import Mesh
from jax.sharding import PartitionSpec as P

SOURCES = (1, 2, 3, 5, 6, 7)
PAR = ("x", "y", "c")
EVERY = ("z", "x", "y", "c")
VMEM = pl.BlockSpec(memory_space=pltpu.VMEM)
LIMIT = pltpu.CompilerParams(vmem_limit_bytes=8 * 1024 * 1024)


def work(flops, nbytes):
    return pl.CostEstimate(flops=flops, bytes_accessed=nbytes, transcendentals=0)


def order_rows(kernel, ordered):
    lags, sensors, params = kernel.shape
    planes = 8
    half = sensors // 2
    row = lax.broadcasted_iota(jnp.int32, (sensors, sensors), 0)
    col = lax.broadcasted_iota(jnp.int32, (sensors, sensors), 1)
    other = (row >= half).astype(jnp.int32)
    place = row - half * other
    core = lax.axis_index("c")
    parity = core + other - 2 * core * other
    sensor = (place % planes) * (sensors // planes) + (place // planes) * 2 + parity
    select = (col == sensor).astype(jnp.bfloat16)
    for lag in range(lags):
        rows = jnp.dot(select, kernel[lag], preferred_element_type=jnp.float32)
        ordered[:, lag * params : (lag + 1) * params] = rows.astype(jnp.bfloat16)


def first_part(kernel, ordered, leading):
    order_rows(kernel, ordered)
    leading[...] = ordered[:, : leading.shape[1]]


def windows(value, low, high, params, fields, times):
    for time in range(low, high + 2):
        if time <= high:
            times[(high - time) * params : (high - time + 1) * params, :fields] = value(time)
        if time > low:
            at = high + 1 - time
            times[at * params : (at + 1) * params, fields:] = value(time)


def after(first, then):
    block = first.shape[0]
    return lambda time: first[time] if time < block else then[time - block]


def product(left, right, start):
    window = right[start : start + left.shape[1]]
    return jnp.dot(left, window, preferred_element_type=jnp.float32)


def put_half(sums, pair, half):
    fields = sums.shape[1] // 2
    sums = sums.astype(jnp.bfloat16)
    for odd in range(2):
        part = sums[:, odd * fields : (odd + 1) * fields]
        half[:, 2 * pair + odd] = part.reshape(half.shape[0], half.shape[2], fields)


def put(sums, pair, mine, theirs):
    count = sums.shape[0] // 2
    put_half(sums[:count], pair, mine)
    put_half(sums[count:], pair, theirs)


def second_part(
    side, ordered, following, older, newer, head, last, half, ahead, behind, arrivals
):
    block, params, fields = older.shape
    lags = following.shape[1] // params
    plane = lax.axis_index("z")
    count = ordered.shape[0] // 2
    rows = slice(side * count, (side + 1) * count)
    windows(after(older, newer), block + 1 - lags, 2 * block - 2, params, fields, ahead)

    def conv(left, right, pair):
        return product(left, right, (block - 2 - 2 * pair) * params)

    @pl.when(plane != 0)
    def _():
        windows(after(newer, head), 1, 2 * block - 2 - lags, params, fields, behind)
        for pair in range(block // 2):
            sums = conv(following[rows], ahead, pair)
            sums = sums + conv(ordered[rows, lags * params :], behind, pair)
            put_half(sums, pair, half)

    @pl.when(plane == 0)
    def _():
        windows(after(newer, last), 1, 2 * block - 2, params, fields, arrivals)
        for pair in range(block // 2):
            sums = conv(following[rows], ahead, pair) + conv(ordered[rows], arrivals, pair)
            put_half(sums, pair, half)


def step_zero(ordered, older, newer, mine, theirs, times):
    block, params, fields = newer.shape
    windows(after(older, newer), 1, 2 * block - 2, params, fields, times)
    for pair in range(block // 2):
        start = (block - 2 - 2 * pair) * params
        put(product(ordered[...], times, start), pair, mine, theirs)


def row_of(pieces, step, time):
    own, first, second, third, fifth, sixth, seventh = pieces
    source, row = divmod(time, own.shape[1])
    if source == 4:
        return third[own.shape[0] + step, row]
    return (own, first, second, third, None, fifth, sixth, seventh)[source][step, row]


def joined(own, other, both):
    both[: own.shape[0]] = own[...]
    both[own.shape[0] :] = other[...]


def head_part(*refs):
    *near, received, head = refs
    here = lax.axis_index("z") == 0
    for time in range(head.shape[0]):
        row = row_of((*near, None, None, None), 0, time)
        head[time] = jnp.where(here, row, received[time])


def newer_part(*refs):
    *pieces, received, newer, last = refs
    here = lax.axis_index("z") == 0
    for time in range(newer.shape[0]):
        newer[time] = jnp.where(here, row_of(pieces, 0, time), received[time])
        last[time] = row_of(pieces, 1, time)


def pair_part(step, mine, received, *refs):
    paired = refs[-1]
    block = mine.shape[1]
    for chip in range(mine.shape[0]):
        both = mine[chip].astype(jnp.float32) + received[chip].astype(jnp.float32)
        paired[chip, step * block : (step + 1) * block] = both.astype(jnp.bfloat16)


def plane_part(arrived, summed):
    for time in range(arrived.shape[1]):
        total = arrived[0, time].astype(jnp.float32)
        for chip in range(1, arrived.shape[0]):
            total = total + arrived[chip, time].astype(jnp.float32)
        summed[time] = total.astype(jnp.bfloat16)


def ring(array, axis, by):
    size = lax.axis_size(axis)
    return lax.ppermute(array, axis, [(i, (i + by) % size) for i in range(size)])


def onward(array, axis, by):
    size = lax.axis_size(axis)
    return lax.ppermute(array, axis, [(i, i + by) for i in range(size) if 0 <= i + by < size])


def exchange(parts, axis):
    return lax.all_to_all(parts, axis, split_axis=0, concat_axis=0, tiled=True)


def observed(kernel, history, arrivals):
    block, sensors, params = kernel.shape
    steps, _, _, fields = arrivals.shape
    planes = lax.axis_size("z")
    chips = lax.axis_size("x") * lax.axis_size("y")
    part = jax.ShapeDtypeStruct((chips, block, planes, fields), jnp.bfloat16)

    shifted = onward(history, "z", 1)
    relayed = lax.ppermute(arrivals, "z", [(4, 3)])
    both = pl.pallas_call(
        joined,
        out_shape=jax.ShapeDtypeStruct((2 * steps, *arrivals.shape[1:]), jnp.bfloat16),
        in_specs=[VMEM] * 2,
        out_specs=VMEM,
        compiler_params=LIMIT,
        name="joined",
    )(arrivals, relayed)
    pieces = [arrivals]
    for source in SOURCES:
        operand = both if source == 3 else arrivals
        pieces.append(lax.ppermute(operand, "z", [(source, 0)]))

    ordered, leading = pl.pallas_call(
        first_part,
        out_shape=(
            jax.ShapeDtypeStruct((sensors, block * params), jnp.bfloat16),
            jax.ShapeDtypeStruct((sensors, block // 2 * params), jnp.bfloat16),
        ),
        in_specs=[VMEM],
        out_specs=(VMEM, VMEM),
        compiler_params=LIMIT,
        cost_estimate=work(2 * 10**9, 4 * 10**6),
        name="first_part",
    )(kernel)

    following = onward(leading, "z", -1)

    def pair(step, mine, theirs, *paired):
        received = ring(theirs, "c", 1)
        return pl.pallas_call(
            functools.partial(pair_part, step),
            out_shape=jax.ShapeDtypeStruct((chips, steps * block, planes, fields), jnp.bfloat16),
            in_specs=[VMEM] * (2 + len(paired)),
            out_specs=VMEM,
            input_output_aliases={2: 0} if paired else {},
            compiler_params=LIMIT,
            name="pair_part",
        )(mine, received, *paired)

    near = planes // 2
    head = pl.pallas_call(
        head_part,
        out_shape=jax.ShapeDtypeStruct((block // 2, params, fields), jnp.bfloat16),
        in_specs=[VMEM] * (near + 1),
        out_specs=VMEM,
        compiler_params=LIMIT,
        name="head_part",
    )(*pieces[:near], shifted)
    head_twice = onward(head, "z", 1)
    newer, last = pl.pallas_call(
        newer_part,
        out_shape=(jax.ShapeDtypeStruct(shifted.shape, jnp.bfloat16),) * 2,
        in_specs=[VMEM] * planes,
        out_specs=(VMEM, VMEM),
        compiler_params=LIMIT,
        name="newer_part",
    )(*pieces, shifted)
    mine, theirs = pl.pallas_call(
        step_zero,
        out_shape=(part, part),
        in_specs=[VMEM] * 3,
        out_specs=(VMEM, VMEM),
        scratch_shapes=[pltpu.VMEM(((2 * block - 2) * params, 2 * fields), jnp.bfloat16)],
        compiler_params=LIMIT,
        cost_estimate=work(2 * 10**9, 6 * 10**6),
        name="step_zero",
    )(ordered, history, newer)
    paired = pair(0, mine, theirs)
    width = 2 * fields

    def second(side):
        return pl.pallas_call(
            functools.partial(second_part, side),
            out_shape=part,
            in_specs=[VMEM] * 6,
            out_specs=VMEM,
            scratch_shapes=[
                pltpu.VMEM(((3 * block // 2 - 2) * params, width), jnp.bfloat16),
                pltpu.VMEM(((3 * block // 2 - 2) * params, width), jnp.bfloat16),
                pltpu.VMEM(((2 * block - 2) * params, width), jnp.bfloat16),
            ],
            compiler_params=pltpu.CompilerParams(vmem_limit_bytes=12 * 1024 * 1024),
            cost_estimate=work(2 * 10**9, 8 * 10**6),
            name="second_part",
        )(ordered, following, history, newer, head_twice, last)

    theirs = second(1)
    mine = second(0)
    paired = pair(1, mine, theirs, paired)
    arrived = exchange(paired, ("x", "y"))
    summed = pl.pallas_call(
        plane_part,
        out_shape=jax.ShapeDtypeStruct((steps * block, planes, fields), jnp.bfloat16),
        in_specs=[VMEM],
        out_specs=VMEM,
        compiler_params=LIMIT,
        name="plane_part",
    )(arrived)
    across = exchange(jnp.moveaxis(summed, 1, 0), "z")
    across = across.astype(jnp.float32).sum(axis=0).astype(jnp.bfloat16)
    return across.reshape(steps, block, 1, fields)


def solution(mesh):
    split = Mesh(mesh.devices.reshape(mesh.shape["tm"], 4, 4, 2), EVERY)
    placed = (P("z", None, PAR), P("z", PAR, None), P(None, "z", PAR, None))
    return jax.shard_map(
        observed,
        mesh=split,
        in_specs=placed,
        out_specs=P(None, None, EVERY, None),
        check_vma=False,
    )
```

time: 89.9 us -> 91.1 us (1.013)
  waiting for transfers between devices: 22.7 us -> 25.2 us
  blocking collectives: 42.1 us -> 40.6 us
    ppermute x7, waiting for transfers between devices: 13.5 us -> 18.8 us  [the longest x6 18.8 us: observed(): pieces.append(lax.ppermute(operand, 'z', [(source, 0)]))]
    all_to_all x2, blocking collectives: 42.1 us -> 40.6 us  [exchange(): return lax.all_to_all(parts, axis, split_axis=0, concat_axis=0, tiled=True)]
    ppermute x2, waiting for transfers between devices: 1.76 us -> 0.26 us  [ring(): lax.ppermute(array, axis, [(i, (i + by) % size) for i in range(size)])]
    pallas_call x2 -> x4, Pallas kernels: 3.98 us -> 5.37 us  [the longest x2 2.98 us: second(): pl.pallas_call(functools.partial(second_part, side), out_shape=part, in_s...]
    ppermute x3, waiting for transfers between devices: 7.46 us -> 6.11 us  [onward(): lax.ppermute(array, axis, [(i, i + by) for i in range(size) if 0 <= i + b...]
    pallas_call x1, Pallas kernels: 1.77 us -> 0.82 us  [observed(): pl.pallas_call(first_part, out_shape=(jax.ShapeDtypeStruct((sensors, bloc...]
where the time goes in v5:
time: 91.1 us; the launch traced here: 90.4 us
  blocking collectives  40.6 us (45%)
  waiting for transfers between devices  25.2 us (28%)
  starting transfers between devices  14.8 us (16%)
  Pallas kernels  6.82 us (7%)
  local copies, waits for them, and re-layouts  2.14 us (2%)
    all_to_all x2, blocking collectives, exchange(): return lax.all_to_all(parts, axis, split_axis=0, concat_axis=0, tiled=True)  40.6 us
    ppermute x6, waiting for transfers between devices, observed(): pieces.append(lax.ppermute(operand, 'z', [(source, 0)]))  18.8 us
    ppermute x3, starting transfers between devices, onward(): lax.ppermute(array, axis, [(i, i + by) for i in range(size) if 0 <= i + b...  8.54 us
    ppermute x3, waiting for transfers between devices, onward(): lax.ppermute(array, axis, [(i, i + by) for i in range(size) if 0 <= i + b...  6.11 us
    ppermute x6, starting transfers between devices, observed(): pieces.append(lax.ppermute(operand, 'z', [(source, 0)]))  5.39 us
    pallas_call x2, Pallas kernels, second(): pl.pallas_call(functools.partial(second_part, side), out_shape=part, in_s...  2.98 us
    pallas_call x1, Pallas kernels, observed(): pl.pallas_call(step_zero, out_shape=(part, part), in_specs=[VMEM] * 3, ou...  2.37 us
    unnamed x8, local copies, waits for them, and re-layouts  2.13 us
  transfers between devices with their start and end apart: 12, of which 3 were waited for; matrix products, arithmetic and copies ran while one was open for 0% of the time, Pallas kernels for 7%

profile of v5, /device:TPU:32, one launch (start us, length us, event | category | flops | bytes accessed | tf_op | source)
XLA Modules:
  0.0 90.4 jit_solution(3500777010009812955)
XLA Ops:
  0.0 0.7 collective-permute-start.3
  0.7 3.8 %collective-permute-start.8 = (bf16[16,128,128]{2,1,0:T(8,128)(2,1)}, bf16[16,128,128]{2,1,0:T(8,128)(2,1)S(1)}, u32[]{:S(2)}, u32[]{:S(2)}) collective-permute-start(bf16[16,128,128]{2,1,0:T(8,128)(2,1)} %older.5), channel_id=1, source_target_pairs={{0,32},{32,64},{64,96},{96,128},{128,160},{160,192},{192,224},{1,3... | collective-permute-start | bytes 1572872 | tf_op jit(solution)/shard_map/ppermute | solution.py:166
  4.5 0.0 collective-permute-done.3.other
  4.5 0.0 copy-start
  4.5 0.9 copy-done
  5.4 0.0 copy-start.1
  5.5 0.8 collective-permute-start.4
  6.3 0.0 copy-start.2
  6.3 1.2 %copy-done.2 = bf16[16,256,128]{2,1,0:T(8,128)(2,1)S(1)} copy-done((bf16[16,256,128]{2,1,0:T(8,128)(2,1)S(1)}, bf16[16,256,128]{2,1,0:T(8,128)(2,1)}, u32[]{:S(2)}) %copy-start.2) | copy-done | bytes 1048600
  7.5 0.8 first_part.1
  8.3 2.7 %collective-permute-start = (bf16[256,1024]{1,0:T(8,128)(2,1)S(1)}, bf16[256,1024]{1,0:T(8,128)(2,1)S(1)}, u32[]{:S(2)}, u32[]{:S(2)}) collective-permute-start(bf16[256,1024]{1,0:T(8,128)(2,1)S(1)} %get-tuple-element.12), channel_id=1, source_target_pairs={{32,0},{64,32},{96,64},{128,96},{160,128},{192,160},{224,192},{33,... | collective-permute-start | bytes 1572872 | tf_op jit(solution)/shard_map/ppermute | solution.py:166
  11.0 0.0 copy-done.1
  11.0 0.7 collective-permute-start.2
  11.7 1.9 %collective-permute-start.1 = (bf16[2,2,128,128]{3,2,1,0:T(8,128)(2,1)S(1)}, bf16[2,2,128,128]{3,2,1,0:T(8,128)(2,1)S(1)}, u32[]{:S(2)}, u32[]{:S(2)}) collective-permute-start(bf16[2,2,128,128]{3,2,1,0:T(8,128)(2,1)S(1)} %copy-done.1), channel_id=1, source_target_pairs={{32,0},{33,1},{34,2},{35,3},{36,4},{37,5},{38,6},{39,7},{40,8},{41... | collective-permute-start | bytes 393224 | tf_op jit(solution)/shard_map/ppermute | solution.py:193
  13.6 0.0 collective-permute-done.2.refs_2_
  13.6 0.7 collective-permute-start.7
  14.3 18.8 %collective-permute-done.1.refs_1_ = bf16[2,2,128,128]{3,2,1,0:T(8,128)(2,1)S(1)} collective-permute-done((bf16[2,2,128,128]{3,2,1,0:T(8,128)(2,1)S(1)}, bf16[2,2,128,128]{3,2,1,0:T(8,128)(2,1)S(1)}, u32[]{:S(2)}, u32[]{:S(2)}) %collective-permute-start.1) | collective-permute-done | bytes 131104 | tf_op jit(solution)/shard_map/ppermute | solution.py:193
  33.1 0.7 collective-permute-start.6
  33.8 0.0 collective-permute-done.4.refs_3_
  33.8 0.7 collective-permute-start.5
  34.5 0.0 collective-permute-done.8.refs_7_.refs_4_
  34.5 0.1 head_part.1
  34.6 0.0 copy-start.3
  34.6 2.1 %collective-permute-start.9 = (bf16[8,128,128]{2,1,0:T(8,128)(2,1)S(1)}, bf16[8,128,128]{2,1,0:T(8,128)(2,1)S(1)}, u32[]{:S(2)}, u32[]{:S(2)}) collective-permute-start(bf16[8,128,128]{2,1,0:T(8,128)(2,1)S(1)} %head_part.1), channel_id=1, source_target_pairs={{0,32},{32,64},{64,96},{96,128},{128,160},{160,192},{192,224},{1,3... | collective-permute-start | bytes 786440 | tf_op jit(solution)/shard_map/ppermute | solution.py:166
  36.6 0.0 collective-permute-done.7.refs_6_
  36.6 0.0 collective-permute-done.6.refs_5_
  36.6 0.0 collective-permute-done.5.refs_4_
  36.7 0.2 newer_part.1
  36.8 0.0 copy-done.3
  36.8 2.4 %step_zero.1 = (bf16[16,16,8,128]{3,2,1,0:T(8,128)(2,1)S(1)}, bf16[16,16,8,128]{3,2,1,0:T(8,128)(2,1)S(1)}) custom-call(bf16[256,2048]{1,0:T(8,128)(2,1)S(1)} %get-tuple-element.11.ordered, bf16[16,128,128]{2,1,0:T(8,128)(2,1)S(1)} %copy-done.3, bf16[16,128,128]{2,1,0:T(8,128)(2,1)S(1)} %get-tuple-element.13.newer), custom_call_target="tpu_custom_call" | custom-call | flops 2000000000 | bytes 6000000 | tf_op jit(solution)/shard_map/step_zero/pallas_call | solution.py:240
  39.2 0.1 collective-permute-start.11
  39.3 0.0 collective-permute-done.following
  39.3 6.1 %collective-permute-done.9.head = bf16[8,128,128]{2,1,0:T(8,128)(2,1)S(1)} collective-permute-done((bf16[8,128,128]{2,1,0:T(8,128)(2,1)S(1)}, bf16[8,128,128]{2,1,0:T(8,128)(2,1)S(1)}, u32[]{:S(2)}, u32[]{:S(2)}) %collective-permute-start.9) | collective-permute-done | bytes 262176 | tf_op jit(solution)/shard_map/ppermute | solution.py:166
  45.4 1.5 %second_part.3 = bf16[16,16,8,128]{3,2,1,0:T(8,128)(2,1)S(1)} custom-call(bf16[256,2048]{1,0:T(8,128)(2,1)S(1)} %get-tuple-element.11.ordered, bf16[256,1024]{1,0:T(8,128)(2,1)S(1)} %collective-permute-done.following, bf16[16,128,128]{2,1,0:T(8,128)(2,1)S(1)} %copy-done.3, bf16[16,128,128]{2,1,0:T(8,128)(2,1)S(1)} %get-tuple-element.13.newer, ...), custom_call_target="tpu_custom_call" | custom-call | flops 2000000000 | bytes 8000000 | tf_op jit(solution)/shard_map/second_part/pallas_call | solution.py:254
  46.9 0.1 collective-permute-start.10
  47.0 1.5 %second_part.2.mine = bf16[16,16,8,128]{3,2,1,0:T(8,128)(2,1)S(1)} custom-call(bf16[256,2048]{1,0:T(8,128)(2,1)S(1)} %get-tuple-element.11.ordered, bf16[256,1024]{1,0:T(8,128)(2,1)S(1)} %collective-permute-done.following, bf16[16,128,128]{2,1,0:T(8,128)(2,1)S(1)} %copy-done.3, bf16[16,128,128]{2,1,0:T(8,128)(2,1)S(1)} %get-tuple-element.13.newer, ...), custom_call_target="tpu_custom_call" | custom-call | flops 2000000000 | bytes 8000000 | tf_op jit(solution)/shard_map/second_part/pallas_call | solution.py:254
  48.5 0.0 collective-permute-done.11.received
  48.5 0.1 pair_part.2.refs_0_
  48.7 0.3 collective-permute-done.10.received
  48.9 0.1 pair_part.3
  49.1 24.4 %all_to_all.10.arrived = bf16[16,32,8,128]{3,2,1,0:T(8,128)(2,1)S(1)} all-to-all(bf16[16,32,8,128]{3,2,1,0:T(8,128)(2,1)S(1)} %pair_part.3), channel_id=1, replica_groups=mesh['z'=8,'x'=4,'y'=4,'c'=2] {'x','y'}, dimensions={0} | all-to-all | bytes 2097152 | tf_op jit(solution)/shard_map/all_to_all | solution.py:170
  73.4 0.1 plane_part.1
  73.6 16.2 %all_to_all.11 = bf16[8,32,128]{2,1,0:T(8,128)(2,1)S(1)} all-to-all(bf16[8,32,128]{2,1,0:T(8,128)(2,1)S(1)} %copy.5), channel_id=1, replica_groups=mesh['z'=8,'x'=4,'y'=4,'c'=2] {'z'}, dimensions={0} | all-to-all | bytes 131072 | tf_op jit(solution)/shard_map/all_to_all | solution.py:170
  89.8 0.6 reduce_sum.12
  (2 shorter events, 0.0 us)
Async XLA Ops:
  0.0 4.5 %collective-permute-start.3 = (bf16[2,2,128,128]{3,2,1,0:T(8,128)(2,1)}, bf16[2,2,128,128]{3,2,1,0:T(8,128)(2,1)S(1)}, u32[]{:S(2)}, u32[]{:S(2)}) collective-permute-start(bf16[2,2,128,128]{3,2,1,0:T(8,128)(2,1)} %refs_0_.3), channel_id=1, source_target_pairs={{128,96},{129,97},{130,98},{131,99},{132,100},{133,101},{134,102},... | collective-permute-start | bytes 393224 | tf_op jit(solution)/shard_map/ppermute | solution.py:181
  0.7 33.8 %collective-permute-start.8 = (bf16[16,128,128]{2,1,0:T(8,128)(2,1)}, bf16[16,128,128]{2,1,0:T(8,128)(2,1)S(1)}, u32[]{:S(2)}, u32[]{:S(2)}) collective-permute-start(bf16[16,128,128]{2,1,0:T(8,128)(2,1)} %older.5), channel_id=1, source_target_pairs={{0,32},{32,64},{64,96},{96,128},{128,160},{160,192},{192,224},{1,3... | collective-permute-start | bytes 1572872 | tf_op jit(solution)/shard_map/ppermute | solution.py:166
  4.5 0.9 %copy-start = (bf16[2,2,128,128]{3,2,1,0:T(8,128)(2,1)S(1)}, bf16[2,2,128,128]{3,2,1,0:T(8,128)(2,1)}, u32[]{:S(2)}) copy-start(bf16[2,2,128,128]{3,2,1,0:T(8,128)(2,1)} %refs_0_.3) | copy-start | bytes 393220
  5.4 5.6 %copy-start.1 = (bf16[2,2,128,128]{3,2,1,0:T(8,128)(2,1)S(1)}, bf16[2,2,128,128]{3,2,1,0:T(8,128)(2,1)}, u32[]{:S(2)}) copy-start(bf16[2,2,128,128]{3,2,1,0:T(8,128)(2,1)} %refs_0_.3) | copy-start | bytes 393220
  5.5 28.3 %collective-permute-start.4 = (bf16[4,2,128,128]{3,2,1,0:T(8,128)(2,1)S(1)}, bf16[4,2,128,128]{3,2,1,0:T(8,128)(2,1)S(1)}, u32[]{:S(2)}, u32[]{:S(2)}) collective-permute-start(bf16[4,2,128,128]{3,2,1,0:T(8,128)(2,1)S(1)} %joined.1), channel_id=1, source_target_pairs={{96,0},{97,1},{98,2},{99,3},{100,4},{101,5},{102,6},{103,7},{104,8... | collective-permute-start | bytes 786440 | tf_op jit(solution)/shard_map/ppermute | solution.py:193
  6.3 1.2 %copy-start.2 = (bf16[16,256,128]{2,1,0:T(8,128)(2,1)S(1)}, bf16[16,256,128]{2,1,0:T(8,128)(2,1)}, u32[]{:S(2)}) copy-start(bf16[16,256,128]{2,1,0:T(8,128)(2,1)} %kernel.1) | copy-start | bytes 3145732
  8.3 31.0 %collective-permute-start = (bf16[256,1024]{1,0:T(8,128)(2,1)S(1)}, bf16[256,1024]{1,0:T(8,128)(2,1)S(1)}, u32[]{:S(2)}, u32[]{:S(2)}) collective-permute-start(bf16[256,1024]{1,0:T(8,128)(2,1)S(1)} %get-tuple-element.12), channel_id=1, source_target_pairs={{32,0},{64,32},{96,64},{128,96},{160,128},{192,160},{224,192},{33,... | collective-permute-start | bytes 1572872 | tf_op jit(solution)/shard_map/ppermute | solution.py:166
  11.0 2.6 %collective-permute-start.2 = (bf16[2,2,128,128]{3,2,1,0:T(8,128)(2,1)S(1)}, bf16[2,2,128,128]{3,2,1,0:T(8,128)(2,1)S(1)}, u32[]{:S(2)}, u32[]{:S(2)}) collective-permute-start(bf16[2,2,128,128]{3,2,1,0:T(8,128)(2,1)S(1)} %copy-done.1), channel_id=1, source_target_pairs={{64,0},{65,1},{66,2},{67,3},{68,4},{69,5},{70,6},{71,7},{72,8},{73... | collective-permute-start | bytes 393224 | tf_op jit(solution)/shard_map/ppermute | solution.py:193
  11.7 21.4 %collective-permute-start.1 = (bf16[2,2,128,128]{3,2,1,0:T(8,128)(2,1)S(1)}, bf16[2,2,128,128]{3,2,1,0:T(8,128)(2,1)S(1)}, u32[]{:S(2)}, u32[]{:S(2)}) collective-permute-start(bf16[2,2,128,128]{3,2,1,0:T(8,128)(2,1)S(1)} %copy-done.1), channel_id=1, source_target_pairs={{32,0},{33,1},{34,2},{35,3},{36,4},{37,5},{38,6},{39,7},{40,8},{41... | collective-permute-start | bytes 393224 | tf_op jit(solution)/shard_map/ppermute | solution.py:193
  13.6 23.0 %collective-permute-start.7 = (bf16[2,2,128,128]{3,2,1,0:T(8,128)(2,1)S(1)}, bf16[2,2,128,128]{3,2,1,0:T(8,128)(2,1)S(1)}, u32[]{:S(2)}, u32[]{:S(2)}) collective-permute-start(bf16[2,2,128,128]{3,2,1,0:T(8,128)(2,1)S(1)} %copy-done.1), channel_id=1, source_target_pairs={{224,0},{225,1},{226,2},{227,3},{228,4},{229,5},{230,6},{231,7},{2... | collective-permute-start | bytes 393224 | tf_op jit(solution)/shard_map/ppermute | solution.py:193
  33.1 3.5 %collective-permute-start.6 = (bf16[2,2,128,128]{3,2,1,0:T(8,128)(2,1)S(1)}, bf16[2,2,128,128]{3,2,1,0:T(8,128)(2,1)S(1)}, u32[]{:S(2)}, u32[]{:S(2)}) collective-permute-start(bf16[2,2,128,128]{3,2,1,0:T(8,128)(2,1)S(1)} %copy-done.1), channel_id=1, source_target_pairs={{192,0},{193,1},{194,2},{195,3},{196,4},{197,5},{198,6},{199,7},{2... | collective-permute-start | bytes 393224 | tf_op jit(solution)/shard_map/ppermute | solution.py:193
  33.8 2.9 %collective-permute-start.5 = (bf16[2,2,128,128]{3,2,1,0:T(8,128)(2,1)S(1)}, bf16[2,2,128,128]{3,2,1,0:T(8,128)(2,1)S(1)}, u32[]{:S(2)}, u32[]{:S(2)}) collective-permute-start(bf16[2,2,128,128]{3,2,1,0:T(8,128)(2,1)S(1)} %copy-done.1), channel_id=1, source_target_pairs={{160,0},{161,1},{162,2},{163,3},{164,4},{165,5},{166,6},{167,7},{1... | collective-permute-start | bytes 393224 | tf_op jit(solution)/shard_map/ppermute | solution.py:193
  34.6 2.3 %copy-start.3 = (bf16[16,128,128]{2,1,0:T(8,128)(2,1)S(1)}, bf16[16,128,128]{2,1,0:T(8,128)(2,1)}, u32[]{:S(2)}) copy-start(bf16[16,128,128]{2,1,0:T(8,128)(2,1)} %older.5) | copy-start | bytes 1572868
  34.6 10.9 %collective-permute-start.9 = (bf16[8,128,128]{2,1,0:T(8,128)(2,1)S(1)}, bf16[8,128,128]{2,1,0:T(8,128)(2,1)S(1)}, u32[]{:S(2)}, u32[]{:S(2)}) collective-permute-start(bf16[8,128,128]{2,1,0:T(8,128)(2,1)S(1)} %head_part.1), channel_id=1, source_target_pairs={{0,32},{32,64},{64,96},{96,128},{128,160},{160,192},{192,224},{1,3... | collective-permute-start | bytes 786440 | tf_op jit(solution)/shard_map/ppermute | solution.py:166
  39.2 9.3 %collective-permute-start.11 = (bf16[16,16,8,128]{3,2,1,0:T(8,128)(2,1)S(1)}, bf16[16,16,8,128]{3,2,1,0:T(8,128)(2,1)S(1)}, u32[]{:S(2)}, u32[]{:S(2)}) collective-permute-start(bf16[16,16,8,128]{3,2,1,0:T(8,128)(2,1)S(1)} %get-tuple-element.16), channel_id=1, source_target_pairs={{0,1},{1,0},{2,3},{3,2},{4,5},{5,4},{6,7},{7,6},{8,9},{9,8},{10,11... | collective-permute-start | bytes 1572872 | tf_op jit(solution)/shard_map/ppermute | solution.py:161
  46.9 2.0 %collective-permute-start.10 = (bf16[16,16,8,128]{3,2,1,0:T(8,128)(2,1)S(1)}, bf16[16,16,8,128]{3,2,1,0:T(8,128)(2,1)S(1)}, u32[]{:S(2)}, u32[]{:S(2)}) collective-permute-start(bf16[16,16,8,128]{3,2,1,0:T(8,128)(2,1)S(1)} %second_part.3), channel_id=1, source_target_pairs={{0,1},{1,0},{2,3},{3,2},{4,5},{5,4},{6,7},{7,6},{8,9},{9,8},{10,11... | collective-permute-start | bytes 1572872 | tf_op jit(solution)/shard_map/ppermute | solution.py:161

commit v6 on v4

--- a/solution.py
+++ b/solution.py
@@ -9,6 +9,7 @@
 from jax.sharding import PartitionSpec as P
 
 ORDER = (5, 6, 7, 4, 3, 2, 1)
+LEADING = 9
 PAR = ("x", "y", "c")
 EVERY = ("z", "x", "y", "c")
 VMEM = pl.BlockSpec(memory_space=pltpu.VMEM)
@@ -67,48 +68,57 @@
             times[at * params : (at + 1) * params, fields:] = value(time)
 
 
-def put(sums, pair, mine, theirs):
-    half = sums.shape[0] // 2
+def after(first, then):
+    block = first.shape[0]
+    return lambda time: first[time] if time < block else then[time - block]
+
+
+def product(left, right, start):
+    window = right[start : start + left.shape[1]]
+    return jnp.dot(left, window, preferred_element_type=jnp.float32)
+
+
+def put_half(sums, pair, half):
     fields = sums.shape[1] // 2
     sums = sums.astype(jnp.bfloat16)
     for odd in range(2):
         part = sums[:, odd * fields : (odd + 1) * fields]
-        mine[:, 2 * pair + odd] = part[:half].reshape(mine.shape[0], mine.shape[2], fields)
-        theirs[:, 2 * pair + odd] = part[half:].reshape(mine.shape[0], mine.shape[2], fields)
+        half[:, 2 * pair + odd] = part.reshape(half.shape[0], half.shape[2], fields)
+
+
+def put(sums, pair, mine, theirs):
+    count = sums.shape[0] // 2
+    put_half(sums[:count], pair, mine)
+    put_half(sums[count:], pair, theirs)
 
 
 def second_part(
-    ordered, following, older, newer, head, last, mine, theirs, ahead, behind, arrivals
+    side, ordered, following, older, newer, head, last, half, ahead, behind, arrivals
 ):
     block, params, fields = older.shape
     lags = following.shape[1] // params
     plane = lax.axis_index("z")
-
-    def after(first, then):
-        return lambda time: first[time] if time < block else then[time - block]
-
-    windows(after(older, newer), lags + 1, 2 * block - 2, params, fields, ahead)
+    count = ordered.shape[0] // 2
+    rows = slice(side * count, (side + 1) * count)
+    windows(after(older, newer), block + 1 - lags, 2 * block - 2, params, fields, ahead)
 
     def conv(left, right, pair):
-        start = (block - 2 - 2 * pair) * params
-        return jnp.dot(
-            left, right[start : start + left.shape[1]], preferred_element_type=jnp.float32
-        )
+        return product(left, right, (block - 2 - 2 * pair) * params)
 
     @pl.when(plane != 0)
     def _():
         windows(after(newer, head), 1, 2 * block - 2 - lags, params, fields, behind)
         for pair in range(block // 2):
-            sums = conv(following[...], ahead, pair)
-            sums = sums + conv(ordered[:, lags * params :], behind, pair)
-            put(sums, pair, mine, theirs)
+            sums = conv(following[rows], ahead, pair)
+            sums = sums + conv(ordered[rows, lags * params :], behind, pair)
+            put_half(sums, pair, half)
 
     @pl.when(plane == 0)
     def _():
         windows(after(newer, last), 1, 2 * block - 2, params, fields, arrivals)
         for pair in range(block // 2):
-            sums = conv(following[...], ahead, pair) + conv(ordered[...], arrivals, pair)
-            put(sums, pair, mine, theirs)
+            sums = conv(following[rows], ahead, pair) + conv(ordered[rows], arrivals, pair)
+            put_half(sums, pair, half)
 
 
 def lower_part(ordered, older, newer, upper, mine, theirs, times):
@@ -197,7 +207,7 @@
         first_part,
         out_shape=(
             jax.ShapeDtypeStruct((sensors, block * params), jnp.bfloat16),
-            jax.ShapeDtypeStruct((sensors, block // 2 * params), jnp.bfloat16),
+            jax.ShapeDtypeStruct((sensors, LEADING * params), jnp.bfloat16),
             jax.ShapeDtypeStruct(pairs, jnp.float32),
         ),
         in_specs=[VMEM, VMEM],
@@ -222,10 +232,10 @@
             name="pair_part",
         )(mine, received, *paired)
 
-    near = planes // 2
+    near = -(-(block - LEADING) // arrivals.shape[1])
     head = pl.pallas_call(
         head_part,
-        out_shape=jax.ShapeDtypeStruct((block // 2, params, fields), jnp.bfloat16),
+        out_shape=jax.ShapeDtypeStruct((block - LEADING, params, fields), jnp.bfloat16),
         in_specs=[VMEM] * (near + 1),
         out_specs=VMEM,
         compiler_params=LIMIT,
@@ -252,20 +262,25 @@
     )(ordered, history, newer, upper)
     paired = pair(0, mine, theirs)
     width = 2 * fields
-    mine, theirs = pl.pallas_call(
-        second_part,
-        out_shape=(part, part),
-        in_specs=[VMEM] * 6,
-        out_specs=(VMEM, VMEM),
-        scratch_shapes=[
-            pltpu.VMEM(((3 * block // 2 - 2) * params, width), jnp.bfloat16),
-            pltpu.VMEM(((3 * block // 2 - 2) * params, width), jnp.bfloat16),
-            pltpu.VMEM(((2 * block - 2) * params, width), jnp.bfloat16),
-        ],
-        compiler_params=pltpu.CompilerParams(vmem_limit_bytes=12 * 1024 * 1024),
-        cost_estimate=work(4 * 10**9, 8 * 10**6),
-        name="second_part",
-    )(ordered, following, history, newer, head_twice, last)
+
+    def second(side):
+        return pl.pallas_call(
+            functools.partial(second_part, side),
+            out_shape=part,
+            in_specs=[VMEM] * 6,
+            out_specs=VMEM,
+            scratch_shapes=[
+                pltpu.VMEM(((block - 2 + LEADING) * params, width), jnp.bfloat16),
+                pltpu.VMEM(((2 * block - 2 - LEADING) * params, width), jnp.bfloat16),
+                pltpu.VMEM(((2 * block - 2) * params, width), jnp.bfloat16),
+            ],
+            compiler_params=pltpu.CompilerParams(vmem_limit_bytes=12 * 1024 * 1024),
+            cost_estimate=work(2 * 10**9, 8 * 10**6),
+            name="second_part",
+        )(ordered, following, history, newer, head_twice, last)
+
+    theirs = second(1)
+    mine = second(0)
     paired = pair(1, mine, theirs, paired)
     arrived = exchange(paired, ("x", "y"))
     summed = pl.pallas_call(

time: 89.9 us -> 91.7 us (1.020)
  waiting for transfers between devices: 22.7 us -> 31.4 us
  blocking collectives: 42.1 us -> 34.6 us
    ppermute x3, waiting for transfers between devices: 7.46 us -> 15.6 us  [onward(): lax.ppermute(array, axis, [(i, i + by) for i in range(size) if 0 <= i + b...]
    all_to_all x2, blocking collectives: 42.1 us -> 34.6 us  [exchange(): return lax.all_to_all(parts, axis, split_axis=0, concat_axis=0, tiled=True)]
    ppermute x7, waiting for transfers between devices: 13.5 us -> 15.6 us  [observed(): pieces[source] = lax.ppermute(arrivals, 'z', [(source, 0)])]
    ppermute x2, waiting for transfers between devices: 1.76 us -> 0.12 us  [ring(): lax.ppermute(array, axis, [(i, (i + by) % size) for i in range(size)])]
    pallas_call x2 -> x3, Pallas kernels: 2.62 us -> 3.32 us  [the longest x2 3.25 us: second(): pl.pallas_call(functools.partial(second_part, side), out_shape=part, in_s...]
where the time goes in v6:
time: 91.7 us; the launch traced here: 90.9 us
  blocking collectives  34.6 us (38%)
  waiting for transfers between devices  31.4 us (34%)
  starting transfers between devices  14.8 us (16%)
  Pallas kernels  7.08 us (8%)
  local copies, waits for them, and re-layouts  2.28 us (2%)
    all_to_all x2, blocking collectives, exchange(): return lax.all_to_all(parts, axis, split_axis=0, concat_axis=0, tiled=True)  34.6 us
    ppermute x3, waiting for transfers between devices, onward(): lax.ppermute(array, axis, [(i, i + by) for i in range(size) if 0 <= i + b...  15.6 us
    ppermute x7, waiting for transfers between devices, observed(): pieces[source] = lax.ppermute(arrivals, 'z', [(source, 0)])  15.6 us
    ppermute x3, starting transfers between devices, onward(): lax.ppermute(array, axis, [(i, i + by) for i in range(size) if 0 <= i + b...  8.04 us
    ppermute x7, starting transfers between devices, observed(): pieces[source] = lax.ppermute(arrivals, 'z', [(source, 0)])  6.54 us
    pallas_call x2, Pallas kernels, second(): pl.pallas_call(functools.partial(second_part, side), out_shape=part, in_s...  3.25 us
    unnamed x8, local copies, waits for them, and re-layouts  2.27 us
  transfers between devices with their start and end apart: 12, of which 3 were waited for; matrix products, arithmetic and copies ran while one was open for 0% of the time, Pallas kernels for 7%

profile of v6, /device:TPU:32, one launch (start us, length us, event | category | flops | bytes accessed | tf_op | source)
XLA Modules:
  0.0 90.9 jit_solution(15893380982580642142)
XLA Ops:
  0.0 0.0 copy-start
  0.0 3.9 %collective-permute-start.8 = (bf16[16,128,128]{2,1,0:T(8,128)(2,1)}, bf16[16,128,128]{2,1,0:T(8,128)(2,1)S(1)}, u32[]{:S(2)}, u32[]{:S(2)}) collective-permute-start(bf16[16,128,128]{2,1,0:T(8,128)(2,1)} %older.7), channel_id=1, source_target_pairs={{0,32},{32,64},{64,96},{96,128},{128,160},{160,192},{192,224},{1,3... | collective-permute-start | bytes 1572872 | tf_op jit(solution)/shard_map/ppermute | solution.py:185
  4.0 0.0 copy-start.1
  4.0 1.2 %copy-done.1 = bf16[16,256,128]{2,1,0:T(8,128)(2,1)S(1)} copy-done((bf16[16,256,128]{2,1,0:T(8,128)(2,1)S(1)}, bf16[16,256,128]{2,1,0:T(8,128)(2,1)}, u32[]{:S(2)}) %copy-start.1) | copy-done | bytes 1048600
  5.2 0.0 copy-start.2
  5.2 1.0 %copy-done.2 = bf16[16,128,128]{2,1,0:T(8,128)(2,1)S(1)} copy-done((bf16[16,128,128]{2,1,0:T(8,128)(2,1)S(1)}, bf16[16,128,128]{2,1,0:T(8,128)(2,1)}, u32[]{:S(2)}) %copy-start.2) | copy-done | bytes 524312
  6.2 1.8 %first_part.1 = (bf16[256,2048]{1,0:T(8,128)(2,1)S(1)}, bf16[256,1152]{1,0:T(8,128)(2,1)S(1)}, f32[7,256,256]{2,1,0:T(8,128)S(1)}) custom-call(bf16[16,256,128]{2,1,0:T(8,128)(2,1)S(1)} %copy-done.1, bf16[16,128,128]{2,1,0:T(8,128)(2,1)S(1)} %copy-done.2), custom_call_target="tpu_custom_call" | custom-call | flops 2000000000 | bytes 4000000 | tf_op jit(solution)/shard_map/first_part/pallas_call | solution.py:206
  8.0 0.0 copy-start.3
  8.0 2.2 %collective-permute-start = (bf16[256,1152]{1,0:T(8,128)(2,1)S(1)}, bf16[256,1152]{1,0:T(8,128)(2,1)S(1)}, u32[]{:S(2)}, u32[]{:S(2)}) collective-permute-start(bf16[256,1152]{1,0:T(8,128)(2,1)S(1)} %get-tuple-element.13), channel_id=1, source_target_pairs={{32,0},{64,32},{96,64},{128,96},{160,128},{192,160},{224,192},{33,... | collective-permute-start | bytes 1769480 | tf_op jit(solution)/shard_map/ppermute | solution.py:185
  10.2 0.0 copy-done
  10.2 0.7 collective-permute-start.3
  10.9 0.7 collective-permute-start.2
  11.6 2.5 %collective-permute-start.1 = (bf16[2,2,128,128]{3,2,1,0:T(8,128)(2,1)S(1)}, bf16[2,2,128,128]{3,2,1,0:T(8,128)(2,1)S(1)}, u32[]{:S(2)}, u32[]{:S(2)}) collective-permute-start(bf16[2,2,128,128]{3,2,1,0:T(8,128)(2,1)S(1)} %copy-done), channel_id=1, source_target_pairs={{32,0},{33,1},{34,2},{35,3},{36,4},{37,5},{38,6},{39,7},{40,8},{41... | collective-permute-start | bytes 393224 | tf_op jit(solution)/shard_map/ppermute | solution.py:204
  14.1 0.0 collective-permute-done.3.refs_3_
  14.1 0.7 collective-permute-start.7
  14.8 0.0 collective-permute-done.2.refs_2_
  14.8 0.7 collective-permute-start.6
  15.5 15.6 %collective-permute-done.1.refs_1_ = bf16[2,2,128,128]{3,2,1,0:T(8,128)(2,1)S(1)} collective-permute-done((bf16[2,2,128,128]{3,2,1,0:T(8,128)(2,1)S(1)}, bf16[2,2,128,128]{3,2,1,0:T(8,128)(2,1)S(1)}, u32[]{:S(2)}, u32[]{:S(2)}) %collective-permute-start.1) | collective-permute-done | bytes 131104 | tf_op jit(solution)/shard_map/ppermute | solution.py:204
  31.1 0.7 collective-permute-start.5
  31.7 0.0 collective-permute-done.8.refs_8_.refs_4_
  31.7 0.7 collective-permute-start.4
  32.4 0.1 head_part.1
  32.5 0.0 collective-permute-done.7.refs_7_
  32.5 1.9 %collective-permute-start.9 = (bf16[7,128,128]{2,1,0:T(8,128)(2,1)S(1)}, bf16[7,128,128]{2,1,0:T(8,128)(2,1)S(1)}, u32[]{:S(2)}, u32[]{:S(2)}) collective-permute-start(bf16[7,128,128]{2,1,0:T(8,128)(2,1)S(1)} %head_part.1), channel_id=1, source_target_pairs={{0,32},{32,64},{64,96},{96,128},{128,160},{160,192},{192,224},{1,3... | collective-permute-start | bytes 688136 | tf_op jit(solution)/shard_map/ppermute | solution.py:185
  34.4 0.0 collective-permute-done.6.refs_6_
  34.4 0.0 collective-permute-done.5.refs_5_
  34.5 0.0 collective-permute-done.4.refs_4_
  34.5 0.2 newer_part.1
  34.6 0.0 copy-done.3
  34.7 1.4 %lower_part.1 = (bf16[16,16,8,128]{3,2,1,0:T(8,128)(2,1)S(1)}, bf16[16,16,8,128]{3,2,1,0:T(8,128)(2,1)S(1)}) custom-call(bf16[256,2048]{1,0:T(8,128)(2,1)S(1)} %get-tuple-element.12.ordered, bf16[16,128,128]{2,1,0:T(8,128)(2,1)S(1)} %copy-done.3, bf16[16,128,128]{2,1,0:T(8,128)(2,1)S(1)} %get-tuple-element.14.newer, f32[7,256,256]{2,1,0:T(8,128)S(1)} %get-tuple-element.16.upper), custom_call_target="tpu_custom_call" | custom-call | flops 2000000000 | bytes 6000000 | tf_op jit(solution)/shard_map/lower_part/pallas_call | solution.py:253
  36.1 0.1 collective-permute-start.11
  36.2 0.0 collective-permute-done.following
  36.2 15.6 %collective-permute-done.9.head = bf16[7,128,128]{2,1,0:T(8,128)(2,1)S(1)} collective-permute-done((bf16[7,128,128]{2,1,0:T(8,128)(2,1)S(1)}, bf16[7,128,128]{2,1,0:T(8,128)(2,1)S(1)}, u32[]{:S(2)}, u32[]{:S(2)}) %collective-permute-start.9) | collective-permute-done | bytes 229408 | tf_op jit(solution)/shard_map/ppermute | solution.py:185
  51.8 1.6 %second_part.3 = bf16[16,16,8,128]{3,2,1,0:T(8,128)(2,1)S(1)} custom-call(bf16[256,2048]{1,0:T(8,128)(2,1)S(1)} %get-tuple-element.12.ordered, bf16[256,1152]{1,0:T(8,128)(2,1)S(1)} %collective-permute-done.following, bf16[16,128,128]{2,1,0:T(8,128)(2,1)S(1)} %copy-done.3, bf16[16,128,128]{2,1,0:T(8,128)(2,1)S(1)} %get-tuple-element.14.newer, ...), custom_call_target="tpu_custom_call" | custom-call | flops 2000000000 | bytes 8000000 | tf_op jit(solution)/shard_map/second_part/pallas_call | solution.py:267
  53.5 0.1 collective-permute-start.10
  53.6 1.6 %second_part.2.mine = bf16[16,16,8,128]{3,2,1,0:T(8,128)(2,1)S(1)} custom-call(bf16[256,2048]{1,0:T(8,128)(2,1)S(1)} %get-tuple-element.12.ordered, bf16[256,1152]{1,0:T(8,128)(2,1)S(1)} %collective-permute-done.following, bf16[16,128,128]{2,1,0:T(8,128)(2,1)S(1)} %copy-done.3, bf16[16,128,128]{2,1,0:T(8,128)(2,1)S(1)} %get-tuple-element.14.newer, ...), custom_call_target="tpu_custom_call" | custom-call | flops 2000000000 | bytes 8000000 | tf_op jit(solution)/shard_map/second_part/pallas_call | solution.py:267
  55.2 0.0 collective-permute-done.11.received
  55.2 0.1 pair_part.2.refs_0_
  55.4 0.1 collective-permute-done.10.received
  55.5 0.1 pair_part.3
  55.6 24.5 %all_to_all.10.arrived = bf16[16,32,8,128]{3,2,1,0:T(8,128)(2,1)S(1)} all-to-all(bf16[16,32,8,128]{3,2,1,0:T(8,128)(2,1)S(1)} %pair_part.3), channel_id=1, replica_groups=mesh['z'=8,'x'=4,'y'=4,'c'=2] {'x','y'}, dimensions={0} | all-to-all | bytes 2097152 | tf_op jit(solution)/shard_map/all_to_all | solution.py:189
  80.1 0.1 plane_part.1
  80.3 10.0 %all_to_all.11 = bf16[8,32,128]{2,1,0:T(8,128)(2,1)S(1)} all-to-all(bf16[8,32,128]{2,1,0:T(8,128)(2,1)S(1)} %copy.5), channel_id=1, replica_groups=mesh['z'=8,'x'=4,'y'=4,'c'=2] {'z'}, dimensions={0} | all-to-all | bytes 131072 | tf_op jit(solution)/shard_map/all_to_all | solution.py:189
  90.3 0.6 reduce_sum.12
  (1 shorter events, 0.0 us)
Async XLA Ops:
  0.0 10.2 %copy-start = (bf16[2,2,128,128]{3,2,1,0:T(8,128)(2,1)S(1)}, bf16[2,2,128,128]{3,2,1,0:T(8,128)(2,1)}, u32[]{:S(2)}) copy-start(bf16[2,2,128,128]{3,2,1,0:T(8,128)(2,1)} %refs_0_.3) | copy-start | bytes 393220
  0.0 31.7 %collective-permute-start.8 = (bf16[16,128,128]{2,1,0:T(8,128)(2,1)}, bf16[16,128,128]{2,1,0:T(8,128)(2,1)S(1)}, u32[]{:S(2)}, u32[]{:S(2)}) collective-permute-start(bf16[16,128,128]{2,1,0:T(8,128)(2,1)} %older.7), channel_id=1, source_target_pairs={{0,32},{32,64},{64,96},{96,128},{128,160},{160,192},{192,224},{1,3... | collective-permute-start | bytes 1572872 | tf_op jit(solution)/shard_map/ppermute | solution.py:185
  4.0 1.2 %copy-start.1 = (bf16[16,256,128]{2,1,0:T(8,128)(2,1)S(1)}, bf16[16,256,128]{2,1,0:T(8,128)(2,1)}, u32[]{:S(2)}) copy-start(bf16[16,256,128]{2,1,0:T(8,128)(2,1)} %kernel.1) | copy-start | bytes 3145732
  5.2 1.0 %copy-start.2 = (bf16[16,128,128]{2,1,0:T(8,128)(2,1)S(1)}, bf16[16,128,128]{2,1,0:T(8,128)(2,1)}, u32[]{:S(2)}) copy-start(bf16[16,128,128]{2,1,0:T(8,128)(2,1)} %older.7) | copy-start | bytes 1572868
  8.0 26.6 %copy-start.3 = (bf16[16,128,128]{2,1,0:T(8,128)(2,1)S(1)}, bf16[16,128,128]{2,1,0:T(8,128)(2,1)}, u32[]{:S(2)}) copy-start(bf16[16,128,128]{2,1,0:T(8,128)(2,1)} %older.7) | copy-start | bytes 1572868
  8.0 28.2 %collective-permute-start = (bf16[256,1152]{1,0:T(8,128)(2,1)S(1)}, bf16[256,1152]{1,0:T(8,128)(2,1)S(1)}, u32[]{:S(2)}, u32[]{:S(2)}) collective-permute-start(bf16[256,1152]{1,0:T(8,128)(2,1)S(1)} %get-tuple-element.13), channel_id=1, source_target_pairs={{32,0},{64,32},{96,64},{128,96},{160,128},{192,160},{224,192},{33,... | collective-permute-start | bytes 1769480 | tf_op jit(solution)/shard_map/ppermute | solution.py:185
  10.2 3.9 %collective-permute-start.3 = (bf16[2,2,128,128]{3,2,1,0:T(8,128)(2,1)S(1)}, bf16[2,2,128,128]{3,2,1,0:T(8,128)(2,1)S(1)}, u32[]{:S(2)}, u32[]{:S(2)}) collective-permute-start(bf16[2,2,128,128]{3,2,1,0:T(8,128)(2,1)S(1)} %copy-done), channel_id=1, source_target_pairs={{96,0},{97,1},{98,2},{99,3},{100,4},{101,5},{102,6},{103,7},{104,8... | collective-permute-start | bytes 393224 | tf_op jit(solution)/shard_map/ppermute | solution.py:204
  10.9 3.9 %collective-permute-start.2 = (bf16[2,2,128,128]{3,2,1,0:T(8,128)(2,1)S(1)}, bf16[2,2,128,128]{3,2,1,0:T(8,128)(2,1)S(1)}, u32[]{:S(2)}, u32[]{:S(2)}) collective-permute-start(bf16[2,2,128,128]{3,2,1,0:T(8,128)(2,1)S(1)} %copy-done), channel_id=1, source_target_pairs={{64,0},{65,1},{66,2},{67,3},{68,4},{69,5},{70,6},{71,7},{72,8},{73... | collective-permute-start | bytes 393224 | tf_op jit(solution)/shard_map/ppermute | solution.py:204
  11.6 19.5 %collective-permute-start.1 = (bf16[2,2,128,128]{3,2,1,0:T(8,128)(2,1)S(1)}, bf16[2,2,128,128]{3,2,1,0:T(8,128)(2,1)S(1)}, u32[]{:S(2)}, u32[]{:S(2)}) collective-permute-start(bf16[2,2,128,128]{3,2,1,0:T(8,128)(2,1)S(1)} %copy-done), channel_id=1, source_target_pairs={{32,0},{33,1},{34,2},{35,3},{36,4},{37,5},{38,6},{39,7},{40,8},{41... | collective-permute-start | bytes 393224 | tf_op jit(solution)/shard_map/ppermute | solution.py:204
  14.1 18.4 %collective-permute-start.7 = (bf16[2,2,128,128]{3,2,1,0:T(8,128)(2,1)S(1)}, bf16[2,2,128,128]{3,2,1,0:T(8,128)(2,1)S(1)}, u32[]{:S(2)}, u32[]{:S(2)}) collective-permute-start(bf16[2,2,128,128]{3,2,1,0:T(8,128)(2,1)S(1)} %copy-done), channel_id=1, source_target_pairs={{224,0},{225,1},{226,2},{227,3},{228,4},{229,5},{230,6},{231,7},{2... | collective-permute-start | bytes 393224 | tf_op jit(solution)/shard_map/ppermute | solution.py:204
  14.8 19.6 %collective-permute-start.6 = (bf16[2,2,128,128]{3,2,1,0:T(8,128)(2,1)S(1)}, bf16[2,2,128,128]{3,2,1,0:T(8,128)(2,1)S(1)}, u32[]{:S(2)}, u32[]{:S(2)}) collective-permute-start(bf16[2,2,128,128]{3,2,1,0:T(8,128)(2,1)S(1)} %copy-done), channel_id=1, source_target_pairs={{192,0},{193,1},{194,2},{195,3},{196,4},{197,5},{198,6},{199,7},{2... | collective-permute-start | bytes 393224 | tf_op jit(solution)/shard_map/ppermute | solution.py:204
  31.1 3.4 %collective-permute-start.5 = (bf16[2,2,128,128]{3,2,1,0:T(8,128)(2,1)S(1)}, bf16[2,2,128,128]{3,2,1,0:T(8,128)(2,1)S(1)}, u32[]{:S(2)}, u32[]{:S(2)}) collective-permute-start(bf16[2,2,128,128]{3,2,1,0:T(8,128)(2,1)S(1)} %copy-done), channel_id=1, source_target_pairs={{160,0},{161,1},{162,2},{163,3},{164,4},{165,5},{166,6},{167,7},{1... | collective-permute-start | bytes 393224 | tf_op jit(solution)/shard_map/ppermute | solution.py:204
  31.7 2.7 %collective-permute-start.4 = (bf16[2,2,128,128]{3,2,1,0:T(8,128)(2,1)S(1)}, bf16[2,2,128,128]{3,2,1,0:T(8,128)(2,1)S(1)}, u32[]{:S(2)}, u32[]{:S(2)}) collective-permute-start(bf16[2,2,128,128]{3,2,1,0:T(8,128)(2,1)S(1)} %copy-done), channel_id=1, source_target_pairs={{128,0},{129,1},{130,2},{131,3},{132,4},{133,5},{134,6},{135,7},{1... | collective-permute-start | bytes 393224 | tf_op jit(solution)/shard_map/ppermute | solution.py:204
  32.5 19.3 %collective-permute-start.9 = (bf16[7,128,128]{2,1,0:T(8,128)(2,1)S(1)}, bf16[7,128,128]{2,1,0:T(8,128)(2,1)S(1)}, u32[]{:S(2)}, u32[]{:S(2)}) collective-permute-start(bf16[7,128,128]{2,1,0:T(8,128)(2,1)S(1)} %head_part.1), channel_id=1, source_target_pairs={{0,32},{32,64},{64,96},{96,128},{128,160},{160,192},{192,224},{1,3... | collective-permute-start | bytes 688136 | tf_op jit(solution)/shard_map/ppermute | solution.py:185
  36.1 19.1 %collective-permute-start.11 = (bf16[16,16,8,128]{3,2,1,0:T(8,128)(2,1)S(1)}, bf16[16,16,8,128]{3,2,1,0:T(8,128)(2,1)S(1)}, u32[]{:S(2)}, u32[]{:S(2)}) collective-permute-start(bf16[16,16,8,128]{3,2,1,0:T(8,128)(2,1)S(1)} %get-tuple-element.18), channel_id=1, source_target_pairs={{0,1},{1,0},{2,3},{3,2},{4,5},{5,4},{6,7},{7,6},{8,9},{9,8},{10,11... | collective-permute-start | bytes 1572872 | tf_op jit(solution)/shard_map/ppermute | solution.py:180
  53.5 2.0 %collective-permute-start.10 = (bf16[16,16,8,128]{3,2,1,0:T(8,128)(2,1)S(1)}, bf16[16,16,8,128]{3,2,1,0:T(8,128)(2,1)S(1)}, u32[]{:S(2)}, u32[]{:S(2)}) collective-permute-start(bf16[16,16,8,128]{3,2,1,0:T(8,128)(2,1)S(1)} %second_part.3), channel_id=1, source_target_pairs={{0,1},{1,0},{2,3},{3,2},{4,5},{5,4},{6,7},{7,6},{8,9},{9,8},{10,11... | collective-permute-start | bytes 1572872 | tf_op jit(solution)/shard_map/ppermute | solution.py:180

commit v7 on v6

--- a/solution.py
+++ b/solution.py
@@ -92,22 +92,24 @@
     put_half(sums[count:], pair, theirs)
 
 
-def second_part(
-    side, ordered, following, older, newer, head, last, half, ahead, behind, arrivals
-):
-    block, params, fields = older.shape
+def second_part(side, ordered, following, ahead, *refs):
+    *blocks, half, behind = refs if side else (*refs[1:], refs[0])
+    block = half.shape[1]
+    params = ordered.shape[1] // block
+    fields = ahead.shape[1] // 2
     lags = following.shape[1] // params
     plane = lax.axis_index("z")
     count = ordered.shape[0] // 2
     rows = slice(side * count, (side + 1) * count)
-    windows(after(older, newer), block + 1 - lags, 2 * block - 2, params, fields, ahead)
 
     def conv(left, right, pair):
         return product(left, right, (block - 2 - 2 * pair) * params)
 
     @pl.when(plane != 0)
     def _():
-        windows(after(newer, head), 1, 2 * block - 2 - lags, params, fields, behind)
+        if blocks:
+            newer, head, _ = blocks
+            windows(after(newer, head), 1, 2 * block - 2 - lags, params, fields, behind)
         for pair in range(block // 2):
             sums = conv(following[rows], ahead, pair)
             sums = sums + conv(ordered[rows, lags * params :], behind, pair)
@@ -115,13 +117,15 @@
 
     @pl.when(plane == 0)
     def _():
-        windows(after(newer, last), 1, 2 * block - 2, params, fields, arrivals)
+        if blocks:
+            newer, _, last = blocks
+            windows(after(newer, last), 1, 2 * block - 2, params, fields, behind)
         for pair in range(block // 2):
-            sums = conv(following[rows], ahead, pair) + conv(ordered[rows], arrivals, pair)
+            sums = conv(following[rows], ahead, pair) + conv(ordered[rows], behind, pair)
             put_half(sums, pair, half)
 
 
-def lower_part(ordered, older, newer, upper, mine, theirs, times):
+def lower_part(ordered, older, newer, upper, mine, theirs, ahead, times):
     block, params, fields = newer.shape
     for time in range(-1, block):
         value = newer[time] if time >= 0 else older[block - 1]
@@ -138,6 +142,9 @@
         if pair < block // 2 - 1:
             sums = sums + upper[pair]
         put(sums, pair, mine, theirs)
+    windows(
+        after(older, newer), block + 1 - LEADING, 2 * block - 2, params, fields, ahead
+    )
 
 
 def head_part(*refs):
@@ -250,11 +257,17 @@
         compiler_params=LIMIT,
         name="newer_part",
     )(*pieces, shifted)
-    mine, theirs = pl.pallas_call(
+    mine, theirs, ahead = pl.pallas_call(
         lower_part,
-        out_shape=(part, part),
+        out_shape=(
+            part,
+            part,
+            jax.ShapeDtypeStruct(
+                ((block - 2 + LEADING) * params, 2 * fields), jnp.bfloat16
+            ),
+        ),
         in_specs=[VMEM] * 4,
-        out_specs=(VMEM, VMEM),
+        out_specs=(VMEM, VMEM, VMEM),
         scratch_shapes=scratch,
         compiler_params=LIMIT,
         cost_estimate=work(2 * 10**9, 6 * 10**6),
@@ -263,24 +276,21 @@
     paired = pair(0, mine, theirs)
     width = 2 * fields
 
-    def second(side):
+    window = jax.ShapeDtypeStruct(((2 * block - 2) * params, width), jnp.bfloat16)
+
+    def second(side, *blocks):
         return pl.pallas_call(
             functools.partial(second_part, side),
-            out_shape=part,
-            in_specs=[VMEM] * 6,
-            out_specs=VMEM,
-            scratch_shapes=[
-                pltpu.VMEM(((block - 2 + LEADING) * params, width), jnp.bfloat16),
-                pltpu.VMEM(((2 * block - 2 - LEADING) * params, width), jnp.bfloat16),
-                pltpu.VMEM(((2 * block - 2) * params, width), jnp.bfloat16),
-            ],
+            out_shape=(part, window) if side else part,
+            in_specs=[VMEM] * (3 + len(blocks)),
+            out_specs=(VMEM, VMEM) if side else VMEM,
             compiler_params=pltpu.CompilerParams(vmem_limit_bytes=12 * 1024 * 1024),
             cost_estimate=work(2 * 10**9, 8 * 10**6),
             name="second_part",
-        )(ordered, following, history, newer, head_twice, last)
-
-    theirs = second(1)
-    mine = second(0)
+        )(ordered, following, ahead, *blocks)
+
+    theirs, behind = second(1, newer, head_twice, last)
+    mine = second(0, behind)
     paired = pair(1, mine, theirs, paired)
     arrived = exchange(paired, ("x", "y"))
     summed = pl.pallas_call(

time: 91.7 us -> 91.3 us (level)
  no operation moved by 1% of the time
where the time goes in v7:
time: 91.3 us; the launch traced here: 90.5 us
  blocking collectives  34.3 us (38%)
  waiting for transfers between devices  31.4 us (34%)
  starting transfers between devices  14.8 us (16%)
  Pallas kernels  6.81 us (7%)
  local copies, waits for them, and re-layouts  2.28 us (2%)
    all_to_all x2, blocking collectives, exchange(): return lax.all_to_all(parts, axis, split_axis=0, concat_axis=0, tiled=True)  34.3 us
    ppermute x7, waiting for transfers between devices, observed(): pieces[source] = lax.ppermute(arrivals, 'z', [(source, 0)])  15.6 us
    ppermute x3, waiting for transfers between devices, onward(): lax.ppermute(array, axis, [(i, i + by) for i in range(size) if 0 <= i + b...  15.5 us
    ppermute x3, starting transfers between devices, onward(): lax.ppermute(array, axis, [(i, i + by) for i in range(size) if 0 <= i + b...  8.04 us
    ppermute x7, starting transfers between devices, observed(): pieces[source] = lax.ppermute(arrivals, 'z', [(source, 0)])  6.54 us
    pallas_call x2, Pallas kernels, second(): pl.pallas_call(functools.partial(second_part, side), out_shape=(part, win...  2.85 us
    unnamed x8, local copies, waits for them, and re-layouts  2.27 us
  transfers between devices with their start and end apart: 12, of which 3 were waited for; matrix products, arithmetic and copies ran while one was open for 0% of the time, Pallas kernels for 7%

profile of v7, /device:TPU:32, one launch (start us, length us, event | category | flops | bytes accessed | tf_op | source)
XLA Modules:
  0.0 90.5 jit_solution(14696689684598021266)
XLA Ops:
  0.0 0.0 copy-start
  0.0 3.9 %collective-permute-start.8 = (bf16[16,128,128]{2,1,0:T(8,128)(2,1)}, bf16[16,128,128]{2,1,0:T(8,128)(2,1)S(1)}, u32[]{:S(2)}, u32[]{:S(2)}) collective-permute-start(bf16[16,128,128]{2,1,0:T(8,128)(2,1)} %older.3), channel_id=1, source_target_pairs={{0,32},{32,64},{64,96},{96,128},{128,160},{160,192},{192,224},{1,3... | collective-permute-start | bytes 1572872 | tf_op jit(solution)/shard_map/ppermute | solution.py:192
  4.0 0.0 copy-start.1
  4.0 1.2 %copy-done.1 = bf16[16,256,128]{2,1,0:T(8,128)(2,1)S(1)} copy-done((bf16[16,256,128]{2,1,0:T(8,128)(2,1)S(1)}, bf16[16,256,128]{2,1,0:T(8,128)(2,1)}, u32[]{:S(2)}) %copy-start.1) | copy-done | bytes 1048600
  5.2 0.0 copy-start.2
  5.2 1.0 %copy-done.2 = bf16[16,128,128]{2,1,0:T(8,128)(2,1)S(1)} copy-done((bf16[16,128,128]{2,1,0:T(8,128)(2,1)S(1)}, bf16[16,128,128]{2,1,0:T(8,128)(2,1)}, u32[]{:S(2)}) %copy-start.2) | copy-done | bytes 524312
  6.2 1.8 %first_part.1 = (bf16[256,2048]{1,0:T(8,128)(2,1)S(1)}, bf16[256,1152]{1,0:T(8,128)(2,1)S(1)}, f32[7,256,256]{2,1,0:T(8,128)S(1)}) custom-call(bf16[16,256,128]{2,1,0:T(8,128)(2,1)S(1)} %copy-done.1, bf16[16,128,128]{2,1,0:T(8,128)(2,1)S(1)} %copy-done.2), custom_call_target="tpu_custom_call" | custom-call | flops 2000000000 | bytes 4000000 | tf_op jit(solution)/shard_map/first_part/pallas_call | solution.py:213
  8.0 0.0 copy-start.3
  8.0 2.2 %collective-permute-start = (bf16[256,1152]{1,0:T(8,128)(2,1)S(1)}, bf16[256,1152]{1,0:T(8,128)(2,1)S(1)}, u32[]{:S(2)}, u32[]{:S(2)}) collective-permute-start(bf16[256,1152]{1,0:T(8,128)(2,1)S(1)} %get-tuple-element.16), channel_id=1, source_target_pairs={{32,0},{64,32},{96,64},{128,96},{160,128},{192,160},{224,192},{33,... | collective-permute-start | bytes 1769480 | tf_op jit(solution)/shard_map/ppermute | solution.py:192
  10.2 0.0 copy-done
  10.2 0.7 collective-permute-start.3
  10.9 0.7 collective-permute-start.2
  11.6 2.5 %collective-permute-start.1 = (bf16[2,2,128,128]{3,2,1,0:T(8,128)(2,1)S(1)}, bf16[2,2,128,128]{3,2,1,0:T(8,128)(2,1)S(1)}, u32[]{:S(2)}, u32[]{:S(2)}) collective-permute-start(bf16[2,2,128,128]{3,2,1,0:T(8,128)(2,1)S(1)} %copy-done), channel_id=1, source_target_pairs={{32,0},{33,1},{34,2},{35,3},{36,4},{37,5},{38,6},{39,7},{40,8},{41... | collective-permute-start | bytes 393224 | tf_op jit(solution)/shard_map/ppermute | solution.py:211
  14.1 0.0 collective-permute-done.3.refs_3_
  14.1 0.7 collective-permute-start.7
  14.8 0.0 collective-permute-done.2.refs_2_
  14.8 0.7 collective-permute-start.6
  15.5 15.6 %collective-permute-done.1.refs_1_ = bf16[2,2,128,128]{3,2,1,0:T(8,128)(2,1)S(1)} collective-permute-done((bf16[2,2,128,128]{3,2,1,0:T(8,128)(2,1)S(1)}, bf16[2,2,128,128]{3,2,1,0:T(8,128)(2,1)S(1)}, u32[]{:S(2)}, u32[]{:S(2)}) %collective-permute-start.1) | collective-permute-done | bytes 131104 | tf_op jit(solution)/shard_map/ppermute | solution.py:211
  31.1 0.7 collective-permute-start.5
  31.7 0.0 collective-permute-done.8.refs_8_.refs_4_
  31.7 0.7 collective-permute-start.4
  32.4 0.1 head_part.1
  32.5 0.0 collective-permute-done.7.refs_7_
  32.5 1.9 %collective-permute-start.9 = (bf16[7,128,128]{2,1,0:T(8,128)(2,1)S(1)}, bf16[7,128,128]{2,1,0:T(8,128)(2,1)S(1)}, u32[]{:S(2)}, u32[]{:S(2)}) collective-permute-start(bf16[7,128,128]{2,1,0:T(8,128)(2,1)S(1)} %head_part.1), channel_id=1, source_target_pairs={{0,32},{32,64},{64,96},{96,128},{128,160},{160,192},{192,224},{1,3... | collective-permute-start | bytes 688136 | tf_op jit(solution)/shard_map/ppermute | solution.py:192
  34.4 0.0 collective-permute-done.6.refs_6_
  34.4 0.0 collective-permute-done.5.refs_5_
  34.5 0.0 collective-permute-done.4.refs_4_
  34.5 0.2 newer_part.1
  34.6 0.0 copy-done.3
  34.7 1.6 %lower_part.1 = (bf16[16,16,8,128]{3,2,1,0:T(8,128)(2,1)S(1)}, bf16[16,16,8,128]{3,2,1,0:T(8,128)(2,1)S(1)}, bf16[2944,256]{1,0:T(8,128)(2,1)S(1)}) custom-call(bf16[256,2048]{1,0:T(8,128)(2,1)S(1)} %get-tuple-element.15.ordered, bf16[16,128,128]{2,1,0:T(8,128)(2,1)S(1)} %copy-done.3, bf16[16,128,128]{2,1,0:T(8,128)(2,1)S(1)} %get-tuple-element.17.newer.refs_0_, ...), custom_call_target="tpu_custom_call" | custom-call | flops 2000000000 | bytes 6000000 | tf_op jit(solution)/shard_map/lower_part/pallas_call | solution.py:260
  36.2 0.1 collective-permute-start.11
  36.3 0.0 collective-permute-done.following
  36.3 15.5 %collective-permute-done.9.refs_1_ = bf16[7,128,128]{2,1,0:T(8,128)(2,1)S(1)} collective-permute-done((bf16[7,128,128]{2,1,0:T(8,128)(2,1)S(1)}, bf16[7,128,128]{2,1,0:T(8,128)(2,1)S(1)}, u32[]{:S(2)}, u32[]{:S(2)}) %collective-permute-start.9) | collective-permute-done | bytes 229408 | tf_op jit(solution)/shard_map/ppermute | solution.py:192
  51.8 1.4 %second_part.2 = (bf16[16,16,8,128]{3,2,1,0:T(8,128)(2,1)S(1)}, bf16[3840,256]{1,0:T(8,128)(2,1)S(1)}) custom-call(bf16[256,2048]{1,0:T(8,128)(2,1)S(1)} %get-tuple-element.15.ordered, bf16[256,1152]{1,0:T(8,128)(2,1)S(1)} %collective-permute-done.following, bf16[2944,256]{1,0:T(8,128)(2,1)S(1)} %get-tuple-element.19.ahead, ...), custom_call_target="tpu_custom_call" | custom-call | flops 2000000000 | bytes 8000000 | tf_op jit(solution)/shard_map/second_part/pallas_call | solution.py:282
  53.3 0.1 collective-permute-start.10
  53.4 1.4 %second_part.3.mine = bf16[16,16,8,128]{3,2,1,0:T(8,128)(2,1)S(1)} custom-call(bf16[256,2048]{1,0:T(8,128)(2,1)S(1)} %get-tuple-element.15.ordered, bf16[256,1152]{1,0:T(8,128)(2,1)S(1)} %collective-permute-done.following, bf16[2944,256]{1,0:T(8,128)(2,1)S(1)} %get-tuple-element.19.ahead, bf16[3840,256]{1,0:T(8,128)(2,1)S(1)} %get-tuple-element.21.refs_0_), custom_call_target="tpu_custom_call" | custom-call | flops 2000000000 | bytes 8000000 | tf_op jit(solution)/shard_map/second_part/pallas_call | solution.py:282
  54.8 0.0 collective-permute-done.11.received
  54.8 0.1 pair_part.2.refs_0_
  54.9 0.3 collective-permute-done.10.received
  55.3 0.1 pair_part.3
  55.4 24.3 %all_to_all.10.arrived = bf16[16,32,8,128]{3,2,1,0:T(8,128)(2,1)S(1)} all-to-all(bf16[16,32,8,128]{3,2,1,0:T(8,128)(2,1)S(1)} %pair_part.3), channel_id=1, replica_groups=mesh['z'=8,'x'=4,'y'=4,'c'=2] {'x','y'}, dimensions={0} | all-to-all | bytes 2097152 | tf_op jit(solution)/shard_map/all_to_all | solution.py:196
  79.7 0.1 plane_part.1
  79.9 10.0 %all_to_all.11 = bf16[8,32,128]{2,1,0:T(8,128)(2,1)S(1)} all-to-all(bf16[8,32,128]{2,1,0:T(8,128)(2,1)S(1)} %copy.5), channel_id=1, replica_groups=mesh['z'=8,'x'=4,'y'=4,'c'=2] {'z'}, dimensions={0} | all-to-all | bytes 131072 | tf_op jit(solution)/shard_map/all_to_all | solution.py:196
  89.9 0.6 reduce_sum.12
  (1 shorter events, 0.0 us)
Async XLA Ops:
  0.0 10.2 %copy-start = (bf16[2,2,128,128]{3,2,1,0:T(8,128)(2,1)S(1)}, bf16[2,2,128,128]{3,2,1,0:T(8,128)(2,1)}, u32[]{:S(2)}) copy-start(bf16[2,2,128,128]{3,2,1,0:T(8,128)(2,1)} %refs_0_.3) | copy-start | bytes 393220
  0.0 31.7 %collective-permute-start.8 = (bf16[16,128,128]{2,1,0:T(8,128)(2,1)}, bf16[16,128,128]{2,1,0:T(8,128)(2,1)S(1)}, u32[]{:S(2)}, u32[]{:S(2)}) collective-permute-start(bf16[16,128,128]{2,1,0:T(8,128)(2,1)} %older.3), channel_id=1, source_target_pairs={{0,32},{32,64},{64,96},{96,128},{128,160},{160,192},{192,224},{1,3... | collective-permute-start | bytes 1572872 | tf_op jit(solution)/shard_map/ppermute | solution.py:192
  4.0 1.2 %copy-start.1 = (bf16[16,256,128]{2,1,0:T(8,128)(2,1)S(1)}, bf16[16,256,128]{2,1,0:T(8,128)(2,1)}, u32[]{:S(2)}) copy-start(bf16[16,256,128]{2,1,0:T(8,128)(2,1)} %kernel.1) | copy-start | bytes 3145732
  5.2 1.0 %copy-start.2 = (bf16[16,128,128]{2,1,0:T(8,128)(2,1)S(1)}, bf16[16,128,128]{2,1,0:T(8,128)(2,1)}, u32[]{:S(2)}) copy-start(bf16[16,128,128]{2,1,0:T(8,128)(2,1)} %older.3) | copy-start | bytes 1572868
  8.0 26.6 %copy-start.3 = (bf16[16,128,128]{2,1,0:T(8,128)(2,1)S(1)}, bf16[16,128,128]{2,1,0:T(8,128)(2,1)}, u32[]{:S(2)}) copy-start(bf16[16,128,128]{2,1,0:T(8,128)(2,1)} %older.3) | copy-start | bytes 1572868
  8.0 28.3 %collective-permute-start = (bf16[256,1152]{1,0:T(8,128)(2,1)S(1)}, bf16[256,1152]{1,0:T(8,128)(2,1)S(1)}, u32[]{:S(2)}, u32[]{:S(2)}) collective-permute-start(bf16[256,1152]{1,0:T(8,128)(2,1)S(1)} %get-tuple-element.16), channel_id=1, source_target_pairs={{32,0},{64,32},{96,64},{128,96},{160,128},{192,160},{224,192},{33,... | collective-permute-start | bytes 1769480 | tf_op jit(solution)/shard_map/ppermute | solution.py:192
  10.2 3.9 %collective-permute-start.3 = (bf16[2,2,128,128]{3,2,1,0:T(8,128)(2,1)S(1)}, bf16[2,2,128,128]{3,2,1,0:T(8,128)(2,1)S(1)}, u32[]{:S(2)}, u32[]{:S(2)}) collective-permute-start(bf16[2,2,128,128]{3,2,1,0:T(8,128)(2,1)S(1)} %copy-done), channel_id=1, source_target_pairs={{96,0},{97,1},{98,2},{99,3},{100,4},{101,5},{102,6},{103,7},{104,8... | collective-permute-start | bytes 393224 | tf_op jit(solution)/shard_map/ppermute | solution.py:211
  10.9 3.9 %collective-permute-start.2 = (bf16[2,2,128,128]{3,2,1,0:T(8,128)(2,1)S(1)}, bf16[2,2,128,128]{3,2,1,0:T(8,128)(2,1)S(1)}, u32[]{:S(2)}, u32[]{:S(2)}) collective-permute-start(bf16[2,2,128,128]{3,2,1,0:T(8,128)(2,1)S(1)} %copy-done), channel_id=1, source_target_pairs={{64,0},{65,1},{66,2},{67,3},{68,4},{69,5},{70,6},{71,7},{72,8},{73... | collective-permute-start | bytes 393224 | tf_op jit(solution)/shard_map/ppermute | solution.py:211
  11.6 19.5 %collective-permute-start.1 = (bf16[2,2,128,128]{3,2,1,0:T(8,128)(2,1)S(1)}, bf16[2,2,128,128]{3,2,1,0:T(8,128)(2,1)S(1)}, u32[]{:S(2)}, u32[]{:S(2)}) collective-permute-start(bf16[2,2,128,128]{3,2,1,0:T(8,128)(2,1)S(1)} %copy-done), channel_id=1, source_target_pairs={{32,0},{33,1},{34,2},{35,3},{36,4},{37,5},{38,6},{39,7},{40,8},{41... | collective-permute-start | bytes 393224 | tf_op jit(solution)/shard_map/ppermute | solution.py:211
  14.1 18.4 %collective-permute-start.7 = (bf16[2,2,128,128]{3,2,1,0:T(8,128)(2,1)S(1)}, bf16[2,2,128,128]{3,2,1,0:T(8,128)(2,1)S(1)}, u32[]{:S(2)}, u32[]{:S(2)}) collective-permute-start(bf16[2,2,128,128]{3,2,1,0:T(8,128)(2,1)S(1)} %copy-done), channel_id=1, source_target_pairs={{224,0},{225,1},{226,2},{227,3},{228,4},{229,5},{230,6},{231,7},{2... | collective-permute-start | bytes 393224 | tf_op jit(solution)/shard_map/ppermute | solution.py:211
  14.8 19.6 %collective-permute-start.6 = (bf16[2,2,128,128]{3,2,1,0:T(8,128)(2,1)S(1)}, bf16[2,2,128,128]{3,2,1,0:T(8,128)(2,1)S(1)}, u32[]{:S(2)}, u32[]{:S(2)}) collective-permute-start(bf16[2,2,128,128]{3,2,1,0:T(8,128)(2,1)S(1)} %copy-done), channel_id=1, source_target_pairs={{192,0},{193,1},{194,2},{195,3},{196,4},{197,5},{198,6},{199,7},{2... | collective-permute-start | bytes 393224 | tf_op jit(solution)/shard_map/ppermute | solution.py:211
  31.1 3.4 %collective-permute-start.5 = (bf16[2,2,128,128]{3,2,1,0:T(8,128)(2,1)S(1)}, bf16[2,2,128,128]{3,2,1,0:T(8,128)(2,1)S(1)}, u32[]{:S(2)}, u32[]{:S(2)}) collective-permute-start(bf16[2,2,128,128]{3,2,1,0:T(8,128)(2,1)S(1)} %copy-done), channel_id=1, source_target_pairs={{160,0},{161,1},{162,2},{163,3},{164,4},{165,5},{166,6},{167,7},{1... | collective-permute-start | bytes 393224 | tf_op jit(solution)/shard_map/ppermute | solution.py:211
  31.7 2.7 %collective-permute-start.4 = (bf16[2,2,128,128]{3,2,1,0:T(8,128)(2,1)S(1)}, bf16[2,2,128,128]{3,2,1,0:T(8,128)(2,1)S(1)}, u32[]{:S(2)}, u32[]{:S(2)}) collective-permute-start(bf16[2,2,128,128]{3,2,1,0:T(8,128)(2,1)S(1)} %copy-done), channel_id=1, source_target_pairs={{128,0},{129,1},{130,2},{131,3},{132,4},{133,5},{134,6},{135,7},{1... | collective-permute-start | bytes 393224 | tf_op jit(solution)/shard_map/ppermute | solution.py:211
  32.5 19.3 %collective-permute-start.9 = (bf16[7,128,128]{2,1,0:T(8,128)(2,1)S(1)}, bf16[7,128,128]{2,1,0:T(8,128)(2,1)S(1)}, u32[]{:S(2)}, u32[]{:S(2)}) collective-permute-start(bf16[7,128,128]{2,1,0:T(8,128)(2,1)S(1)} %head_part.1), channel_id=1, source_target_pairs={{0,32},{32,64},{64,96},{96,128},{128,160},{160,192},{192,224},{1,3... | collective-permute-start | bytes 688136 | tf_op jit(solution)/shard_map/ppermute | solution.py:192
  36.2 18.6 %collective-permute-start.11 = (bf16[16,16,8,128]{3,2,1,0:T(8,128)(2,1)S(1)}, bf16[16,16,8,128]{3,2,1,0:T(8,128)(2,1)S(1)}, u32[]{:S(2)}, u32[]{:S(2)}) collective-permute-start(bf16[16,16,8,128]{3,2,1,0:T(8,128)(2,1)S(1)} %get-tuple-element.24), channel_id=1, source_target_pairs={{0,1},{1,0},{2,3},{3,2},{4,5},{5,4},{6,7},{7,6},{8,9},{9,8},{10,11... | collective-permute-start | bytes 1572872 | tf_op jit(solution)/shard_map/ppermute | solution.py:187
  53.3 2.0 %collective-permute-start.10 = (bf16[16,16,8,128]{3,2,1,0:T(8,128)(2,1)S(1)}, bf16[16,16,8,128]{3,2,1,0:T(8,128)(2,1)S(1)}, u32[]{:S(2)}, u32[]{:S(2)}) collective-permute-start(bf16[16,16,8,128]{3,2,1,0:T(8,128)(2,1)S(1)} %get-tuple-element.22), channel_id=1, source_target_pairs={{0,1},{1,0},{2,3},{3,2},{4,5},{5,4},{6,7},{7,6},{8,9},{9,8},{10,11... | collective-permute-start | bytes 1572872 | tf_op jit(solution)/shard_map/ppermute | solution.py:187

commit v8 on v6

--- a/solution.py
+++ b/solution.py
@@ -9,7 +9,7 @@
 from jax.sharding import PartitionSpec as P
 
 ORDER = (5, 6, 7, 4, 3, 2, 1)
-LEADING = 9
+LEADING = 8
 PAR = ("x", "y", "c")
 EVERY = ("z", "x", "y", "c")
 VMEM = pl.BlockSpec(memory_space=pltpu.VMEM)
@@ -92,15 +92,12 @@
     put_half(sums[count:], pair, theirs)
 
 
-def second_part(
-    side, ordered, following, older, newer, head, last, half, ahead, behind, arrivals
-):
-    block, params, fields = older.shape
+def second_part(side, ordered, following, ahead, newer, head, last, half, behind, arrivals):
+    block, params, fields = newer.shape
     lags = following.shape[1] // params
     plane = lax.axis_index("z")
     count = ordered.shape[0] // 2
     rows = slice(side * count, (side + 1) * count)
-    windows(after(older, newer), block + 1 - lags, 2 * block - 2, params, fields, ahead)
 
     def conv(left, right, pair):
         return product(left, right, (block - 2 - 2 * pair) * params)
@@ -121,7 +118,7 @@
             put_half(sums, pair, half)
 
 
-def lower_part(ordered, older, newer, upper, mine, theirs, times):
+def lower_part(ordered, older, newer, upper, mine, theirs, ahead, times):
     block, params, fields = newer.shape
     for time in range(-1, block):
         value = newer[time] if time >= 0 else older[block - 1]
@@ -138,6 +135,9 @@
         if pair < block // 2 - 1:
             sums = sums + upper[pair]
         put(sums, pair, mine, theirs)
+    windows(
+        after(older, newer), block + 1 - LEADING, 2 * block - 2, params, fields, ahead
+    )
 
 
 def head_part(*refs):
@@ -250,11 +250,17 @@
         compiler_params=LIMIT,
         name="newer_part",
     )(*pieces, shifted)
-    mine, theirs = pl.pallas_call(
+    mine, theirs, ahead = pl.pallas_call(
         lower_part,
-        out_shape=(part, part),
+        out_shape=(
+            part,
+            part,
+            jax.ShapeDtypeStruct(
+                ((block - 2 + LEADING) * params, 2 * fields), jnp.bfloat16
+            ),
+        ),
         in_specs=[VMEM] * 4,
-        out_specs=(VMEM, VMEM),
+        out_specs=(VMEM, VMEM, VMEM),
         scratch_shapes=scratch,
         compiler_params=LIMIT,
         cost_estimate=work(2 * 10**9, 6 * 10**6),
@@ -270,14 +276,13 @@
             in_specs=[VMEM] * 6,
             out_specs=VMEM,
             scratch_shapes=[
-                pltpu.VMEM(((block - 2 + LEADING) * params, width), jnp.bfloat16),
                 pltpu.VMEM(((2 * block - 2 - LEADING) * params, width), jnp.bfloat16),
                 pltpu.VMEM(((2 * block - 2) * params, width), jnp.bfloat16),
             ],
             compiler_params=pltpu.CompilerParams(vmem_limit_bytes=12 * 1024 * 1024),
             cost_estimate=work(2 * 10**9, 8 * 10**6),
             name="second_part",
-        )(ordered, following, history, newer, head_twice, last)
+        )(ordered, following, ahead, newer, head_twice, last)
 
     theirs = second(1)
     mine = second(0)

time: 91.7 us -> 88.6 us (0.966)
  waiting for transfers between devices: 31.4 us -> 21.3 us
  blocking collectives: 34.6 us -> 42.1 us
    ppermute x3, waiting for transfers between devices: 15.6 us -> 7.32 us  [onward(): lax.ppermute(array, axis, [(i, i + by) for i in range(size) if 0 <= i + b...]
    all_to_all x2, blocking collectives: 34.6 us -> 42.1 us  [exchange(): return lax.all_to_all(parts, axis, split_axis=0, concat_axis=0, tiled=True)]
    ppermute x7, waiting for transfers between devices: 15.6 us -> 13.5 us  [observed(): pieces[source] = lax.ppermute(arrivals, 'z', [(source, 0)])]
where the time goes in v8:
time: 88.6 us; the launch traced here: 87.8 us
  blocking collectives  42.1 us (48%)
  waiting for transfers between devices  21.3 us (24%)
  starting transfers between devices  14.8 us (17%)
  Pallas kernels  6.57 us (7%)
  local copies, waits for them, and re-layouts  2.28 us (3%)
    all_to_all x2, blocking collectives, exchange(): return lax.all_to_all(parts, axis, split_axis=0, concat_axis=0, tiled=True)  42.1 us
    ppermute x7, waiting for transfers between devices, observed(): pieces[source] = lax.ppermute(arrivals, 'z', [(source, 0)])  13.5 us
    ppermute x3, starting transfers between devices, onward(): lax.ppermute(array, axis, [(i, i + by) for i in range(size) if 0 <= i + b...  8.67 us
    ppermute x3, waiting for transfers between devices, onward(): lax.ppermute(array, axis, [(i, i + by) for i in range(size) if 0 <= i + b...  7.32 us
    ppermute x7, starting transfers between devices, observed(): pieces[source] = lax.ppermute(arrivals, 'z', [(source, 0)])  5.92 us
    pallas_call x2, Pallas kernels, second(): pl.pallas_call(functools.partial(second_part, side), out_shape=part, in_s...  2.6 us
    unnamed x8, local copies, waits for them, and re-layouts  2.27 us
  transfers between devices with their start and end apart: 12, of which 3 were waited for; matrix products, arithmetic and copies ran while one was open for 0% of the time, Pallas kernels for 7%

profile of v8, /device:TPU:32, one launch (start us, length us, event | category | flops | bytes accessed | tf_op | source)
XLA Modules:
  0.0 87.8 jit_solution(4529994236645076772)
XLA Ops:
  0.0 0.0 copy-start
  0.0 3.9 %collective-permute-start.8 = (bf16[16,128,128]{2,1,0:T(8,128)(2,1)}, bf16[16,128,128]{2,1,0:T(8,128)(2,1)S(1)}, u32[]{:S(2)}, u32[]{:S(2)}) collective-permute-start(bf16[16,128,128]{2,1,0:T(8,128)(2,1)} %older.3), channel_id=1, source_target_pairs={{0,32},{32,64},{64,96},{96,128},{128,160},{160,192},{192,224},{1,3... | collective-permute-start | bytes 1572872 | tf_op jit(solution)/shard_map/ppermute | solution.py:185
  4.0 0.7 collective-permute-start.3
  4.6 0.0 copy-start.1
  4.6 1.2 %copy-done.1 = bf16[16,256,128]{2,1,0:T(8,128)(2,1)S(1)} copy-done((bf16[16,256,128]{2,1,0:T(8,128)(2,1)S(1)}, bf16[16,256,128]{2,1,0:T(8,128)(2,1)}, u32[]{:S(2)}) %copy-start.1) | copy-done | bytes 1048600
  5.9 0.0 copy-start.2
  5.9 1.0 %copy-done.2 = bf16[16,128,128]{2,1,0:T(8,128)(2,1)S(1)} copy-done((bf16[16,128,128]{2,1,0:T(8,128)(2,1)S(1)}, bf16[16,128,128]{2,1,0:T(8,128)(2,1)}, u32[]{:S(2)}) %copy-start.2) | copy-done | bytes 524312
  6.9 1.8 %first_part.1 = (bf16[256,2048]{1,0:T(8,128)(2,1)S(1)}, bf16[256,1024]{1,0:T(8,128)(2,1)S(1)}, f32[7,256,256]{2,1,0:T(8,128)S(1)}) custom-call(bf16[16,256,128]{2,1,0:T(8,128)(2,1)S(1)} %copy-done.1, bf16[16,128,128]{2,1,0:T(8,128)(2,1)S(1)} %copy-done.2), custom_call_target="tpu_custom_call" | custom-call | flops 2000000000 | bytes 4000000 | tf_op jit(solution)/shard_map/first_part/pallas_call | solution.py:206
  8.7 0.0 copy-start.3
  8.7 2.8 %collective-permute-start = (bf16[256,1024]{1,0:T(8,128)(2,1)S(1)}, bf16[256,1024]{1,0:T(8,128)(2,1)S(1)}, u32[]{:S(2)}, u32[]{:S(2)}) collective-permute-start(bf16[256,1024]{1,0:T(8,128)(2,1)S(1)} %get-tuple-element.14), channel_id=1, source_target_pairs={{32,0},{64,32},{96,64},{128,96},{160,128},{192,160},{224,192},{33,... | collective-permute-start | bytes 1572872 | tf_op jit(solution)/shard_map/ppermute | solution.py:185
  11.5 0.0 copy-done
  11.5 0.7 collective-permute-start.2
  12.2 1.9 %collective-permute-start.1 = (bf16[2,2,128,128]{3,2,1,0:T(8,128)(2,1)S(1)}, bf16[2,2,128,128]{3,2,1,0:T(8,128)(2,1)S(1)}, u32[]{:S(2)}, u32[]{:S(2)}) collective-permute-start(bf16[2,2,128,128]{3,2,1,0:T(8,128)(2,1)S(1)} %copy-done), channel_id=1, source_target_pairs={{32,0},{33,1},{34,2},{35,3},{36,4},{37,5},{38,6},{39,7},{40,8},{41... | collective-permute-start | bytes 393224 | tf_op jit(solution)/shard_map/ppermute | solution.py:204
  14.1 0.0 collective-permute-done.3.refs_3_
  14.1 0.7 collective-permute-start.7
  14.8 0.0 collective-permute-done.2.refs_2_
  14.8 0.7 collective-permute-start.6
  15.5 13.5 %collective-permute-done.1.refs_1_ = bf16[2,2,128,128]{3,2,1,0:T(8,128)(2,1)S(1)} collective-permute-done((bf16[2,2,128,128]{3,2,1,0:T(8,128)(2,1)S(1)}, bf16[2,2,128,128]{3,2,1,0:T(8,128)(2,1)S(1)}, u32[]{:S(2)}, u32[]{:S(2)}) %collective-permute-start.1) | collective-permute-done | bytes 131104 | tf_op jit(solution)/shard_map/ppermute | solution.py:204
  29.0 0.7 collective-permute-start.5
  29.6 0.0 collective-permute-done.8.refs_8_.refs_4_
  29.6 0.7 collective-permute-start.4
  30.3 0.1 head_part.1
  30.4 0.0 collective-permute-done.7.refs_7_
  30.4 1.9 %collective-permute-start.9 = (bf16[8,128,128]{2,1,0:T(8,128)(2,1)S(1)}, bf16[8,128,128]{2,1,0:T(8,128)(2,1)S(1)}, u32[]{:S(2)}, u32[]{:S(2)}) collective-permute-start(bf16[8,128,128]{2,1,0:T(8,128)(2,1)S(1)} %head_part.1), channel_id=1, source_target_pairs={{0,32},{32,64},{64,96},{96,128},{128,160},{160,192},{192,224},{1,3... | collective-permute-start | bytes 786440 | tf_op jit(solution)/shard_map/ppermute | solution.py:185
  32.3 0.0 collective-permute-done.6.refs_6_
  32.4 0.0 collective-permute-done.5.refs_5_
  32.4 0.0 collective-permute-done.4.refs_4_
  32.4 0.2 newer_part.1
  32.6 0.0 copy-done.3
  32.6 1.6 %lower_part.1 = (bf16[16,16,8,128]{3,2,1,0:T(8,128)(2,1)S(1)}, bf16[16,16,8,128]{3,2,1,0:T(8,128)(2,1)S(1)}, bf16[2816,256]{1,0:T(8,128)(2,1)S(1)}) custom-call(bf16[256,2048]{1,0:T(8,128)(2,1)S(1)} %get-tuple-element.13.ordered, bf16[16,128,128]{2,1,0:T(8,128)(2,1)S(1)} %copy-done.3, bf16[16,128,128]{2,1,0:T(8,128)(2,1)S(1)} %get-tuple-element.15.newer, ...), custom_call_target="tpu_custom_call" | custom-call | flops 2000000000 | bytes 6000000 | tf_op jit(solution)/shard_map/lower_part/pallas_call | solution.py:253
  34.1 0.1 collective-permute-start.11
  34.2 0.0 collective-permute-done.following
  34.2 7.3 %collective-permute-done.9.head = bf16[8,128,128]{2,1,0:T(8,128)(2,1)S(1)} collective-permute-done((bf16[8,128,128]{2,1,0:T(8,128)(2,1)S(1)}, bf16[8,128,128]{2,1,0:T(8,128)(2,1)S(1)}, u32[]{:S(2)}, u32[]{:S(2)}) %collective-permute-start.9) | collective-permute-done | bytes 262176 | tf_op jit(solution)/shard_map/ppermute | solution.py:185
  41.6 1.3 %second_part.3 = bf16[16,16,8,128]{3,2,1,0:T(8,128)(2,1)S(1)} custom-call(bf16[256,2048]{1,0:T(8,128)(2,1)S(1)} %get-tuple-element.13.ordered, bf16[256,1024]{1,0:T(8,128)(2,1)S(1)} %collective-permute-done.following, bf16[2816,256]{1,0:T(8,128)(2,1)S(1)} %get-tuple-element.17.ahead, bf16[16,128,128]{2,1,0:T(8,128)(2,1)S(1)} %get-tuple-element.15.newer, ...), custom_call_target="tpu_custom_call" | custom-call | flops 2000000000 | bytes 8000000 | tf_op jit(solution)/shard_map/second_part/pallas_call | solution.py:273
  42.9 0.1 collective-permute-start.10
  43.0 1.3 %second_part.2.mine = bf16[16,16,8,128]{3,2,1,0:T(8,128)(2,1)S(1)} custom-call(bf16[256,2048]{1,0:T(8,128)(2,1)S(1)} %get-tuple-element.13.ordered, bf16[256,1024]{1,0:T(8,128)(2,1)S(1)} %collective-permute-done.following, bf16[2816,256]{1,0:T(8,128)(2,1)S(1)} %get-tuple-element.17.ahead, bf16[16,128,128]{2,1,0:T(8,128)(2,1)S(1)} %get-tuple-element.15.newer, ...), custom_call_target="tpu_custom_call" | custom-call | flops 2000000000 | bytes 8000000 | tf_op jit(solution)/shard_map/second_part/pallas_call | solution.py:273
  44.3 0.0 collective-permute-done.11.received
  44.3 0.1 pair_part.2.refs_0_
  44.4 0.4 collective-permute-done.10.received
  44.9 0.1 pair_part.3
  45.0 24.2 %all_to_all.10.arrived = bf16[16,32,8,128]{3,2,1,0:T(8,128)(2,1)S(1)} all-to-all(bf16[16,32,8,128]{3,2,1,0:T(8,128)(2,1)S(1)} %pair_part.3), channel_id=1, replica_groups=mesh['z'=8,'x'=4,'y'=4,'c'=2] {'x','y'}, dimensions={0} | all-to-all | bytes 2097152 | tf_op jit(solution)/shard_map/all_to_all | solution.py:189
  69.2 0.1 plane_part.1
  69.4 17.8 %all_to_all.11 = bf16[8,32,128]{2,1,0:T(8,128)(2,1)S(1)} all-to-all(bf16[8,32,128]{2,1,0:T(8,128)(2,1)S(1)} %copy.5), channel_id=1, replica_groups=mesh['z'=8,'x'=4,'y'=4,'c'=2] {'z'}, dimensions={0} | all-to-all | bytes 131072 | tf_op jit(solution)/shard_map/all_to_all | solution.py:189
  87.2 0.6 reduce_sum.12
  (1 shorter events, 0.0 us)
Async XLA Ops:
  0.0 11.5 %copy-start = (bf16[2,2,128,128]{3,2,1,0:T(8,128)(2,1)S(1)}, bf16[2,2,128,128]{3,2,1,0:T(8,128)(2,1)}, u32[]{:S(2)}) copy-start(bf16[2,2,128,128]{3,2,1,0:T(8,128)(2,1)} %refs_0_.3) | copy-start | bytes 393220
  0.0 29.6 %collective-permute-start.8 = (bf16[16,128,128]{2,1,0:T(8,128)(2,1)}, bf16[16,128,128]{2,1,0:T(8,128)(2,1)S(1)}, u32[]{:S(2)}, u32[]{:S(2)}) collective-permute-start(bf16[16,128,128]{2,1,0:T(8,128)(2,1)} %older.3), channel_id=1, source_target_pairs={{0,32},{32,64},{64,96},{96,128},{128,160},{160,192},{192,224},{1,3... | collective-permute-start | bytes 1572872 | tf_op jit(solution)/shard_map/ppermute | solution.py:185
  4.0 10.2 %collective-permute-start.3 = (bf16[2,2,128,128]{3,2,1,0:T(8,128)(2,1)}, bf16[2,2,128,128]{3,2,1,0:T(8,128)(2,1)S(1)}, u32[]{:S(2)}, u32[]{:S(2)}) collective-permute-start(bf16[2,2,128,128]{3,2,1,0:T(8,128)(2,1)} %refs_0_.3), channel_id=1, source_target_pairs={{96,0},{97,1},{98,2},{99,3},{100,4},{101,5},{102,6},{103,7},{104,8... | collective-permute-start | bytes 393224 | tf_op jit(solution)/shard_map/ppermute | solution.py:204
  4.6 1.2 %copy-start.1 = (bf16[16,256,128]{2,1,0:T(8,128)(2,1)S(1)}, bf16[16,256,128]{2,1,0:T(8,128)(2,1)}, u32[]{:S(2)}) copy-start(bf16[16,256,128]{2,1,0:T(8,128)(2,1)} %kernel.1) | copy-start | bytes 3145732
  5.9 1.0 %copy-start.2 = (bf16[16,128,128]{2,1,0:T(8,128)(2,1)S(1)}, bf16[16,128,128]{2,1,0:T(8,128)(2,1)}, u32[]{:S(2)}) copy-start(bf16[16,128,128]{2,1,0:T(8,128)(2,1)} %older.3) | copy-start | bytes 1572868
  8.7 23.9 %copy-start.3 = (bf16[16,128,128]{2,1,0:T(8,128)(2,1)S(1)}, bf16[16,128,128]{2,1,0:T(8,128)(2,1)}, u32[]{:S(2)}) copy-start(bf16[16,128,128]{2,1,0:T(8,128)(2,1)} %older.3) | copy-start | bytes 1572868
  8.7 25.5 %collective-permute-start = (bf16[256,1024]{1,0:T(8,128)(2,1)S(1)}, bf16[256,1024]{1,0:T(8,128)(2,1)S(1)}, u32[]{:S(2)}, u32[]{:S(2)}) collective-permute-start(bf16[256,1024]{1,0:T(8,128)(2,1)S(1)} %get-tuple-element.14), channel_id=1, source_target_pairs={{32,0},{64,32},{96,64},{128,96},{160,128},{192,160},{224,192},{33,... | collective-permute-start | bytes 1572872 | tf_op jit(solution)/shard_map/ppermute | solution.py:185
  11.5 3.3 %collective-permute-start.2 = (bf16[2,2,128,128]{3,2,1,0:T(8,128)(2,1)S(1)}, bf16[2,2,128,128]{3,2,1,0:T(8,128)(2,1)S(1)}, u32[]{:S(2)}, u32[]{:S(2)}) collective-permute-start(bf16[2,2,128,128]{3,2,1,0:T(8,128)(2,1)S(1)} %copy-done), channel_id=1, source_target_pairs={{64,0},{65,1},{66,2},{67,3},{68,4},{69,5},{70,6},{71,7},{72,8},{73... | collective-permute-start | bytes 393224 | tf_op jit(solution)/shard_map/ppermute | solution.py:204
  12.2 16.8 %collective-permute-start.1 = (bf16[2,2,128,128]{3,2,1,0:T(8,128)(2,1)S(1)}, bf16[2,2,128,128]{3,2,1,0:T(8,128)(2,1)S(1)}, u32[]{:S(2)}, u32[]{:S(2)}) collective-permute-start(bf16[2,2,128,128]{3,2,1,0:T(8,128)(2,1)S(1)} %copy-done), channel_id=1, source_target_pairs={{32,0},{33,1},{34,2},{35,3},{36,4},{37,5},{38,6},{39,7},{40,8},{41... | collective-permute-start | bytes 393224 | tf_op jit(solution)/shard_map/ppermute | solution.py:204
  14.1 16.3 %collective-permute-start.7 = (bf16[2,2,128,128]{3,2,1,0:T(8,128)(2,1)S(1)}, bf16[2,2,128,128]{3,2,1,0:T(8,128)(2,1)S(1)}, u32[]{:S(2)}, u32[]{:S(2)}) collective-permute-start(bf16[2,2,128,128]{3,2,1,0:T(8,128)(2,1)S(1)} %copy-done), channel_id=1, source_target_pairs={{224,0},{225,1},{226,2},{227,3},{228,4},{229,5},{230,6},{231,7},{2... | collective-permute-start | bytes 393224 | tf_op jit(solution)/shard_map/ppermute | solution.py:204
  14.8 17.5 %collective-permute-start.6 = (bf16[2,2,128,128]{3,2,1,0:T(8,128)(2,1)S(1)}, bf16[2,2,128,128]{3,2,1,0:T(8,128)(2,1)S(1)}, u32[]{:S(2)}, u32[]{:S(2)}) collective-permute-start(bf16[2,2,128,128]{3,2,1,0:T(8,128)(2,1)S(1)} %copy-done), channel_id=1, source_target_pairs={{192,0},{193,1},{194,2},{195,3},{196,4},{197,5},{198,6},{199,7},{2... | collective-permute-start | bytes 393224 | tf_op jit(solution)/shard_map/ppermute | solution.py:204
  29.0 3.4 %collective-permute-start.5 = (bf16[2,2,128,128]{3,2,1,0:T(8,128)(2,1)S(1)}, bf16[2,2,128,128]{3,2,1,0:T(8,128)(2,1)S(1)}, u32[]{:S(2)}, u32[]{:S(2)}) collective-permute-start(bf16[2,2,128,128]{3,2,1,0:T(8,128)(2,1)S(1)} %copy-done), channel_id=1, source_target_pairs={{160,0},{161,1},{162,2},{163,3},{164,4},{165,5},{166,6},{167,7},{1... | collective-permute-start | bytes 393224 | tf_op jit(solution)/shard_map/ppermute | solution.py:204
  29.6 2.7 %collective-permute-start.4 = (bf16[2,2,128,128]{3,2,1,0:T(8,128)(2,1)S(1)}, bf16[2,2,128,128]{3,2,1,0:T(8,128)(2,1)S(1)}, u32[]{:S(2)}, u32[]{:S(2)}) collective-permute-start(bf16[2,2,128,128]{3,2,1,0:T(8,128)(2,1)S(1)} %copy-done), channel_id=1, source_target_pairs={{128,0},{129,1},{130,2},{131,3},{132,4},{133,5},{134,6},{135,7},{1... | collective-permute-start | bytes 393224 | tf_op jit(solution)/shard_map/ppermute | solution.py:204
  30.4 11.1 %collective-permute-start.9 = (bf16[8,128,128]{2,1,0:T(8,128)(2,1)S(1)}, bf16[8,128,128]{2,1,0:T(8,128)(2,1)S(1)}, u32[]{:S(2)}, u32[]{:S(2)}) collective-permute-start(bf16[8,128,128]{2,1,0:T(8,128)(2,1)S(1)} %head_part.1), channel_id=1, source_target_pairs={{0,32},{32,64},{64,96},{96,128},{128,160},{160,192},{192,224},{1,3... | collective-permute-start | bytes 786440 | tf_op jit(solution)/shard_map/ppermute | solution.py:185
  34.1 10.2 %collective-permute-start.11 = (bf16[16,16,8,128]{3,2,1,0:T(8,128)(2,1)S(1)}, bf16[16,16,8,128]{3,2,1,0:T(8,128)(2,1)S(1)}, u32[]{:S(2)}, u32[]{:S(2)}) collective-permute-start(bf16[16,16,8,128]{3,2,1,0:T(8,128)(2,1)S(1)} %get-tuple-element.20), channel_id=1, source_target_pairs={{0,1},{1,0},{2,3},{3,2},{4,5},{5,4},{6,7},{7,6},{8,9},{9,8},{10,11... | collective-permute-start | bytes 1572872 | tf_op jit(solution)/shard_map/ppermute | solution.py:180
  42.9 2.0 %collective-permute-start.10 = (bf16[16,16,8,128]{3,2,1,0:T(8,128)(2,1)S(1)}, bf16[16,16,8,128]{3,2,1,0:T(8,128)(2,1)S(1)}, u32[]{:S(2)}, u32[]{:S(2)}) collective-permute-start(bf16[16,16,8,128]{3,2,1,0:T(8,128)(2,1)S(1)} %second_part.3), channel_id=1, source_target_pairs={{0,1},{1,0},{2,3},{3,2},{4,5},{5,4},{6,7},{7,6},{8,9},{9,8},{10,11... | collective-permute-start | bytes 1572872 | tf_op jit(solution)/shard_map/ppermute | solution.py:180
